TPU v7x, 16 devices: a whole 2x2x2 slice. The times are simulated.
16 devices in a mesh: vp: 2 (over z), dp: 8 (over y, x, core).
Axes of the slice: x: 2, y: 2, z: 2, core: 2. Of those that a mesh axis runs over, the one named last changes fastest.
Arguments:
- student_x: bfloat16 [2560, 1536], P('dp')
- teacher_x: bfloat16 [512, 1536], P('dp')
- w_in: bfloat16 [1536, 2048], replicated
- b_in: bfloat16 [2048], replicated
- w_mid: bfloat16 [2048, 2048], replicated
- b_mid: bfloat16 [2048], replicated
- w_out: bfloat16 [2048, 256], replicated
- b_out: bfloat16 [256], replicated
- protos: bfloat16 [256, 65536], P(None, 'vp')
- ema_w_in: bfloat16 [1536, 2048], replicated
- ema_b_in: bfloat16 [2048], replicated
- ema_w_mid: bfloat16 [2048, 2048], replicated
- ema_b_mid: bfloat16 [2048], replicated
- ema_w_out: bfloat16 [2048, 256], replicated
- ema_b_out: bfloat16 [256], replicated
- ema_protos: bfloat16 [256, 65536], P(None, 'vp')
Outputs:
- output 1: float32 [], replicated
- output 2: float32 [1536, 2048], replicated
- output 3: float32 [2048], replicated
- output 4: float32 [2048, 2048], replicated
- output 5: float32 [2048], replicated
- output 6: float32 [2048, 256], replicated
- output 7: float32 [256], replicated
- output 8: float32 [256, 65536], P(None, 'vp')
All inputs are finite; a program needn't handle non-finite values.
Results may differ from a plain program's by a relative error of at most 0.00517659.
Values sent between devices are 32-bit elements.
A program may use at most 1 GiB of HBM per device.

v0:
```python
import jax
import jax.numpy as jnp
from jax import lax
from jax.sharding import PartitionSpec as P

ALL_CROPS = 10
GLOBAL_CROPS = 2
SINK_ITERS = 3
TEMP_STUDENT = 0.1
TEMP_TEACHER = 0.04


def gelu_slope(pre):
    cdf = 0.5 * (1.0 + lax.erf(pre * 0.7071067811865476))
    return cdf + pre * jnp.exp(-0.5 * pre * pre) * 0.3989422804014327


def mlp_forward(feats, w_in, b_in, w_mid, b_mid, w_out, b_out):
    pre_one = jnp.dot(feats, w_in, preferred_element_type=jnp.float32) + b_in.astype(jnp.float32)
    hid_one = jax.nn.gelu(pre_one, approximate=False).astype(jnp.bfloat16)
    pre_two = jnp.dot(hid_one, w_mid, preferred_element_type=jnp.float32) + b_mid.astype(jnp.float32)
    hid_two = jax.nn.gelu(pre_two, approximate=False).astype(jnp.bfloat16)
    proj = jnp.dot(hid_two, w_out, preferred_element_type=jnp.float32) + b_out.astype(jnp.float32)
    inv_norm = lax.rsqrt(jnp.sum(proj * proj, axis=-1, keepdims=True))
    unit = proj * inv_norm
    return unit.astype(jnp.bfloat16), (pre_one, hid_one, pre_two, hid_two, unit, inv_norm)


def mlp_backward(g_emb, feats, saved, w_mid, w_out):
    pre_one, hid_one, pre_two, hid_two, unit, inv_norm = saved
    g_proj = (g_emb - unit * jnp.sum(unit * g_emb, axis=-1, keepdims=True)) * inv_norm
    g_proj_lo = g_proj.astype(jnp.bfloat16)
    g_w_out = jnp.einsum('nh,nb->hb', hid_two, g_proj_lo, preferred_element_type=jnp.float32)
    g_hid_two = jnp.einsum('nb,hb->nh', g_proj_lo, w_out, preferred_element_type=jnp.float32)
    g_pre_two = g_hid_two.astype(jnp.bfloat16).astype(jnp.float32) * gelu_slope(pre_two)
    g_pre_two_lo = g_pre_two.astype(jnp.bfloat16)
    g_w_mid = jnp.einsum('ng,nh->gh', hid_one, g_pre_two_lo, preferred_element_type=jnp.float32)
    g_hid_one = jnp.einsum('nh,gh->ng', g_pre_two_lo, w_mid, preferred_element_type=jnp.float32)
    g_pre_one = g_hid_one.astype(jnp.bfloat16).astype(jnp.float32) * gelu_slope(pre_one)
    g_w_in = jnp.einsum('nf,nh->fh', feats, g_pre_one.astype(jnp.bfloat16), preferred_element_type=jnp.float32)
    return (g_w_in, jnp.sum(g_pre_one, axis=0), g_w_mid, jnp.sum(g_pre_two, axis=0), g_w_out, jnp.sum(g_proj, axis=0))


def col_normalize(protos):
    proto_f = protos.astype(jnp.float32)
    inv_col = lax.rsqrt(jnp.sum(proto_f * proto_f, axis=0, keepdims=True))
    unit = proto_f * inv_col
    return unit.astype(jnp.bfloat16), unit, inv_col


def col_normalize_backward(g_unit, unit, inv_col):
    return (g_unit - unit * jnp.sum(unit * g_unit, axis=0, keepdims=True)) * inv_col


def pair_targets(q_three):
    pad_rows = ALL_CROPS - GLOBAL_CROPS
    return jnp.sum(q_three, axis=1, keepdims=True) - jnp.pad(q_three, ((0, 0), (0, pad_rows), (0, 0)))


def crop_counts():
    crop_idx = jnp.arange(ALL_CROPS)
    return (GLOBAL_CROPS - (crop_idx < GLOBAL_CROPS).astype(jnp.int32)).astype(jnp.float32)


def solution(mesh):
    vp_size = mesh.shape['vp']
    dp_size = mesh.shape['dp']

    def local_step(student_x, teacher_x, w_in, b_in, w_mid, b_mid, w_out, b_out, protos,
                   ema_w_in, ema_b_in, ema_w_mid, ema_b_mid, ema_w_out, ema_b_out, ema_protos):
        n_img = student_x.shape[0] // ALL_CROPS
        local_proto = protos.shape[1]
        n_proto = local_proto * vp_size
        n_rows = GLOBAL_CROPS * n_img * dp_size
        t_emb, _ = mlp_forward(teacher_x, ema_w_in, ema_b_in, ema_w_mid, ema_b_mid, ema_w_out, ema_b_out)
        t_unit = col_normalize(ema_protos)[0]
        q_mat = jnp.exp(jnp.dot(t_emb, t_unit, preferred_element_type=jnp.float32) / TEMP_TEACHER)
        q_mat = q_mat / lax.psum(jnp.sum(q_mat), ('vp', 'dp'))
        for _ in range(SINK_ITERS):
            proto_sum = lax.psum(jnp.sum(q_mat, axis=0, keepdims=True), 'dp')
            q_mat = q_mat / (proto_sum * n_proto)
            crop_sum = lax.psum(jnp.sum(q_mat, axis=1, keepdims=True), 'vp')
            q_mat = q_mat / (crop_sum * n_rows)
        q_three = (q_mat * n_rows).reshape(n_img, GLOBAL_CROPS, local_proto)

        s_emb, saved = mlp_forward(student_x, w_in, b_in, w_mid, b_mid, w_out, b_out)
        s_unit, unit_f, inv_col = col_normalize(protos)
        logits = jnp.dot(s_emb, s_unit, preferred_element_type=jnp.float32) / TEMP_STUDENT
        logits = logits.reshape(n_img, ALL_CROPS, local_proto)
        row_max = lax.pmax(jnp.max(logits, axis=-1, keepdims=True), 'vp')
        shifted = logits - row_max
        exp_s = jnp.exp(shifted)
        row_sum = lax.psum(jnp.sum(exp_s, axis=-1, keepdims=True), 'vp')
        scale = 1.0 / (n_img * dp_size * GLOBAL_CROPS * (ALL_CROPS - 1))
        targets = pair_targets(q_three)
        loss = lax.psum(jnp.sum(targets * (jnp.log(row_sum) - shifted)), ('vp', 'dp')) * scale
        g_logits = (crop_counts()[:, None] * (exp_s / row_sum) - targets) * (scale / TEMP_STUDENT)
        g_logits = g_logits.reshape(n_img * ALL_CROPS, local_proto).astype(jnp.bfloat16)
        g_emb = jnp.einsum('rk,bk->rb', g_logits, s_unit, preferred_element_type=jnp.float32)
        g_unit = lax.psum(jnp.einsum('rb,rk->bk', s_emb, g_logits, preferred_element_type=jnp.float32), 'dp')
        head_grads = lax.psum(mlp_backward(g_emb, student_x, saved, w_mid, w_out), ('vp', 'dp'))
        g_protos = col_normalize_backward(g_unit, unit_f, inv_col)
        return (loss,) + tuple(head_grads) + (g_protos,)

    by_rows = P('dp', None)
    by_cols = P(None, 'vp')
    replicated = P()
    head_specs = (replicated,) * 6
    in_specs = (by_rows, by_rows) + head_specs + (by_cols,) + head_specs + (by_cols,)
    out_specs = (replicated,) * 7 + (by_cols,)
    return jax.shard_map(local_step, mesh=mesh, in_specs=in_specs, out_specs=out_specs, check_vma=False)
```

profile of v0, /device:TPU:0, one launch (start us, length us, event | category | flops | bytes accessed | tf_op | source)
XLA Modules:
  0.0 1192.6 jit_solution(8235019740496561609)
XLA Ops:
  24.0 14.3 %fusion.154 = (f32[]{:T(128)}, f32[64,32768]{1,0:T(8,128)}) fusion(bf16[256,32768]{1,0:T(8,128)(2,1)} %param.31, f32[32768]{0:T(1024)S(1)} %rsqrt.33, f32[64,256]{1,0:T(8,128)S(1)} %get-tuple-element.38, f32[64]{0:T(128)S(1)} %rsqrt.32), kind=kOutput, calls=%fused_computation.224 | convolution fusion | flops 1103134720 | bytes 25362692 | tf_op jit(solution)/shard_map/dot_general | solution.py:77
  38.4 34.7 %psum.112 = f32[]{:T(128)} all-reduce(f32[]{:T(128)} %get-tuple-element.39), channel_id=1, replica_groups=mesh['vp'=2,'dp'=8] {'vp','dp'}, use_global_device_ids=true, to_apply=%region_3.0 | all-reduce | flops 1 | bytes 8 | tf_op jit(solution)/shard_map/psum | solution.py:78
  91.6 14.8 %fusion.36 = (bf16[320,2048]{1,0:T(8,128)(2,1)S(1)}, f32[320,2048]{1,0:T(8,128)}) fusion(f32[2048]{0:T(1024)S(1)} %convert_element_type.101, bf16[2048,2048]{1,0:T(8,128)(2,1)S(1)} %bitcast.65, f32[320,2048]{1,0:T(8,128)S(1)} %convolution_add_fusion.1), kind=kOutput, calls=%fused_computation.56 | convolution fusion | flops 2770206720 | bytes 14950400 | tf_op jit(solution)/shard_map/dot_general | solution.py:21
  107.0 20.0 %fusion.155 = (f32[320]{0:T(512)S(1)}, f32[320,32768]{1,0:T(8,128)}) fusion(bf16[256,32768]{1,0:T(8,128)(2,1)} %param.24, f32[32768]{0:T(1024)S(1)} %rsqrt.35, f32[320,256]{1,0:T(8,128)S(1)} %get-tuple-element.44, f32[320]{0:T(512)S(1)} %rsqrt.34), kind=kOutput, calls=%fused_computation.225 | convolution fusion | flops 5415009792 | bytes 59181568 | tf_op jit(solution)/shard_map/dot_general | solution.py:88
  127.7 9.3 pmax.7
  152.8 16.8 %exponential_reduce_fusion = f32[320]{0:T(512)S(1)} fusion(f32[320,32768]{1,0:T(8,128)} %get-tuple-element.46, f32[320]{0:T(512)S(1)} %sub.53), kind=kLoop, calls=%fused_computation.11 | loop fusion | flops 20971200 | bytes 41945600 | tf_op jit(solution)/shard_map/reduce_sum | solution.py:93
  169.6 51.4 %reshape.68 = f32[32,10,32768]{2,1,0:T(8,128)} reshape(f32[320,32768]{1,0:T(8,128)} %get-tuple-element.46) | data formatting | bytes 83886080 | tf_op jit(solution)/shard_map/reshape | solution.py:89
  237.0 45.0 %all-reduce.14.cloned.1.call-done = f32[1,32768]{1,0:T(1,128)} async-done(((f32[1,32768]{1,0:T(1,128)}), f32[1,32768]{1,0:T(1,128)}) %all-reduce.14.cloned.1.call-update) | async-done | bytes 131088 | tf_op jit(solution)/shard_map/psum | solution.py:80
  287.6 8.4 all-reduce.3
  302.7 10.5 reshape.67
  313.3 13.3 %reduce_sum.180 = f32[32,32768]{1,0:T(8,128)} reduce(f32[32,2,32768]{2,1,0:T(2,128)} %reshape.67, f32[]{:T(128)} %constant.50.clone.1), dimensions={1}, to_apply=%region_16.0 | reduce | flops 1048576 | bytes 12582916 | tf_op jit(solution)/shard_map/reduce_sum | solution.py:57
  326.6 39.0 %multiply_convert_fusion = (bf16[32,10,32768]{2,1,0:T(8,128)(2,1)}, f32[]{:T(128)}) fusion(f32[32,2,32768]{2,1,0:T(2,128)} %reshape.67, f32[32,10,32768]{2,1,0:T(8,128)} %reshape.68, f32[32,10]{1,0:T(8,128)S(1)} %bitcast.60, f32[10]{0:T(128)S(1)} %fusion.119, f32[32,10]{1,0:T(8,128)S(1)} %bitcast.59, f32[32,32768]{1,0:T(8,128)} %reduce_sum.180, ...), kind=kLoop, calls=%fused_computation | loop fusion | flops 104857600 | bytes 75501360 | tf_op jit(solution)/shard_map/convert_element_type | solution.py:98
  365.6 21.2 %convert_element_type.110 = bf16[320,32768]{1,0:T(8,128)(2,1)} reshape(bf16[32,10,32768]{2,1,0:T(8,128)(2,1)} %get-tuple-element.35) | data formatting | bytes 41943040 | tf_op jit(solution)/shard_map/convert_element_type | solution.py:98
  386.8 14.9 %multiply_reduce_fusion.1 = (f32[320]{0:T(512)S(1)}, f32[320,256]{1,0:T(8,128)S(1)}) fusion(f32[320,256]{1,0:T(8,128)S(1)} %get-tuple-element.44, f32[320]{0:T(512)S(1)} %rsqrt.34, bf16[320,32768]{1,0:T(8,128)(2,1)} %convert_element_type.110, bf16[256,32768]{1,0:T(8,128)(2,1)} %param.24, f32[32768]{0:T(1024)S(1)} %rsqrt.35), kind=kOutput, calls=%fused_computation.142 | convolution fusion | flops 5394120192 | bytes 38537728 | tf_op jit(solution)/shard_map/rk,bk->rb/dot_general | solution.py:99
  412.1 13.1 %fusion.60 = f32[2048,2048]{1,0:T(8,128)} fusion(bf16[320,2048]{1,0:T(8,128)(2,1)S(1)} %get-tuple-element.52, f32[320,2048]{1,0:T(8,128)S(1)} %copy-done.17), kind=kOutput, calls=%fused_computation.102 | convolution fusion | flops 2726952960 | bytes 20709376 | tf_op jit(solution)/shard_map/ng,nh->gh/dot_general | solution.py:37
  434.0 23.6 %fusion.150 = f32[256,32768]{1,0:T(8,128)} fusion(bf16[320,32768]{1,0:T(8,128)(2,1)} %convert_element_type.110, f32[320,256]{1,0:T(8,128)S(1)} %get-tuple-element.44, f32[320]{0:T(512)S(1)} %rsqrt.34), kind=kOutput, calls=%fused_computation.222 | convolution fusion | flops 5368872960 | bytes 54854912 | tf_op jit(solution)/shard_map/rb,rk->bk/dot_general | solution.py:100
  457.6 32.5 %all-reduce.1 = (f32[]{:T(128)}, f32[2048]{0:T(1024)}, f32[2048]{0:T(1024)}, f32[256]{0:T(256)}) all-reduce(f32[]{:T(128)} %get-tuple-element.36, f32[2048]{0:T(1024)S(1)} %get-tuple-element.49, f32[2048]{0:T(1024)S(1)} %get-tuple-element.51, f32[256]{0:T(256)S(1)} %get-tuple-element.33), channel_id=1, replica_groups=mesh['vp'=2,'dp'=8] {'vp','dp'}, use_global_device_ids=true, to_apply=%region_24.25 | all-reduce | flops 4353 | bytes 34824 | tf_op jit(solution)/shard_map/psum | solution.py:96
  490.7 241.5 %all-reduce.18.cloned.1.call-done = (f32[1536,2048]{0,1:T(8,128)}, f32[2048,2048]{1,0:T(8,128)}, f32[2048,256]{1,0:T(8,128)}) async-done(((f32[1536,2048]{0,1:T(8,128)}, f32[2048,2048]{1,0:T(8,128)}, f32[2048,256]{1,0:T(8,128)}), (f32[1536,2048]{0,1:T(8,128)}, f32[2048,2048]{1,0:T(8,128)}, f32[2048,256]{1,0:T(8,128)})) %all-reduce.18.cloned.1.call-update) | async-done | bytes 31457296 | tf_op jit(solution)/shard_map/psum | solution.py:101
  732.2 12.6 %copy.25 = f32[1536,2048]{1,0:T(8,128)} copy(f32[1536,2048]{0,1:T(8,128)} %get-tuple-element.28) | data formatting | bytes 25165824
  744.8 382.2 %all-reduce.16.cloned.1.call-done = f32[256,32768]{1,0:T(8,128)} async-done(((f32[256,32768]{1,0:T(8,128)}), f32[256,32768]{1,0:T(8,128)}) %all-reduce.16.cloned.1.call-update) | async-done | bytes 33554448 | tf_op jit(solution)/shard_map/psum | solution.py:100
  1127.0 16.5 %fusion.6 = f32[32768]{0:T(1024)S(1)} fusion(f32[256,32768]{1,0:T(8,128)} %all-reduce.16.cloned.1.call-done, bf16[256,32768]{1,0:T(8,128)(2,1)} %param.24, f32[32768]{0:T(1024)S(1)} %rsqrt.35), kind=kLoop, calls=%fused_computation.16 | loop fusion | flops 33521664 | bytes 50593792 | tf_op jit(solution)/shard_map/reduce_sum | solution.py:52
  1143.5 8.5 copy-done.1
  1152.0 19.3 %fusion.8 = f32[256,32768]{1,0:T(8,128)} fusion(f32[256,32768]{1,0:T(8,128)S(1)} %copy-done.1, bf16[256,32768]{1,0:T(8,128)(2,1)} %param.24, f32[32768]{0:T(1024)S(1)} %fusion.6, f32[32768]{0:T(1024)S(1)} %rsqrt.35), kind=kLoop, calls=%fused_computation.18 | loop fusion | flops 41943040 | bytes 84148224 | tf_op jit(solution)/shard_map/mul | solution.py:52
  1171.3 11.9 %copy.33 = f32[2048,2048]{1,0:T(8,128)} copy(f32[2048,2048]{1,0:T(8,128)} %get-tuple-element.62) | data formatting | bytes 33554432
  (94 shorter events, 100.2 us)
Async XLA Ops:
  7.2 99.2 %copy-start = (bf16[2048,256]{1,0:T(8,128)(2,1)S(1)}, bf16[2048,256]{1,0:T(8,128)(2,1)}, u32[]{:S(2)}) copy-start(bf16[2048,256]{1,0:T(8,128)(2,1)} %param.22) | copy-start | bytes 3145732
  7.2 8.2 copy-start.14
  7.2 8.2 copy-start.7
  7.2 8.3 copy-start.8
  7.2 8.3 copy-start.13
  7.2 130.0 %all-reduce.10.cloned.1.call-start = ((), (), s32[]{:S(2)}) async-start(), calls=%async_computation | async-start | bytes 262144 | tf_op jit(solution)/shard_map/psum | solution.py:80
  7.3 8.2 copy-start.11
  15.5 2.3 copy-start.12
  78.6 7.7 copy-start.15
  78.6 7.7 copy-start.9
  78.6 7.8 copy-start.10
  78.6 7.8 copy-start.5
  78.6 142.6 %all-reduce.12.cloned.1.call-start = ((), (), s32[]{:S(2)}) async-start(), calls=%async_computation.1 | async-start | bytes 262144 | tf_op jit(solution)/shard_map/psum | solution.py:80
  78.7 12.9 %slice-start = ((s8[8388608]{0:T(1024)(128)(4,1)}), s8[4194304]{0:T(1024)(128)(4,1)S(1)}, s32[]{:S(2)}) async-start(s8[8388608]{0:T(1024)(128)(4,1)} %bitcast.64), calls=%async_computation.5 | async-start | bytes 8388608
  86.4 5.2 slice-start.1
  91.6 14.8 %copy-start.16 = (f32[320,2048]{1,0:T(8,128)}, f32[320,2048]{1,0:T(8,128)S(1)}, u32[]{:S(2)}) copy-start(f32[320,2048]{1,0:T(8,128)S(1)} %convolution_add_fusion.1) | copy-start | bytes 7864324
  106.4 20.6 %copy-start.3 = (bf16[320,2048]{1,0:T(8,128)(2,1)}, bf16[320,2048]{1,0:T(8,128)(2,1)S(1)}, u32[]{:S(2)}) copy-start(bf16[320,2048]{1,0:T(8,128)(2,1)S(1)} %get-tuple-element.41) | copy-start | bytes 3932164
  152.8 129.2 %all-reduce.14.cloned.1.call-start = ((), (), s32[]{:S(2)}) async-start(), calls=%async_computation.2 | async-start | bytes 262144 | tf_op jit(solution)/shard_map/psum | solution.py:80
  236.9 495.3 %all-reduce.18.cloned.1.call-start = ((), (), s32[]{:S(2)}) async-start(), calls=%async_computation.4 | async-start | bytes 62914560 | tf_op jit(solution)/shard_map/psum | solution.py:101
  401.9 3.2 copy-start.17
  412.1 13.1 %copy-start.4 = (bf16[320,2048]{1,0:T(8,128)(2,1)S(1)}, bf16[320,2048]{1,0:T(8,128)(2,1)}, u32[]{:S(2)}) copy-start(bf16[320,2048]{1,0:T(8,128)(2,1)} %copy-done.3) | copy-start | bytes 3932164
  434.0 693.1 %all-reduce.16.cloned.1.call-start = ((), (), s32[]{:S(2)}) async-start(), calls=%async_computation.3 | async-start | bytes 67108864 | tf_op jit(solution)/shard_map/psum | solution.py:100
  1127.0 24.9 %copy-start.1 = (f32[256,32768]{1,0:T(8,128)S(1)}, f32[256,32768]{1,0:T(8,128)}, u32[]{:S(2)}) copy-start(f32[256,32768]{1,0:T(8,128)} %all-reduce.16.cloned.1.call-done) | copy-start | bytes 100663296
  1171.3 11.9 %copy-start.2 = (f32[2048,256]{1,0:T(8,128)S(1)}, f32[2048,256]{1,0:T(8,128)}, u32[]{:S(2)}) copy-start(f32[2048,256]{1,0:T(8,128)} %get-tuple-element.64) | copy-start | bytes 6291460
  (1 other events, 2.1 us)
Sparse Core Ops, SparseCore 0:
  78.7 46.5 all-reduce.9
  152.9 44.8 all-reduce.11
  237.1 44.8 all-reduce.13
  434.1 298.1 all-reduce.17
  736.5 390.5 all-reduce.15
where the time goes:
time: 1200 us; the launch traced here: 1190 us
  waiting for transfers between devices  669 us (56%)
  other arithmetic  160 us (13%)
  matrix products  134 us (11%)
  local copies, waits for them, and re-layouts  118 us (10%)
  blocking collectives  94.8 us (8%)
  between operations  17.1 us (1%)
    psum x1, waiting for transfers between devices, local_step(): lax.psum(jnp.einsum('rb,rk->bk', s_emb, g_logits, preferred_element_type=...  382 us
    psum x1, waiting for transfers between devices, local_step(): lax.psum(mlp_backward(g_emb, student_x, saved, w_mid, w_out), ('vp', 'dp'))  242 us
    reshape x1, local copies, waits for them, and re-layouts, local_step(): logits = logits.reshape(n_img, ALL_CROPS, local_proto)  51.4 us
    psum x3, waiting for transfers between devices, local_step(): proto_sum = lax.psum(jnp.sum(q_mat, axis=0, keepdims=True), 'dp')  45 us
    convert_element_type x1, other arithmetic, local_step(): g_logits.reshape(n_img * ALL_CROPS, local_proto).astype(jnp.bfloat16)  39 us
    psum x1, blocking collectives, local_step(): q_mat = q_mat / lax.psum(jnp.sum(q_mat), ('vp', 'dp'))  34.7 us
    unnamed x43, local copies, waits for them, and re-layouts  34.4 us
    psum x1, blocking collectives, local_step(): lax.psum(jnp.sum(targets * (jnp.log(row_sum) - shifted)), ('vp', 'dp'))  32.5 us
  transfers between devices with their start and end apart: 5, of which 3 were waited for; matrix products, arithmetic and copies ran while one was open for 13% of the time, Pallas kernels for 0%

commit v1 on v0

v1 whole, which is shorter than its diff:
```python
import functools

import jax
import jax.numpy as jnp
from jax import lax
from jax.experimental import pallas as pl
from jax.experimental.pallas import tpu as pltpu
from jax.sharding import Mesh, PartitionSpec as P

ALL_CROPS = 10
GLOBAL_CROPS = 2
SINK_ITERS = 3
TEMP_STUDENT = 0.1
TEMP_TEACHER = 0.04


def gelu_slope(pre):
    cdf = 0.5 * (1.0 + lax.erf(pre * 0.7071067811865476))
    return cdf + pre * jnp.exp(-0.5 * pre * pre) * 0.3989422804014327


def mlp_forward(feats, w_in, b_in, w_mid, b_mid, w_out, b_out):
    pre_one = jnp.dot(feats, w_in, preferred_element_type=jnp.float32) + b_in.astype(jnp.float32)
    hid_one = jax.nn.gelu(pre_one, approximate=False).astype(jnp.bfloat16)
    pre_two = jnp.dot(hid_one, w_mid, preferred_element_type=jnp.float32) + b_mid.astype(jnp.float32)
    hid_two = jax.nn.gelu(pre_two, approximate=False).astype(jnp.bfloat16)
    proj = jnp.dot(hid_two, w_out, preferred_element_type=jnp.float32) + b_out.astype(jnp.float32)
    inv_norm = lax.rsqrt(jnp.sum(proj * proj, axis=-1, keepdims=True))
    unit = proj * inv_norm
    return unit.astype(jnp.bfloat16), (pre_one, hid_one, pre_two, hid_two, unit, inv_norm)


def mlp_project(feats, w_in, b_in, w_mid, b_mid, w_out, b_out):
    pre_one = jnp.dot(feats, w_in, preferred_element_type=jnp.float32) + b_in.astype(jnp.float32)
    hid_one = jax.nn.gelu(pre_one, approximate=False).astype(jnp.bfloat16)
    pre_two = jnp.dot(hid_one, w_mid, preferred_element_type=jnp.float32) + b_mid.astype(jnp.float32)
    hid_two = jax.nn.gelu(pre_two, approximate=False).astype(jnp.bfloat16)
    return jnp.dot(hid_two, w_out, preferred_element_type=jnp.float32) + b_out.astype(jnp.float32)


def mlp_backward(g_emb, feats, saved, w_mid, w_out):
    pre_one, hid_one, pre_two, hid_two, unit, inv_norm = saved
    g_proj = (g_emb - unit * jnp.sum(unit * g_emb, axis=-1, keepdims=True)) * inv_norm
    g_proj_lo = g_proj.astype(jnp.bfloat16)
    g_w_out = jnp.einsum('nh,nb->hb', hid_two, g_proj_lo, preferred_element_type=jnp.float32)
    g_hid_two = jnp.einsum('nb,hb->nh', g_proj_lo, w_out, preferred_element_type=jnp.float32)
    g_pre_two = g_hid_two.astype(jnp.bfloat16).astype(jnp.float32) * gelu_slope(pre_two)
    g_pre_two_lo = g_pre_two.astype(jnp.bfloat16)
    g_w_mid = jnp.einsum('ng,nh->gh', hid_one, g_pre_two_lo, preferred_element_type=jnp.float32)
    g_hid_one = jnp.einsum('nh,gh->ng', g_pre_two_lo, w_mid, preferred_element_type=jnp.float32)
    g_pre_one = g_hid_one.astype(jnp.bfloat16).astype(jnp.float32) * gelu_slope(pre_one)
    g_w_in = jnp.einsum('nf,nh->fh', feats, g_pre_one.astype(jnp.bfloat16), preferred_element_type=jnp.float32)
    return (g_w_in, jnp.sum(g_pre_one, axis=0), g_w_mid, jnp.sum(g_pre_two, axis=0), g_w_out, jnp.sum(g_proj, axis=0))


def col_normalize(protos):
    proto_f = protos.astype(jnp.float32)
    inv_col = lax.rsqrt(jnp.sum(proto_f * proto_f, axis=0, keepdims=True))
    unit = proto_f * inv_col
    return unit.astype(jnp.bfloat16), unit, inv_col


def col_normalize_backward(g_unit, unit, inv_col):
    return (g_unit - unit * jnp.sum(unit * g_unit, axis=0, keepdims=True)) * inv_col


def gather_rows(vals, axis_name):
    return lax.all_gather(vals.astype(jnp.float32), axis_name, axis=0, tiled=True)


def round_kernel(wide_ref, out_ref):
    out_ref[...] = wide_ref[...].astype(out_ref.dtype)


def round_rows(wide):
    rows, width = wide.shape
    block = pl.BlockSpec((rows // 4, width), lambda i: (i, 0))
    return pl.pallas_call(
        round_kernel, out_shape=jax.ShapeDtypeStruct((rows, width), jnp.bfloat16), grid=(4,),
        in_specs=[block], out_specs=block,
        cost_estimate=pl.CostEstimate(flops=rows * width, bytes_accessed=6 * rows * width, transcendentals=0))(wide)


def unit_rows(proj):
    return (proj * lax.rsqrt(jnp.sum(proj * proj, axis=-1, keepdims=True))).astype(jnp.bfloat16)


def view_major(rows, n_img, views):
    width = rows.shape[1]
    return rows.reshape(n_img, views, width).transpose(1, 0, 2).reshape(n_img * views, width)


LANES = 128
AXES = ('vp', 'y', 'x', 'core')


def my_place(sizes):
    flat = 0
    for name, size in zip(AXES, sizes):
        flat = flat * size + lax.axis_index(name)
    return flat


def place_of(flat, sizes):
    coords = []
    for size in reversed(sizes):
        coords.append(lax.rem(flat, size))
        flat = flat // size
    return tuple(reversed(coords))


def greet_all(sizes, n_dev):
    barrier = pltpu.get_barrier_semaphore()
    me = my_place(sizes)
    for step in range(1, n_dev):
        peer = lax.rem(me + step, n_dev)
        pl.semaphore_signal(barrier, inc=1, device_id=place_of(peer, sizes), device_id_type=pl.DeviceIdType.MESH)


def await_all(n_dev):
    pl.semaphore_wait(pltpu.get_barrier_semaphore(), n_dev - 1)


def exchange(send_ref, recv_ref, send_sem, recv_sem, sizes, n_dev):
    me = my_place(sizes)
    copies = []
    for step in range(1, n_dev):
        peer = lax.rem(me + step, n_dev)
        copy = pltpu.make_async_remote_copy(
            src_ref=send_ref, dst_ref=recv_ref.at[step], send_sem=send_sem.at[step], recv_sem=recv_sem.at[step],
            device_id=place_of(peer, sizes), device_id_type=pl.DeviceIdType.MESH)
        copy.start()
        copies.append(copy)
    for copy in copies:
        copy.wait()
    total = send_ref[...]
    for step in range(1, n_dev):
        total = total + recv_ref[step]
    return total


def eye_mask():
    rows = lax.broadcasted_iota(jnp.int32, (LANES, LANES), 0)
    cols = lax.broadcasted_iota(jnp.int32, (LANES, LANES), 1)
    return rows == cols


def to_lanes(column):
    return jnp.sum(jnp.where(eye_mask(), jnp.broadcast_to(column, (LANES, LANES)), 0.0), axis=0, keepdims=True)


def to_rows(line):
    return jnp.sum(jnp.where(eye_mask(), jnp.broadcast_to(line, (LANES, LANES)), 0.0), axis=1, keepdims=True)


def fold_lanes(tile):
    total = tile[:, :LANES]
    for start in range(LANES, tile.shape[1], LANES):
        total = total + tile[:, start:start + LANES]
    return total


def sink_kernel(sizes, n_proto, block, t_ref, v_ref, hi_ref, lo_ref, row_ref,
                exp_ref, col_ref, scale_ref, part_ref, send_ref, recv_ref, send_sem, recv_sem):
    n_dev = 1
    for size in sizes:
        n_dev *= size
    n_rows, width = exp_ref.shape
    groups = n_rows // LANES
    steps = width // block
    greet_all(sizes, n_dev)

    def fill(step, total):
        cols = pl.ds(pl.multiple_of(step * block, block), block)
        proto_f = v_ref[:, cols].astype(jnp.float32)
        unit = (proto_f * lax.rsqrt(jnp.sum(proto_f * proto_f, axis=0, keepdims=True))).astype(jnp.bfloat16)
        grown = jnp.exp(jnp.dot(t_ref[...], unit, preferred_element_type=jnp.float32) * (1.0 / TEMP_TEACHER))
        exp_ref[:, cols] = grown
        sums = jnp.sum(grown, axis=0, keepdims=True)
        return total + fold_lanes(sums)

    total = lax.fori_loop(0, steps, fill, jnp.zeros((1, LANES), jnp.float32))
    total = jnp.broadcast_to(jnp.sum(total, axis=1, keepdims=True), (1, LANES))
    scale_ref[...] = jnp.ones_like(scale_ref)
    await_all(n_dev)
    for it in range(SINK_ITERS):
        part_ref[...] = jnp.zeros_like(part_ref)

        lax.fori_loop(0, width // LANES, lambda s, c: sweep_at(s, c, exp_ref, scale_ref, col_ref, part_ref, n_proto), 0)
        for group in range(groups):
            rows = pl.ds(group * LANES, LANES)
            send_ref[it, group:group + 1, :] = to_lanes(jnp.sum(part_ref[rows, :], axis=1, keepdims=True))
        send_ref[it, groups:groups + 1, :] = total
        sums = exchange(send_ref.at[it], recv_ref.at[it], send_sem.at[it], recv_sem.at[it], sizes, n_dev)
        crop = sums[:groups]
        if it == 0:
            whole = sums[groups:groups + 1]
            crop = crop * (whole * (1.0 / whole))
        scale = 1.0 / (crop * n_rows)
        for group in range(groups):
            rows = pl.ds(group * LANES, LANES)
            scale_ref[rows, :] = jnp.broadcast_to(to_rows(scale[group:group + 1]), (LANES, LANES))
        if it == SINK_ITERS - 1:
            row_ref[...] = jnp.zeros_like(row_ref)
            row_ref[:groups, :] = crop * scale * n_rows

    def finish(step, carry):
        cols = pl.ds(pl.multiple_of(step * LANES, LANES), LANES)
        target = exp_ref[:, cols] * scale_ref[...] * col_ref[:, cols] * n_rows
        high = target.astype(jnp.bfloat16)
        hi_ref[:, cols] = high
        lo_ref[:, cols] = (target - high.astype(jnp.float32)).astype(jnp.bfloat16)
        return carry

    lax.fori_loop(0, width // LANES, finish, 0)


def sweep_at(step, carry, exp_ref, scale_ref, col_ref, part_ref, n_proto):
    cols = pl.ds(pl.multiple_of(step * LANES, LANES), LANES)
    grown = exp_ref[:, cols]
    col = 1.0 / (jnp.sum(grown * scale_ref[...], axis=0, keepdims=True) * n_proto)
    col_ref[:, cols] = col
    part_ref[...] += grown * col
    return carry


def sinkhorn(t_all, ema_own, sizes, n_proto):
    n_rows, depth = t_all.shape
    width = ema_own.shape[1]
    n_dev = 1
    for size in sizes:
        n_dev *= size
    vmem = pl.BlockSpec(memory_space=pltpu.VMEM)
    target = jax.ShapeDtypeStruct((n_rows, width), jnp.bfloat16)
    return pl.pallas_call(
        functools.partial(sink_kernel, sizes, n_proto, 512),
        out_shape=(target, target, jax.ShapeDtypeStruct((8, LANES), jnp.float32)),
        in_specs=[vmem] * 2, out_specs=(vmem,) * 3,
        scratch_shapes=[
            pltpu.VMEM((n_rows, width), jnp.float32), pltpu.VMEM((1, width), jnp.float32),
            pltpu.VMEM((n_rows, LANES), jnp.float32), pltpu.VMEM((n_rows, LANES), jnp.float32),
            pltpu.VMEM((SINK_ITERS, 8, LANES), jnp.float32), pltpu.VMEM((SINK_ITERS, n_dev, 8, LANES), jnp.float32),
            pltpu.SemaphoreType.DMA((SINK_ITERS, n_dev)), pltpu.SemaphoreType.DMA((SINK_ITERS, n_dev))],
        compiler_params=pltpu.CompilerParams(collective_id=0, has_side_effects=True, vmem_limit_bytes=40 << 20),
        cost_estimate=pl.CostEstimate(flops=20 * 10 ** 9, bytes_accessed=12 << 20, transcendentals=n_rows * width),
    )(t_all, ema_own)


def soft_kernel(rows, s_ref, v_ref, hi_ref, lo_ref, exp_ref, part_ref, exp_u_ref, hi_u_ref, lo_u_ref):
    @pl.when(pl.program_id(0) == 0)
    def _():
        part_ref[...] = jnp.zeros_like(part_ref)
        exp_u_ref[...] = jnp.zeros_like(exp_u_ref)
        hi_u_ref[...] = jnp.zeros_like(hi_u_ref)
        lo_u_ref[...] = jnp.zeros_like(lo_u_ref)

    proto_f = v_ref[...].astype(jnp.float32)
    unit = (proto_f * lax.rsqrt(jnp.sum(proto_f * proto_f, axis=0, keepdims=True))).astype(jnp.bfloat16)
    across = (((1,), (1,)), ((), ()))
    hi_u_ref[...] += lax.dot_general(hi_ref[...], unit, across, preferred_element_type=jnp.float32)
    lo_u_ref[...] += lax.dot_general(lo_ref[...], unit, across, preferred_element_type=jnp.float32)

    def one(step, carry):
        at = pl.ds(pl.multiple_of(step * rows, rows), rows)
        logits = jnp.dot(s_ref[at, :], unit, preferred_element_type=jnp.float32) * (1.0 / TEMP_STUDENT)
        grown = jnp.exp(logits)
        part_ref[at, :] += fold_lanes(grown)
        low = grown.astype(jnp.bfloat16)
        exp_ref[at, :] = low
        exp_u_ref[at, :] += lax.dot_general(low, unit, across, preferred_element_type=jnp.float32)
        return carry

    lax.fori_loop(0, s_ref.shape[0] // rows, one, 0)


def soft_pass(s_all, protos_own, hi, lo):
    n_student, depth = s_all.shape
    n_rows, width = hi.shape
    block = 512
    whole = lambda shape: pl.BlockSpec(shape, lambda k: (0, 0))
    cols = lambda height: pl.BlockSpec((height, block), lambda k: (0, k))
    wide = lambda height, span: jax.ShapeDtypeStruct((height, span), jnp.float32)
    return pl.pallas_call(
        functools.partial(soft_kernel, 640),
        grid=(width // block,),
        out_shape=(jax.ShapeDtypeStruct((n_student, width), jnp.bfloat16), wide(n_student, LANES),
                   wide(n_student, depth), wide(n_rows, depth), wide(n_rows, depth)),
        in_specs=[whole((n_student, depth)), cols(depth), cols(n_rows), cols(n_rows)],
        out_specs=(cols(n_student), whole((n_student, LANES)), whole((n_student, depth)),
                   whole((n_rows, depth)), whole((n_rows, depth))),
        compiler_params=pltpu.CompilerParams(dimension_semantics=('arbitrary',), vmem_limit_bytes=50 << 20),
        cost_estimate=pl.CostEstimate(flops=13 * 10 ** 9, bytes_accessed=35 << 20, transcendentals=n_student * width),
    )(s_all, protos_own, hi, lo)


def total_kernel(sizes, part_ref, out_ref, send_ref, recv_ref, send_sem, recv_sem):
    n_dev = 1
    for size in sizes:
        n_dev *= size
    greet_all(sizes, n_dev)
    send_ref[...] = jnp.zeros_like(send_ref)
    for group in range(part_ref.shape[0] // LANES):
        rows = pl.ds(group * LANES, LANES)
        send_ref[group:group + 1, :] = to_lanes(jnp.sum(part_ref[rows, :], axis=1, keepdims=True))
    await_all(n_dev)
    out_ref[...] = exchange(send_ref, recv_ref, send_sem, recv_sem, sizes, n_dev)


def total_rows(part, sizes):
    lines = -(-part.shape[0] // (8 * LANES)) * 8
    n_dev = 1
    for size in sizes:
        n_dev *= size
    vmem = pl.BlockSpec(memory_space=pltpu.VMEM)
    return pl.pallas_call(
        functools.partial(total_kernel, sizes),
        out_shape=jax.ShapeDtypeStruct((lines, LANES), jnp.float32), in_specs=[vmem], out_specs=vmem,
        scratch_shapes=[
            pltpu.VMEM((lines, LANES), jnp.float32), pltpu.VMEM((n_dev, lines, LANES), jnp.float32),
            pltpu.SemaphoreType.DMA((n_dev,)), pltpu.SemaphoreType.DMA((n_dev,))],
        compiler_params=pltpu.CompilerParams(collective_id=1, has_side_effects=True),
        cost_estimate=pl.CostEstimate(flops=10 ** 9, bytes_accessed=2 << 20, transcendentals=0),
    )(part)


def grad_kernel(factor, soft_ref, pair_ref, exp_ref, hi_ref, v_ref, out_ref):
    g_unit = jnp.dot(soft_ref[...], exp_ref[...], preferred_element_type=jnp.float32)
    g_unit = (g_unit - jnp.dot(pair_ref[...], hi_ref[...], preferred_element_type=jnp.float32)) * factor
    proto_f = v_ref[...].astype(jnp.float32)
    inv_col = lax.rsqrt(jnp.sum(proto_f * proto_f, axis=0, keepdims=True))
    unit = proto_f * inv_col
    out_ref[...] = (g_unit - unit * jnp.sum(unit * g_unit, axis=0, keepdims=True)) * inv_col


def grad_pass(soft, pair, exp_lo, hi, protos_own, factor):
    depth, n_student = soft.shape
    n_rows, width = hi.shape
    block = 512
    whole = lambda shape: pl.BlockSpec(shape, lambda k: (0, 0))
    cols = lambda height: pl.BlockSpec((height, block), lambda k: (0, k))
    return pl.pallas_call(
        functools.partial(grad_kernel, factor), grid=(width // block,),
        out_shape=jax.ShapeDtypeStruct((depth, width), jnp.float32),
        in_specs=[whole((depth, n_student)), whole((depth, n_rows)), cols(n_student), cols(n_rows), cols(depth)],
        out_specs=cols(depth),
        compiler_params=pltpu.CompilerParams(dimension_semantics=('arbitrary',), vmem_limit_bytes=40 << 20),
        cost_estimate=pl.CostEstimate(flops=7 * 10 ** 9, bytes_accessed=33 << 20, transcendentals=0),
    )(soft, pair, exp_lo, hi, protos_own)


def crop_counts():
    crop_idx = jnp.arange(ALL_CROPS)
    return (GLOBAL_CROPS - (crop_idx < GLOBAL_CROPS).astype(jnp.int32)).astype(jnp.float32)


def solution(mesh):
    vp_size = mesh.shape['vp']
    dp_size = mesh.shape['dp']
    sizes = (vp_size, dp_size // 4, 2, 2)
    fine = Mesh(mesh.devices.reshape(sizes), AXES)
    data = ('y', 'x', 'core')

    def local_step(student_x, teacher_x, w_in, b_in, w_mid, b_mid, w_out, b_out, protos,
                   ema_w_in, ema_b_in, ema_w_mid, ema_b_mid, ema_w_out, ema_b_out, ema_protos):
        n_img = student_x.shape[0] // ALL_CROPS
        part = protos.shape[1] // dp_size
        n_proto = protos.shape[1] * vp_size
        n_rows = GLOBAL_CROPS * n_img * dp_size
        n_student = ALL_CROPS * n_img * dp_size
        depth = w_out.shape[1]
        core = lax.axis_index('core')
        data_idx = (lax.axis_index('y') * 2 + lax.axis_index('x')) * 2 + core
        protos_own = lax.dynamic_slice_in_dim(protos, data_idx * part, part, axis=1)
        ema_own = lax.dynamic_slice_in_dim(ema_protos, data_idx * part, part, axis=1)

        own_x = view_major(student_x, n_img, ALL_CROPS)
        own_tx = view_major(teacher_x, n_img, GLOBAL_CROPS)
        t_proj = mlp_project(own_tx, ema_w_in, ema_b_in, ema_w_mid, ema_b_mid, ema_w_out, ema_b_out)
        s_proj = mlp_project(own_x, w_in, b_in, w_mid, b_mid, w_out, b_out)
        both = gather_rows(jnp.concatenate([t_proj, s_proj], axis=0)[None], data)
        both, own_x = lax.optimization_barrier((both, own_x))
        t_all = unit_rows(both[:, :t_proj.shape[0]].reshape(n_rows, depth))
        s_all = unit_rows(both[:, t_proj.shape[0]:].reshape(n_student, depth))
        half_x = round_rows(gather_rows(own_x, ('y', 'x')))

        q_hi, q_lo, q_row = sinkhorn(t_all, ema_own, sizes, n_proto)
        exp_lo, row_part, exp_u, hi_u, lo_u = soft_pass(s_all, protos_own, q_hi, q_lo)
        row_sum = total_rows(row_part, sizes)

        scale = 1.0 / (n_img * dp_size * GLOBAL_CROPS * (ALL_CROPS - 1))
        counts = jnp.broadcast_to(crop_counts()[None, :, None], (dp_size, ALL_CROPS, n_img)).reshape(n_student)
        row_line = row_sum.reshape(-1)[:n_student]
        weight = counts / row_line
        s_views = s_all.astype(jnp.float32).reshape(dp_size, ALL_CROPS, n_img, depth)
        s_pair = (jnp.sum(s_views, axis=1, keepdims=True) - s_views[:, :GLOBAL_CROPS]).reshape(n_rows, depth)
        s_soft = s_all.astype(jnp.float32) * weight[:, None]
        g_own = grad_pass(s_soft.T.astype(jnp.bfloat16), s_pair.T.astype(jnp.bfloat16), exp_lo, q_hi, protos_own,
                          scale / TEMP_STUDENT)

        def targets_of(per_teacher):
            width = per_teacher.shape[-1]
            per_view = per_teacher.reshape(dp_size, GLOBAL_CROPS, n_img, width)
            pad = jnp.pad(per_view, ((0, 0), (0, ALL_CROPS - GLOBAL_CROPS), (0, 0), (0, 0)))
            return (jnp.sum(per_view, axis=1, keepdims=True) - pad).reshape(n_student, width)

        g_part = (weight[:, None] * exp_u - targets_of(hi_u)) * (scale / TEMP_STUDENT)
        hit_part = jnp.sum(s_pair * (hi_u + lo_u))
        packed = jnp.concatenate([g_part, jnp.broadcast_to(hit_part, (8, depth))], axis=0)
        packed, half_x = lax.optimization_barrier((packed, half_x))
        packed = lax.psum(packed, AXES)
        t_row = targets_of(q_row[:n_rows // LANES].reshape(n_rows, 1)).reshape(n_student)
        loss = (jnp.sum(t_row * jnp.log(row_line)) - packed[n_student, 0] / TEMP_STUDENT) * scale
        packed, g_own = lax.optimization_barrier((packed, g_own))
        g_protos = lax.all_gather(g_own, data, axis=1, tiled=True)

        per_dev = n_student // dp_size
        g_emb = packed[:n_student].reshape(dp_size // 2, 2, per_dev, depth)
        g_emb = lax.dynamic_slice_in_dim(g_emb, core, 1, axis=1).reshape(n_student // 2, depth)
        _, saved = mlp_forward(half_x, w_in, b_in, w_mid, b_mid, w_out, b_out)
        grads = mlp_backward(g_emb, half_x, saved, w_mid, w_out)
        swap = lambda g: g + lax.ppermute(g, 'core', [(0, 1), (1, 0)])
        biases = swap(jnp.concatenate([grads[1], grads[3], grads[5]]))
        b_grads = jnp.split(biases, [b_in.shape[0], b_in.shape[0] + b_mid.shape[0]])
        return (loss, swap(grads[0]), b_grads[0], swap(grads[2]), b_grads[1], swap(grads[4]), b_grads[2], g_protos)

    by_rows = P(data, None)
    by_cols = P(None, 'vp')
    replicated = P()
    head_specs = (replicated,) * 6
    in_specs = (by_rows, by_rows) + head_specs + (by_cols,) + head_specs + (by_cols,)
    out_specs = (replicated,) * 7 + (by_cols,)
    return jax.shard_map(local_step, mesh=fine, in_specs=in_specs, out_specs=out_specs, check_vma=False)
```

time: 1200 us -> 518 us (0.43)
  waiting for transfers between devices: 669 us -> 99.3 us
  other arithmetic: 160 us -> 62.3 us
  blocking collectives: 94.8 us -> 0 us
  Pallas kernels: 0 us -> 86.8 us
  local copies, waits for them, and re-layouts: 118 us -> 70.3 us
  matrix products: 134 us -> 170 us
    psum x5 -> x1, waiting for transfers between devices: 669 us -> 52.1 us  [local_step(): packed = lax.psum(packed, AXES)]
    pallas_call x0 -> x5, Pallas kernels: none -> 86.8 us  [the longest x1 32.6 us: sinkhorn(): pl.pallas_call(functools.partial(sink_kernel, sizes, n_proto, 512), out_s...]
    psum x5 -> x0, blocking collectives: 85.4 us -> none  [the longest x1 34.7 us: local_step(): q_mat = q_mat / lax.psum(jnp.sum(q_mat), ('vp', 'dp'))]
    reduce_sum x11 -> x8, other arithmetic: 91.7 us -> 9.9 us  [the longest x2 3.87 us: unit_rows(): jnp.sum(proj * proj, axis=-1, keepdims=True)]
    reshape x2 -> x7, local copies, waits for them, and re-layouts: 62 us -> 12.3 us  [the longest x1 3.7 us: local_step(): s_all = unit_rows(both[:, t_proj.shape[0]:].reshape(n_student, depth))]
    dot_general x4, matrix products: 72.8 us -> 34.9 us  [the longest x1 21.6 us: mlp_project(): jnp.dot(hid_one, w_mid, preferred_element_type=jnp.float32)]
    add x0 -> x4, other arithmetic: none -> 35.1 us  [local_step(): swap = lambda g: g + lax.ppermute(g, 'core', [(0, 1), (1, 0)])]
    all_gather x0 -> x3, waiting for transfers between devices: none -> 31.1 us  [the longest x2 31.1 us: gather_rows(): lax.all_gather(vals.astype(jnp.float32), axis_name, axis=0, tiled=True)]
  transfers between devices with their start and end apart: 5 -> 8, of which waited for: 3 -> 3; matrix products, arithmetic and copies ran while one was open for 13% -> 44% of each run, Pallas kernels for 0% -> 16%
where the time goes in v1:
time: 518 us; the launch traced here: 507 us
  matrix products  170 us (33%)
  waiting for transfers between devices  99.3 us (19%)
  Pallas kernels  86.8 us (17%)
  local copies, waits for them, and re-layouts  70.3 us (14%)
  other arithmetic  62.3 us (12%)
  between operations  17.1 us (3%)
    psum x1, waiting for transfers between devices, local_step(): packed = lax.psum(packed, AXES)  52.1 us
    dot_general x1, matrix products, mlp_forward(): jnp.dot(hid_one, w_mid, preferred_element_type=jnp.float32)  37 us
    add x4, other arithmetic, local_step(): swap = lambda g: g + lax.ppermute(g, 'core', [(0, 1), (1, 0)])  35.1 us
    unnamed x57, local copies, waits for them, and re-layouts  34.2 us
    dot_general x1, matrix products, mlp_forward(): jnp.dot(feats, w_in, preferred_element_type=jnp.float32)  33.9 us
    pallas_call x1, Pallas kernels, sinkhorn(): pl.pallas_call(functools.partial(sink_kernel, sizes, n_proto, 512), out_s...  32.6 us
    all_gather x2, waiting for transfers between devices, gather_rows(): lax.all_gather(vals.astype(jnp.float32), axis_name, axis=0, tiled=True)  31.1 us
    pallas_call x1, Pallas kernels, soft_pass(): pl.pallas_call(functools.partial(soft_kernel, 640), grid=(width // block,...  26.6 us
  transfers between devices with their start and end apart: 8, of which 3 were waited for; matrix products, arithmetic and copies ran while one was open for 44% of the time, Pallas kernels for 16%

profile of v1, /device:TPU:0, one launch (start us, length us, event | category | flops | bytes accessed | tf_op | source)
XLA Modules:
  0.0 507.4 jit_solution(5645254740076269826)
XLA Ops:
  15.3 5.1 %fusion.92 = bf16[64,2048]{1,0:T(8,128)(2,1)S(1)} fusion(bf16[64,1536]{1,0:T(8,128)(2,1)S(1)} %bitcast.66, bf16[1536,2048]{1,0:T(8,128)(2,1)} %param.25, f32[2048]{0:T(1024)S(1)} %convert_element_type.106), kind=kOutput, calls=%fused_computation.147 | convolution fusion | flops 411303936 | bytes 6758400 | tf_op jit(solution)/shard_map/dot_general | solution.py:34
  20.5 21.6 %fusion.37 = bf16[320,2048]{1,0:T(8,128)(2,1)} fusion(bf16[2048,2048]{1,0:T(8,128)(2,1)} %param.20, f32[2048]{0:T(1024)S(1)} %convert_element_type.113, bf16[320,1536]{1,0:T(8,128)(2,1)S(1)} %bitcast.61, bf16[1536,2048]{1,0:T(8,128)(2,1)} %param.18, f32[2048]{0:T(1024)S(1)} %convert_element_type.111), kind=kOutput, calls=%fused_computation.64 | convolution fusion | flops 4784128000 | bytes 16990208 | tf_op jit(solution)/shard_map/dot_general | solution.py:36
  43.9 6.3 %convolution_add_fusion.6 = f32[64,256]{1,0:T(8,128)S(1)} fusion(bf16[2048,256]{1,0:T(8,128)(2,1)} %param.29, bf16[64,2048]{1,0:T(8,128)(2,1)S(1)} %fusion.92, bf16[2048,2048]{1,0:T(8,128)(2,1)} %param.27, f32[2048]{0:T(1024)S(1)} %convert_element_type.108, f32[256]{0:T(256)S(1)} %convert_element_type.110), kind=kOutput, calls=%fused_computation.142 | convolution fusion | flops 612646912 | bytes 9774080 | tf_op jit(solution)/shard_map/dot_general | solution.py:38
  51.1 31.1 %all-gather.9.cloned.1.call-done = f32[3072,256]{1,0:T(8,128)} async-done(((f32[384,256]{1,0:T(8,128)}), f32[3072,256]{1,0:T(8,128)}) %all-gather.9.cloned.1.call-update) | async-done | bytes 3145744 | tf_op jit(solution)/shard_map/all_gather | solution.py:68
  84.0 4.1 constant_dynamic-slice_fusion.1
  92.2 3.7 copy.42
  102.4 32.6 %shard_map.215 = (bf16[512,4096]{1,0:T(8,128)(2,1)S(1)}, bf16[512,4096]{1,0:T(8,128)(2,1)S(1)}, f32[8,128]{1,0:T(8,128)S(1)}) custom-call(bf16[512,256]{1,0:T(8,128)(2,1)S(1)} %fusion.96.t_ref, bf16[256,4096]{1,0:T(8,128)(2,1)S(1)} %get-tuple-element.59.v_ref), custom_call_target="tpu_custom_call" | custom-call | flops 20000000000 | bytes 12582912 | tf_op jit(solution)/shard_map/pallas_call | solution.py:235
  139.0 26.6 %shard_map.216 = (bf16[2560,4096]{1,0:T(8,128)(2,1)}, f32[2560,128]{1,0:T(8,128)S(1)}, f32[2560,256]{1,0:T(8,128)}, f32[512,256]{1,0:T(8,128)S(1)}, f32[512,256]{1,0:T(8,128)S(1)}) custom-call(bf16[2560,256]{1,0:T(8,128)(2,1)S(1)} %copy-done.6, bf16[256,4096]{1,0:T(8,128)(2,1)} %get-tuple-element.58.v_ref, bf16[512,4096]{1,0:T(8,128)(2,1)} %copy-done.4, ...), custom_call_target="tpu_custom_call" | custom-call | flops 12999999488 | bytes 36700160 | tf_op jit(solution)/shard_map/pallas_call | solution.py:283
  169.2 3.2 copy.45
  175.6 8.7 %shard_map.217 = f32[24,128]{1,0:T(8,128)} custom-call(f32[2560,128]{1,0:T(8,128)} %copy-done.7), custom_call_target="tpu_custom_call" | custom-call | flops 1000000000 | bytes 2097152 | tf_op jit(solution)/shard_map/pallas_call | solution.py:315
  193.0 5.7 %shard_map.218 = bf16[1280,1536]{1,0:T(8,128)(2,1)} custom-call(f32[1280,1536]{1,0:T(8,128)} %all-gather.5.cloned.1.call-done.wide_ref), custom_call_target="tpu_custom_call" | custom-call | flops 1966080 | bytes 11796480 | tf_op jit(solution)/shard_map/pallas_call | solution.py:78
  203.5 13.2 %shard_map.219 = f32[256,4096]{1,0:T(8,128)S(1)} custom-call(bf16[256,2560]{1,0:T(8,128)(2,1)S(1)} %copy-done.3, bf16[256,512]{1,0:T(8,128)(2,1)S(1)} %bitcast.53, bf16[2560,4096]{1,0:T(8,128)(2,1)} %get-tuple-element.33.exp_ref, bf16[512,4096]{1,0:T(8,128)(2,1)S(1)} %copy-done.5, bf16[256,4096]{1,0:T(8,128)(2,1)S(1)} %copy-done.2), custom_call_target="tpu_custom_call" | custom-call | flops 7000000000 | bytes 34603008 | tf_op jit(solution)/shard_map/pallas_call | solution.py:341
  218.7 52.1 %all-reduce.5.cloned.1.call-done = f32[2568,256]{0,1:T(8,128)} async-done(((f32[2568,256]{0,1:T(8,128)}), f32[2568,256]{0,1:T(8,128)}) %all-reduce.5.cloned.1.call-update) | async-done | bytes 2629648 | tf_op jit(solution)/shard_map/psum | solution.py:410
  270.9 33.9 %fusion.2 = (bf16[1280,2048]{1,0:T(8,128)(2,1)S(1)}, f32[1280,2048]{1,0:T(8,128)}) fusion(f32[2048]{0:T(1024)S(1)} %convert_element_type.111, bf16[1280,1536]{1,0:T(8,128)(2,1)} %shard_map.218, bf16[1536,2048]{1,0:T(8,128)(2,1)} %param.18), kind=kOutput, calls=%fused_computation.6 | convolution fusion | flops 8226078720 | bytes 25960448 | tf_op jit(solution)/shard_map/dot_general | solution.py:23
  304.8 37.0 %fusion.5 = (bf16[1280,2048]{1,0:T(8,128)(2,1)S(1)}, f32[1280,2048]{1,0:T(8,128)}) fusion(f32[2048]{0:T(1024)S(1)} %copy-done.20, bf16[1280,2048]{1,0:T(8,128)(2,1)S(1)} %get-tuple-element.48, bf16[2048,2048]{1,0:T(8,128)(2,1)} %param.20), kind=kOutput, calls=%fused_computation.9 | convolution fusion | flops 10910433280 | bytes 29368320 | tf_op jit(solution)/shard_map/dot_general | solution.py:25
  358.2 8.5 %fusion.210 = (f32[2048]{0:T(1024)S(1)}, bf16[1280,2048]{1,0:T(8,128)(2,1)S(1)}) fusion(f32[1280,2048]{1,0:T(8,128)} %get-tuple-element.51, f32[2048]{0:T(1024)S(1)} %copy-done.20, bf16[1280,256]{0,1:T(8,128)(2,1)S(1)} %get-tuple-element.43, bf16[2048,256]{1,0:T(8,128)(2,1)S(1)} %copy-done), kind=kOutput, calls=%fused_computation.294 | convolution fusion | flops 1378875392 | bytes 17448960 | tf_op jit(solution)/shard_map/nb,hb->nh/dot_general | solution.py:46
  366.7 13.8 %fusion.38 = f32[2048,2048]{1,0:T(8,128)} fusion(bf16[1280,2048]{1,0:T(8,128)(2,1)S(1)} %bitcast.68, bf16[1280,2048]{1,0:T(8,128)(2,1)S(1)} %get-tuple-element.55), kind=kOutput, calls=%fused_computation.65 | convolution fusion | flops 10737418240 | bytes 27262976 | tf_op jit(solution)/shard_map/ng,nh->gh/dot_general | solution.py:49
  380.5 22.0 %fusion.211 = (f32[2048]{0:T(1024)S(1)}, bf16[1280,2048]{1,0:T(8,128)(2,1)}) fusion(f32[1280,2048]{1,0:T(8,128)} %get-tuple-element.49, f32[2048]{0:T(1024)S(1)} %convert_element_type.111, bf16[2048,2048]{1,0:T(8,128)(2,1)} %param.20, bf16[1280,2048]{1,0:T(8,128)(2,1)} %copy-done.24), kind=kOutput, calls=%fused_computation.295 | convolution fusion | flops 10774116352 | bytes 29376512 | tf_op jit(solution)/shard_map/nh,gh->ng/dot_general | solution.py:50
  402.5 13.3 %fusion.30 = f32[1536,2048]{1,0:T(8,128)} fusion(bf16[1280,1536]{1,0:T(8,128)(2,1)S(1)} %copy-done.13, bf16[1280,2048]{1,0:T(8,128)(2,1)} %get-tuple-element.57), kind=kOutput, calls=%fused_computation.52 | convolution fusion | flops 8053063680 | bytes 21757952 | tf_op jit(solution)/shard_map/nf,nh->fh/dot_general | solution.py:52
  416.4 4.1 fusion.212
  424.4 16.0 %collective-permute-done.1 = f32[4352]{0:T(1024)S(1)} collective-permute-done((f32[4352]{0:T(1024)S(1)}, f32[4352]{0:T(1024)S(1)}, u32[]{:S(2)}, u32[]{:S(2)}) %collective-permute-start.1) | collective-permute-done | bytes 17440 | tf_op jit(solution)/shard_map/ppermute | solution.py:421
  444.8 14.4 %add.147 = f32[1536,2048]{1,0:T(8,128)} add(f32[1536,2048]{1,0:T(8,128)} %fusion.30, f32[1536,2048]{1,0:T(8,128)} %collective-permute-done) | non-fusion elementwise | flops 3145728 | bytes 37748736 | tf_op jit(solution)/shard_map/add | solution.py:421
  459.2 17.5 %add.149 = f32[2048,2048]{1,0:T(8,128)} add(f32[2048,2048]{1,0:T(8,128)} %fusion.38, f32[2048,2048]{1,0:T(8,128)} %collective-permute-done.2) | non-fusion elementwise | flops 4194304 | bytes 50331648 | tf_op jit(solution)/shard_map/add | solution.py:421
  476.7 22.5 %copy.52 = f32[256,32768]{1,0:T(8,128)} copy(f32[256,32768]{1,0:T(8,128)} %all-gather.7.cloned.1.call-done) | data formatting | bytes 67108864
  (130 shorter events, 73.1 us)
Async XLA Ops:
  7.2 34.9 %copy-start = (bf16[2048,256]{1,0:T(8,128)(2,1)S(1)}, bf16[2048,256]{1,0:T(8,128)(2,1)}, u32[]{:S(2)}) copy-start(bf16[2048,256]{1,0:T(8,128)(2,1)} %param.22) | copy-start | bytes 3145732
  7.2 75.0 %all-gather.9.cloned.1.call-start = ((), (), s32[]{:S(2)}) async-start(), calls=%async_computation.3 | async-start | bytes 3538944 | tf_op jit(solution)/shard_map/all_gather | solution.py:68
  8.0 34.1 %copy-start.21 = (f32[256]{0:T(256)}, f32[256]{0:T(256)S(1)}, u32[]{:S(2)}) copy-start(f32[256]{0:T(256)S(1)} %convert_element_type.115) | copy-start | bytes 3076
  10.0 10.4 %copy-start.19 = (f32[2048]{0:T(1024)}, f32[2048]{0:T(1024)S(1)}, u32[]{:S(2)}) copy-start(f32[2048]{0:T(1024)S(1)} %convert_element_type.113) | copy-start | bytes 24580
  15.3 5.1 %copy-start.14 = (bf16[10,32,1536]{2,1,0:T(8,128)(2,1)S(1)}, bf16[10,32,1536]{2,1,0:T(8,128)(2,1)}, u32[]{:S(2)}) copy-start(bf16[10,32,1536]{2,1,0:T(8,128)(2,1)} %copy.41) | copy-start | bytes 2949124
  51.1 141.9 %all-gather.5.cloned.1.call-start = ((), (), s32[]{:S(2)}) async-start(), calls=%async_computation | async-start | bytes 9830400 | tf_op jit(solution)/shard_map/all_gather | solution.py:68
  83.7 187.1 %all-reduce.5.cloned.1.call-start = ((), (), s32[]{:S(2)}) async-start(), calls=%async_computation.1 | async-start | bytes 5505024 | tf_op jit(solution)/shard_map/psum | solution.py:410
  102.4 36.6 %copy-start.6 = (bf16[2560,256]{1,0:T(8,128)(2,1)S(1)}, bf16[2560,256]{1,0:T(8,128)(2,1)}, u32[]{:S(2)}) copy-start(bf16[2560,256]{1,0:T(8,128)(2,1)} %copy.43.s_ref) | copy-start | bytes 3932164
  165.6 10.0 %copy-start.7 = (f32[2560,128]{1,0:T(8,128)}, f32[2560,128]{1,0:T(8,128)S(1)}, u32[]{:S(2)}) copy-start(f32[2560,128]{1,0:T(8,128)S(1)} %get-tuple-element.26.part_ref) | copy-start | bytes 3932164
  184.4 4.3 copy-start.11
  193.0 7.0 %copy-start.2 = (bf16[256,4096]{1,0:T(8,128)(2,1)S(1)}, bf16[256,4096]{1,0:T(8,128)(2,1)}, u32[]{:S(2)}) copy-start(bf16[256,4096]{1,0:T(8,128)(2,1)} %get-tuple-element.58.v_ref) | copy-start | bytes 6291460
  198.7 278.0 %all-gather.7.cloned.1.call-start = ((), (), s32[]{:S(2)}) async-start(), calls=%async_computation.2 | async-start | bytes 37748736 | tf_op jit(solution)/shard_map/all_gather | solution.py:414
  270.9 33.9 %copy-start.20 = (f32[2048]{0:T(1024)S(1)}, f32[2048]{0:T(1024)}, u32[]{:S(2)}) copy-start(f32[2048]{0:T(1024)} %copy-done.19) | copy-start | bytes 24580
  304.8 37.1 %copy-start.25 = (bf16[1280,2048]{1,0:T(8,128)(2,1)}, bf16[1280,2048]{1,0:T(8,128)(2,1)S(1)}, u32[]{:S(2)}) copy-start(bf16[1280,2048]{1,0:T(8,128)(2,1)S(1)} %get-tuple-element.48) | copy-start | bytes 15728644
  304.8 37.1 %copy-start.22 = (f32[256]{0:T(256)S(1)}, f32[256]{0:T(256)}, u32[]{:S(2)}) copy-start(f32[256]{0:T(256)} %copy-done.21) | copy-start | bytes 3076
  356.3 10.3 %slice-start = ((s8[5242880]{0:T(1024)(128)(4,1)}), s8[4194304]{0:T(1024)(128)(4,1)S(1)}, s32[]{:S(2)}) async-start(s8[5242880]{0:T(1024)(128)(4,1)} %bitcast.67), calls=%async_computation.4 | async-start | bytes 8388608
  358.1 8.5 %slice-start.1 = ((s8[5242880]{0:T(1024)(128)(4,1)}), s8[1048576]{0:T(1024)(128)(4,1)S(1)}, s32[]{:S(2)}) async-start(s8[5242880]{0:T(1024)(128)(4,1)} %bitcast.67), calls=%async_computation.5 | async-start | bytes 2097152
  366.6 13.9 %copy-start.24 = (bf16[1280,2048]{1,0:T(8,128)(2,1)}, bf16[1280,2048]{1,0:T(8,128)(2,1)S(1)}, u32[]{:S(2)}) copy-start(bf16[1280,2048]{1,0:T(8,128)(2,1)S(1)} %get-tuple-element.55) | copy-start | bytes 15728644
  380.5 78.7 %collective-permute-start.2 = (f32[2048,2048]{1,0:T(8,128)}, f32[2048,2048]{1,0:T(8,128)}, u32[]{:S(2)}, u32[]{:S(2)}) collective-permute-start(f32[2048,2048]{1,0:T(8,128)} %fusion.38), channel_id=1, source_target_pairs={{0,1},{1,0},{2,3},{3,2},{4,5},{5,4},{6,7},{7,6},{8,9},{9,8},{10,11... | collective-permute-start | bytes 50331656 | tf_op jit(solution)/shard_map/ppermute | solution.py:421
  380.5 22.0 %copy-start.13 = (bf16[1280,1536]{1,0:T(8,128)(2,1)S(1)}, bf16[1280,1536]{1,0:T(8,128)(2,1)}, u32[]{:S(2)}) copy-start(bf16[1280,1536]{1,0:T(8,128)(2,1)} %shard_map.218) | copy-start | bytes 11796484
  415.8 4.9 copy-start.18
  415.8 28.9 %collective-permute-start = (f32[1536,2048]{1,0:T(8,128)}, f32[1536,2048]{1,0:T(8,128)}, u32[]{:S(2)}, u32[]{:S(2)}) collective-permute-start(f32[1536,2048]{1,0:T(8,128)} %fusion.30), channel_id=1, source_target_pairs={{0,1},{1,0},{2,3},{3,2},{4,5},{5,4},{6,7},{7,6},{8,9},{9,8},{10,11... | collective-permute-start | bytes 37748744 | tf_op jit(solution)/shard_map/ppermute | solution.py:421
  420.5 21.1 %collective-permute-start.3 = (f32[2048,256]{1,0:T(8,128)S(1)}, f32[2048,256]{1,0:T(8,128)}, u32[]{:S(2)}, u32[]{:S(2)}) collective-permute-start(f32[2048,256]{1,0:T(8,128)S(1)} %fusion.212), channel_id=1, source_target_pairs={{0,1},{1,0},{2,3},{3,2},{4,5},{5,4},{6,7},{7,6},{8,9},{9,8},{10,11... | collective-permute-start | bytes 6291464 | tf_op jit(solution)/shard_map/ppermute | solution.py:421
  420.8 19.6 %collective-permute-start.1 = (f32[4352]{0:T(1024)S(1)}, f32[4352]{0:T(1024)S(1)}, u32[]{:S(2)}, u32[]{:S(2)}) collective-permute-start(f32[4352]{0:T(1024)S(1)} %pad_maximum_fusion.1), channel_id=1, source_target_pairs={{0,1},{1,0},{2,3},{3,2},{4,5},{5,4},{6,7},{7,6},{8,9},{9,8},{10,11... | collective-permute-start | bytes 52232 | tf_op jit(solution)/shard_map/ppermute | solution.py:421
  (12 other events, 31.3 us)
Sparse Core Ops, SparseCore 0:
  51.2 30.9 all-gather.8
  84.0 80.9 all-gather.4
  198.8 71.9 all-reduce.4
  272.5 157.6 all-gather.6

commit v2 on v1

--- a/solution.py
+++ b/solution.py
@@ -28,14 +28,6 @@
     inv_norm = lax.rsqrt(jnp.sum(proj * proj, axis=-1, keepdims=True))
     unit = proj * inv_norm
     return unit.astype(jnp.bfloat16), (pre_one, hid_one, pre_two, hid_two, unit, inv_norm)
-
-
-def mlp_project(feats, w_in, b_in, w_mid, b_mid, w_out, b_out):
-    pre_one = jnp.dot(feats, w_in, preferred_element_type=jnp.float32) + b_in.astype(jnp.float32)
-    hid_one = jax.nn.gelu(pre_one, approximate=False).astype(jnp.bfloat16)
-    pre_two = jnp.dot(hid_one, w_mid, preferred_element_type=jnp.float32) + b_mid.astype(jnp.float32)
-    hid_two = jax.nn.gelu(pre_two, approximate=False).astype(jnp.bfloat16)
-    return jnp.dot(hid_two, w_out, preferred_element_type=jnp.float32) + b_out.astype(jnp.float32)
 
 
 def mlp_backward(g_emb, feats, saved, w_mid, w_out):
@@ -79,10 +71,6 @@
         round_kernel, out_shape=jax.ShapeDtypeStruct((rows, width), jnp.bfloat16), grid=(4,),
         in_specs=[block], out_specs=block,
         cost_estimate=pl.CostEstimate(flops=rows * width, bytes_accessed=6 * rows * width, transcendentals=0))(wide)
-
-
-def unit_rows(proj):
-    return (proj * lax.rsqrt(jnp.sum(proj * proj, axis=-1, keepdims=True))).astype(jnp.bfloat16)
 
 
 def view_major(rows, n_img, views):
@@ -160,15 +148,93 @@
     return total
 
 
-def sink_kernel(sizes, n_proto, block, t_ref, v_ref, hi_ref, lo_ref, row_ref,
-                exp_ref, col_ref, scale_ref, part_ref, send_ref, recv_ref, send_sem, recv_sem):
+def head_kernel(chunk, tx_ref, sx_ref, bias_ref, *refs):
+    weights, (out_ref,), bufs, (hid_one, hid_two, sems) = refs[:6], refs[6:7], refs[7:13], refs[13:]
+    t_rows = tx_ref.shape[0]
+    order = (0, 3, 1, 4, 2, 5)
+    slot = {}
+    used = 0
+    for which in order:
+        slot[which] = used
+        span = min(chunk, weights[which].shape[1])
+        for step in range(weights[which].shape[1] // span):
+            cols = pl.ds(step * span, span)
+            pltpu.make_async_copy(weights[which].at[:, cols], bufs[which].at[:, cols], sems.at[used]).start()
+            used += 1
+
+    def layer(which, feats, bias_row, store):
+        buf = bufs[which]
+        span = min(chunk, buf.shape[1])
+
+        def one(step, carry):
+            cols = pl.ds(pl.multiple_of(step * span, span), span)
+            pltpu.make_async_copy(weights[which].at[:, cols], buf.at[:, cols], sems.at[slot[which] + step]).wait()
+            store(cols, jnp.dot(feats[...], buf[:, cols], preferred_element_type=jnp.float32) + bias_ref[bias_row, cols])
+            return carry
+
+        lax.fori_loop(0, buf.shape[1] // span, one, 0)
+
+    def hidden(ref, rows):
+        def store(cols, pre):
+            ref[rows, cols] = (0.5 * pre * (1.0 + lax.erf(pre * 0.7071067811865476))).astype(ref.dtype)
+        return store
+
+    def project(rows):
+        def store(cols, proj):
+            out_ref[rows, cols] = proj
+        return store
+
+    ours, theirs = pl.ds(t_rows, sx_ref.shape[0]), pl.ds(0, t_rows)
+    layer(0, tx_ref, slice(0, 1), hidden(hid_one, theirs))
+    layer(3, sx_ref, slice(3, 4), hidden(hid_one, ours))
+    layer(1, hid_one.at[theirs], slice(1, 2), hidden(hid_two, theirs))
+    layer(4, hid_one.at[ours], slice(4, 5), hidden(hid_two, ours))
+    layer(2, hid_two.at[theirs], slice(2, 3), project(theirs))
+    layer(5, hid_two.at[ours], slice(5, 6), project(ours))
+
+
+def head_pass(own_tx, own_x, teacher, student):
+    hidden = student[0].shape[1]
+    lines = [jnp.pad(b.astype(jnp.float32), (0, hidden - b.shape[0])) for b in
+             (teacher[1], teacher[3], teacher[5], student[1], student[3], student[5])]
+    biases = jnp.stack(lines + lines[:2])
+    weights = (teacher[0], teacher[2], teacher[4], student[0], student[2], student[4])
+    rows = own_tx.shape[0] + own_x.shape[0]
+    vmem, hbm = pl.BlockSpec(memory_space=pltpu.VMEM), pl.BlockSpec(memory_space=pl.ANY)
+    return pl.pallas_call(
+        functools.partial(head_kernel, 512),
+        out_shape=jax.ShapeDtypeStruct((rows, student[4].shape[1]), jnp.float32),
+        in_specs=[vmem] * 3 + [hbm] * 6, out_specs=vmem,
+        scratch_shapes=[pltpu.VMEM(w.shape, w.dtype) for w in weights]
+        + [pltpu.VMEM((rows, hidden), jnp.bfloat16)] * 2 + [pltpu.SemaphoreType.DMA((24,))],
+        compiler_params=pltpu.CompilerParams(vmem_limit_bytes=56 << 20),
+        cost_estimate=pl.CostEstimate(flops=10 ** 10, bytes_accessed=34 << 20, transcendentals=rows * hidden * 2),
+    )(own_tx, own_x, biases, *weights)
+
+
+def normal_rows(proj):
+    return (proj * lax.rsqrt(jnp.sum(proj * proj, axis=-1, keepdims=True))).astype(jnp.bfloat16)
+
+
+def sink_kernel(sizes, n_proto, block, both_ref, ema_ref, hi_ref, lo_ref, row_ref, s_ref,
+                t_ref, v_ref, exp_ref, col_ref, scale_ref, part_ref, send_ref, recv_ref, v_sem, send_sem, recv_sem):
     n_dev = 1
     for size in sizes:
         n_dev *= size
     n_rows, width = exp_ref.shape
     groups = n_rows // LANES
     steps = width // block
+    shards, per_dev, _ = both_ref.shape
+    t_rows = n_rows // shards
+    s_rows = per_dev - t_rows
     greet_all(sizes, n_dev)
+    first = pl.multiple_of(lax.rem(my_place(sizes), shards) * width, width)
+    fetch = pltpu.make_async_copy(ema_ref.at[:, pl.ds(first, width)], v_ref, v_sem)
+    fetch.start()
+    for shard in range(shards):
+        t_ref[pl.ds(shard * t_rows, t_rows), :] = normal_rows(both_ref[shard, :t_rows, :])
+        s_ref[pl.ds(shard * s_rows, s_rows), :] = normal_rows(both_ref[shard, t_rows:, :])
+    fetch.wait()
 
     def fill(step, total):
         cols = pl.ds(pl.multiple_of(step * block, block), block)
@@ -185,8 +251,8 @@
     await_all(n_dev)
     for it in range(SINK_ITERS):
         part_ref[...] = jnp.zeros_like(part_ref)
-
         lax.fori_loop(0, width // LANES, lambda s, c: sweep_at(s, c, exp_ref, scale_ref, col_ref, part_ref, n_proto), 0)
+        send_ref[it] = jnp.zeros((8, LANES), jnp.float32)
         for group in range(groups):
             rows = pl.ds(group * LANES, LANES)
             send_ref[it, group:group + 1, :] = to_lanes(jnp.sum(part_ref[rows, :], axis=1, keepdims=True))
@@ -224,29 +290,32 @@
     return carry
 
 
-def sinkhorn(t_all, ema_own, sizes, n_proto):
-    n_rows, depth = t_all.shape
-    width = ema_own.shape[1]
+def sinkhorn(both, ema_protos, sizes, n_proto, n_rows, width):
+    shards, per_dev, depth = both.shape
+    n_student = shards * per_dev - n_rows
     n_dev = 1
     for size in sizes:
         n_dev *= size
-    vmem = pl.BlockSpec(memory_space=pltpu.VMEM)
+    vmem, hbm = pl.BlockSpec(memory_space=pltpu.VMEM), pl.BlockSpec(memory_space=pl.ANY)
     target = jax.ShapeDtypeStruct((n_rows, width), jnp.bfloat16)
     return pl.pallas_call(
         functools.partial(sink_kernel, sizes, n_proto, 512),
-        out_shape=(target, target, jax.ShapeDtypeStruct((8, LANES), jnp.float32)),
-        in_specs=[vmem] * 2, out_specs=(vmem,) * 3,
+        out_shape=(target, target, jax.ShapeDtypeStruct((8, LANES), jnp.float32),
+                   jax.ShapeDtypeStruct((n_student, depth), jnp.bfloat16)),
+        in_specs=[vmem, hbm], out_specs=(vmem,) * 4,
         scratch_shapes=[
+            pltpu.VMEM((n_rows, depth), jnp.bfloat16), pltpu.VMEM((depth, width), jnp.bfloat16),
             pltpu.VMEM((n_rows, width), jnp.float32), pltpu.VMEM((1, width), jnp.float32),
             pltpu.VMEM((n_rows, LANES), jnp.float32), pltpu.VMEM((n_rows, LANES), jnp.float32),
             pltpu.VMEM((SINK_ITERS, 8, LANES), jnp.float32), pltpu.VMEM((SINK_ITERS, n_dev, 8, LANES), jnp.float32),
-            pltpu.SemaphoreType.DMA((SINK_ITERS, n_dev)), pltpu.SemaphoreType.DMA((SINK_ITERS, n_dev))],
+            pltpu.SemaphoreType.DMA, pltpu.SemaphoreType.DMA((SINK_ITERS, n_dev)),
+            pltpu.SemaphoreType.DMA((SINK_ITERS, n_dev))],
         compiler_params=pltpu.CompilerParams(collective_id=0, has_side_effects=True, vmem_limit_bytes=40 << 20),
         cost_estimate=pl.CostEstimate(flops=20 * 10 ** 9, bytes_accessed=12 << 20, transcendentals=n_rows * width),
-    )(t_all, ema_own)
-
-
-def soft_kernel(rows, s_ref, v_ref, hi_ref, lo_ref, exp_ref, part_ref, exp_u_ref, hi_u_ref, lo_u_ref):
+    )(both, ema_protos)
+
+
+def soft_kernel(rows, base_ref, s_ref, v_ref, hi_ref, lo_ref, exp_ref, part_ref, exp_u_ref, hi_u_ref, lo_u_ref):
     @pl.when(pl.program_id(0) == 0)
     def _():
         part_ref[...] = jnp.zeros_like(part_ref)
@@ -273,57 +342,181 @@
     lax.fori_loop(0, s_ref.shape[0] // rows, one, 0)
 
 
-def soft_pass(s_all, protos_own, hi, lo):
+def soft_pass(base, s_all, protos, hi, lo):
     n_student, depth = s_all.shape
     n_rows, width = hi.shape
     block = 512
-    whole = lambda shape: pl.BlockSpec(shape, lambda k: (0, 0))
-    cols = lambda height: pl.BlockSpec((height, block), lambda k: (0, k))
+    whole = lambda shape: pl.BlockSpec(shape, lambda k, base_ref: (0, 0))
+    cols = lambda height: pl.BlockSpec((height, block), lambda k, base_ref: (0, k))
+    own = pl.BlockSpec((depth, block), lambda k, base_ref: (0, base_ref[0] * (width // block) + k))
     wide = lambda height, span: jax.ShapeDtypeStruct((height, span), jnp.float32)
     return pl.pallas_call(
         functools.partial(soft_kernel, 640),
-        grid=(width // block,),
+        grid_spec=pltpu.PrefetchScalarGridSpec(
+            num_scalar_prefetch=1, grid=(width // block,),
+            in_specs=[whole((n_student, depth)), own, cols(n_rows), cols(n_rows)],
+            out_specs=(cols(n_student), whole((n_student, LANES)), whole((n_student, depth)),
+                       whole((n_rows, depth)), whole((n_rows, depth)))),
         out_shape=(jax.ShapeDtypeStruct((n_student, width), jnp.bfloat16), wide(n_student, LANES),
                    wide(n_student, depth), wide(n_rows, depth), wide(n_rows, depth)),
-        in_specs=[whole((n_student, depth)), cols(depth), cols(n_rows), cols(n_rows)],
-        out_specs=(cols(n_student), whole((n_student, LANES)), whole((n_student, depth)),
-                   whole((n_rows, depth)), whole((n_rows, depth))),
         compiler_params=pltpu.CompilerParams(dimension_semantics=('arbitrary',), vmem_limit_bytes=50 << 20),
         cost_estimate=pl.CostEstimate(flops=13 * 10 ** 9, bytes_accessed=35 << 20, transcendentals=n_student * width),
-    )(s_all, protos_own, hi, lo)
-
-
-def total_kernel(sizes, part_ref, out_ref, send_ref, recv_ref, send_sem, recv_sem):
+    )(base, s_all, protos, hi, lo)
+
+
+def crop_weights(lines, per_dev, n_img):
+    spot = (lax.broadcasted_iota(jnp.int32, (lines, LANES), 0) * LANES
+            + lax.broadcasted_iota(jnp.int32, (lines, LANES), 1))
+    is_global = lax.rem(spot, per_dev) < GLOBAL_CROPS * n_img
+    return jnp.where(is_global, float(GLOBAL_CROPS - 1), float(GLOBAL_CROPS))
+
+
+def emb_kernel(sizes, n_img, factor, part_ref, s_ref, exp_u_ref, hi_u_ref, lo_u_ref, out_ref, sum_ref, weight_ref,
+               line_ref, line_recv, wide_ref, g_ref, near_recv, acc_ref, piece_recv, piece_ref, gathered,
+               line_send_sem, line_recv_sem, near_send_sem, near_recv_sem,
+               piece_send_sem, piece_recv_sem, all_send_sem, all_recv_sem):
     n_dev = 1
     for size in sizes:
         n_dev *= size
+    chips = n_dev // 2
+    shards = n_dev // sizes[0]
+    n_student, depth = exp_u_ref.shape
+    per_dev = n_student // shards
+    groups = n_student // LANES
+    mesh_type = pl.DeviceIdType.MESH
+    me = my_place(sizes)
+    core = lax.rem(me, 2)
+    chip = me // 2
     greet_all(sizes, n_dev)
-    send_ref[...] = jnp.zeros_like(send_ref)
-    for group in range(part_ref.shape[0] // LANES):
+    line_ref[...] = jnp.zeros_like(line_ref)
+    for group in range(groups):
         rows = pl.ds(group * LANES, LANES)
-        send_ref[group:group + 1, :] = to_lanes(jnp.sum(part_ref[rows, :], axis=1, keepdims=True))
+        line_ref[group:group + 1, :] = to_lanes(jnp.sum(part_ref[rows, :], axis=1, keepdims=True))
+
+    def view_sum(shard, hits):
+        base = pl.multiple_of(shard * per_dev, n_img)
+        views = [s_ref[pl.ds(base + view * n_img, n_img), :].astype(jnp.float32) for view in range(ALL_CROPS)]
+        total = views[0]
+        for view in views[1:]:
+            total = total + view
+        for crop in range(GLOBAL_CROPS):
+            rows = pl.ds(pl.multiple_of((shard * GLOBAL_CROPS + crop) * n_img, n_img), n_img)
+            hits = hits + (total - views[crop]) * (hi_u_ref[rows, :] + lo_u_ref[rows, :])
+        return hits
+
+    hits = lax.fori_loop(0, shards, view_sum, jnp.zeros((n_img, depth), jnp.float32))
+    hits = jnp.sum(jnp.sum(hits, axis=1, keepdims=True), axis=0, keepdims=True)
+    line_ref[groups:groups + 1, :] = jnp.broadcast_to(hits, (1, LANES))
     await_all(n_dev)
-    out_ref[...] = exchange(send_ref, recv_ref, send_sem, recv_sem, sizes, n_dev)
-
-
-def total_rows(part, sizes):
-    lines = -(-part.shape[0] // (8 * LANES)) * 8
+    sums = exchange(line_ref, line_recv, line_send_sem, line_recv_sem, sizes, n_dev)
+    sum_ref[...] = sums
+    lines = sums.shape[0]
+    weight = crop_weights(lines, per_dev, n_img) / sums
+    weight_ref[...] = weight
+    for group in range(groups):
+        rows = pl.ds(group * LANES, LANES)
+        wide_ref[rows, :] = jnp.broadcast_to(to_rows(weight[group:group + 1]), (LANES, LANES))
+
+    def combine(shard, carry):
+        to_core = lax.rem(shard, 2)
+        base = pl.multiple_of(shard * per_dev, n_img)
+        land = pl.multiple_of((shard // 2) * per_dev, n_img)
+        tops = [hi_u_ref[pl.ds(pl.multiple_of((shard * GLOBAL_CROPS + crop) * n_img, n_img), n_img), :]
+                for crop in range(GLOBAL_CROPS)]
+        both = tops[0] + tops[1]
+        for view in range(ALL_CROPS):
+            rows = pl.ds(base + view * n_img, n_img)
+            target = both - tops[view] if view < GLOBAL_CROPS else both
+            wide = wide_ref[rows, :]
+            soft = exp_u_ref[rows, :] * jnp.concatenate([wide, wide], axis=1)
+            g_ref[to_core, pl.ds(land + view * n_img, n_img), :] = (soft - target) * factor
+        return carry
+
+    lax.fori_loop(0, shards, combine, 0)
+    near = pltpu.make_async_remote_copy(
+        src_ref=g_ref.at[1 - core], dst_ref=near_recv, send_sem=near_send_sem, recv_sem=near_recv_sem,
+        device_id=place_of(chip * 2 + (1 - core), sizes), device_id_type=mesh_type)
+    near.start()
+    near.wait()
+    acc_ref[...] = g_ref[core] + near_recv[...]
+    piece = acc_ref.shape[0] // chips
+    copies = []
+    for step in range(1, chips):
+        peer = lax.rem(chip + step, chips)
+        copy = pltpu.make_async_remote_copy(
+            src_ref=acc_ref.at[pl.ds(pl.multiple_of(peer * piece, n_img), piece)], dst_ref=piece_recv.at[step],
+            send_sem=piece_send_sem.at[step], recv_sem=piece_recv_sem.at[step],
+            device_id=place_of(peer * 2 + core, sizes), device_id_type=mesh_type)
+        copy.start()
+        copies.append(copy)
+    total = acc_ref[pl.ds(pl.multiple_of(chip * piece, n_img), piece), :]
+    for step in range(1, chips):
+        copies[step - 1].wait()
+        total = total + piece_recv[step]
+    piece_ref[...] = total
+    copies = []
+    for step in range(1, chips):
+        peer = lax.rem(chip + step, chips)
+        copy = pltpu.make_async_remote_copy(
+            src_ref=piece_ref, dst_ref=gathered.at[step], send_sem=all_send_sem.at[step], recv_sem=all_recv_sem.at[step],
+            device_id=place_of(peer * 2 + core, sizes), device_id_type=mesh_type)
+        copy.start()
+        copies.append(copy)
+    out_ref[pl.ds(pl.multiple_of(chip * piece, n_img), piece), :] = total
+    for step in range(1, chips):
+        copies[step - 1].wait()
+        owner = lax.rem(chip + chips - step, chips)
+        out_ref[pl.ds(pl.multiple_of(owner * piece, n_img), piece), :] = gathered[step]
+
+
+def emb_grads(part, s_all, exp_u, hi_u, lo_u, sizes, n_img, factor):
+    n_student, depth = exp_u.shape
+    lines = (n_student // LANES // 8 + 1) * 8
     n_dev = 1
     for size in sizes:
         n_dev *= size
+    half, chips = n_student // 2, n_dev // 2
     vmem = pl.BlockSpec(memory_space=pltpu.VMEM)
+    wide = jnp.float32
+    dma = pltpu.SemaphoreType.DMA
     return pl.pallas_call(
-        functools.partial(total_kernel, sizes),
-        out_shape=jax.ShapeDtypeStruct((lines, LANES), jnp.float32), in_specs=[vmem], out_specs=vmem,
+        functools.partial(emb_kernel, sizes, n_img, factor),
+        out_shape=(jax.ShapeDtypeStruct((half, depth), wide), jax.ShapeDtypeStruct((lines, LANES), wide),
+                   jax.ShapeDtypeStruct((lines, LANES), wide)),
+        in_specs=[vmem] * 5, out_specs=(vmem,) * 3,
         scratch_shapes=[
-            pltpu.VMEM((lines, LANES), jnp.float32), pltpu.VMEM((n_dev, lines, LANES), jnp.float32),
-            pltpu.SemaphoreType.DMA((n_dev,)), pltpu.SemaphoreType.DMA((n_dev,))],
-        compiler_params=pltpu.CompilerParams(collective_id=1, has_side_effects=True),
-        cost_estimate=pl.CostEstimate(flops=10 ** 9, bytes_accessed=2 << 20, transcendentals=0),
-    )(part)
-
-
-def grad_kernel(factor, soft_ref, pair_ref, exp_ref, hi_ref, v_ref, out_ref):
+            pltpu.VMEM((lines, LANES), wide), pltpu.VMEM((n_dev, lines, LANES), wide),
+            pltpu.VMEM((n_student, LANES), wide), pltpu.VMEM((2, half, depth), wide), pltpu.VMEM((half, depth), wide),
+            pltpu.VMEM((half, depth), wide), pltpu.VMEM((chips, half // chips, depth), wide),
+            pltpu.VMEM((half // chips, depth), wide), pltpu.VMEM((chips, half // chips, depth), wide),
+            dma((n_dev,)), dma((n_dev,)), dma, dma, dma((chips,)), dma((chips,)), dma((chips,)), dma((chips,))],
+        compiler_params=pltpu.CompilerParams(collective_id=1, has_side_effects=True, vmem_limit_bytes=40 << 20),
+        cost_estimate=pl.CostEstimate(flops=20 * 10 ** 9, bytes_accessed=8 << 20, transcendentals=0),
+    )(part, s_all, exp_u, hi_u, lo_u)
+
+
+def grad_kernel(factor, n_img, base_ref, weight_ref, s_ref, exp_ref, hi_ref, v_ref, out_ref, soft_ref, pair_ref):
+    @pl.when(pl.program_id(0) == 0)
+    def _():
+        n_student = s_ref.shape[0]
+        for group in range(n_student // LANES):
+            rows = pl.ds(group * LANES, LANES)
+            turned = s_ref[rows, :].astype(jnp.float32).T
+            soft_ref[:, rows] = (turned * weight_ref[group:group + 1, :]).astype(soft_ref.dtype)
+        per_dev = ALL_CROPS * n_img
+        pairs = []
+        for shard in range(n_student // per_dev):
+            views = [s_ref[pl.ds(shard * per_dev + view * n_img, n_img), :].astype(jnp.float32)
+                     for view in range(ALL_CROPS)]
+            total = views[0]
+            for view in views[1:]:
+                total = total + view
+            pairs += [total - views[crop] for crop in range(GLOBAL_CROPS)]
+        per_tile = LANES // n_img
+        for tile in range(len(pairs) // per_tile):
+            rows = jnp.concatenate(pairs[tile * per_tile:(tile + 1) * per_tile], axis=0)
+            pair_ref[:, pl.ds(tile * LANES, LANES)] = rows.T.astype(pair_ref.dtype)
+
     g_unit = jnp.dot(soft_ref[...], exp_ref[...], preferred_element_type=jnp.float32)
     g_unit = (g_unit - jnp.dot(pair_ref[...], hi_ref[...], preferred_element_type=jnp.float32)) * factor
     proto_f = v_ref[...].astype(jnp.float32)
@@ -332,25 +525,24 @@
     out_ref[...] = (g_unit - unit * jnp.sum(unit * g_unit, axis=0, keepdims=True)) * inv_col
 
 
-def grad_pass(soft, pair, exp_lo, hi, protos_own, factor):
-    depth, n_student = soft.shape
+def grad_pass(base, weight, s_all, exp_lo, hi, protos, factor, n_img):
+    n_student, depth = s_all.shape
     n_rows, width = hi.shape
     block = 512
-    whole = lambda shape: pl.BlockSpec(shape, lambda k: (0, 0))
-    cols = lambda height: pl.BlockSpec((height, block), lambda k: (0, k))
+    whole = lambda shape: pl.BlockSpec(shape, lambda k, base_ref: (0, 0))
+    cols = lambda height: pl.BlockSpec((height, block), lambda k, base_ref: (0, k))
+    own = pl.BlockSpec((depth, block), lambda k, base_ref: (0, base_ref[0] * (width // block) + k))
     return pl.pallas_call(
-        functools.partial(grad_kernel, factor), grid=(width // block,),
+        functools.partial(grad_kernel, factor, n_img),
+        grid_spec=pltpu.PrefetchScalarGridSpec(
+            num_scalar_prefetch=1, grid=(width // block,),
+            in_specs=[whole(weight.shape), whole((n_student, depth)), cols(n_student), cols(n_rows), own],
+            out_specs=cols(depth),
+            scratch_shapes=[pltpu.VMEM((depth, n_student), jnp.bfloat16), pltpu.VMEM((depth, n_rows), jnp.bfloat16)]),
         out_shape=jax.ShapeDtypeStruct((depth, width), jnp.float32),
-        in_specs=[whole((depth, n_student)), whole((depth, n_rows)), cols(n_student), cols(n_rows), cols(depth)],
-        out_specs=cols(depth),
         compiler_params=pltpu.CompilerParams(dimension_semantics=('arbitrary',), vmem_limit_bytes=40 << 20),
         cost_estimate=pl.CostEstimate(flops=7 * 10 ** 9, bytes_accessed=33 << 20, transcendentals=0),
-    )(soft, pair, exp_lo, hi, protos_own)
-
-
-def crop_counts():
-    crop_idx = jnp.arange(ALL_CROPS)
-    return (GLOBAL_CROPS - (crop_idx < GLOBAL_CROPS).astype(jnp.int32)).astype(jnp.float32)
+    )(base, weight, s_all, exp_lo, hi, protos)
 
 
 def solution(mesh):
@@ -367,55 +559,35 @@
         n_proto = protos.shape[1] * vp_size
         n_rows = GLOBAL_CROPS * n_img * dp_size
         n_student = ALL_CROPS * n_img * dp_size
-        depth = w_out.shape[1]
         core = lax.axis_index('core')
         data_idx = (lax.axis_index('y') * 2 + lax.axis_index('x')) * 2 + core
-        protos_own = lax.dynamic_slice_in_dim(protos, data_idx * part, part, axis=1)
-        ema_own = lax.dynamic_slice_in_dim(ema_protos, data_idx * part, part, axis=1)
+        base = data_idx.reshape(1)
 
         own_x = view_major(student_x, n_img, ALL_CROPS)
         own_tx = view_major(teacher_x, n_img, GLOBAL_CROPS)
-        t_proj = mlp_project(own_tx, ema_w_in, ema_b_in, ema_w_mid, ema_b_mid, ema_w_out, ema_b_out)
-        s_proj = mlp_project(own_x, w_in, b_in, w_mid, b_mid, w_out, b_out)
-        both = gather_rows(jnp.concatenate([t_proj, s_proj], axis=0)[None], data)
+        both = head_pass(own_tx, own_x, (ema_w_in, ema_b_in, ema_w_mid, ema_b_mid, ema_w_out, ema_b_out),
+                         (w_in, b_in, w_mid, b_mid, w_out, b_out))
+        both = gather_rows(both[None], data)
         both, own_x = lax.optimization_barrier((both, own_x))
-        t_all = unit_rows(both[:, :t_proj.shape[0]].reshape(n_rows, depth))
-        s_all = unit_rows(both[:, t_proj.shape[0]:].reshape(n_student, depth))
-        half_x = round_rows(gather_rows(own_x, ('y', 'x')))
-
-        q_hi, q_lo, q_row = sinkhorn(t_all, ema_own, sizes, n_proto)
-        exp_lo, row_part, exp_u, hi_u, lo_u = soft_pass(s_all, protos_own, q_hi, q_lo)
-        row_sum = total_rows(row_part, sizes)
-
+        half_wide = gather_rows(own_x, ('y', 'x'))
+
+        q_hi, q_lo, q_row, s_all = sinkhorn(both, ema_protos, sizes, n_proto, n_rows, part)
+        exp_lo, row_part, exp_u, hi_u, lo_u = soft_pass(base, s_all, protos, q_hi, q_lo)
         scale = 1.0 / (n_img * dp_size * GLOBAL_CROPS * (ALL_CROPS - 1))
-        counts = jnp.broadcast_to(crop_counts()[None, :, None], (dp_size, ALL_CROPS, n_img)).reshape(n_student)
-        row_line = row_sum.reshape(-1)[:n_student]
-        weight = counts / row_line
-        s_views = s_all.astype(jnp.float32).reshape(dp_size, ALL_CROPS, n_img, depth)
-        s_pair = (jnp.sum(s_views, axis=1, keepdims=True) - s_views[:, :GLOBAL_CROPS]).reshape(n_rows, depth)
-        s_soft = s_all.astype(jnp.float32) * weight[:, None]
-        g_own = grad_pass(s_soft.T.astype(jnp.bfloat16), s_pair.T.astype(jnp.bfloat16), exp_lo, q_hi, protos_own,
-                          scale / TEMP_STUDENT)
-
-        def targets_of(per_teacher):
-            width = per_teacher.shape[-1]
-            per_view = per_teacher.reshape(dp_size, GLOBAL_CROPS, n_img, width)
-            pad = jnp.pad(per_view, ((0, 0), (0, ALL_CROPS - GLOBAL_CROPS), (0, 0), (0, 0)))
-            return (jnp.sum(per_view, axis=1, keepdims=True) - pad).reshape(n_student, width)
-
-        g_part = (weight[:, None] * exp_u - targets_of(hi_u)) * (scale / TEMP_STUDENT)
-        hit_part = jnp.sum(s_pair * (hi_u + lo_u))
-        packed = jnp.concatenate([g_part, jnp.broadcast_to(hit_part, (8, depth))], axis=0)
-        packed, half_x = lax.optimization_barrier((packed, half_x))
-        packed = lax.psum(packed, AXES)
-        t_row = targets_of(q_row[:n_rows // LANES].reshape(n_rows, 1)).reshape(n_student)
-        loss = (jnp.sum(t_row * jnp.log(row_line)) - packed[n_student, 0] / TEMP_STUDENT) * scale
-        packed, g_own = lax.optimization_barrier((packed, g_own))
+        factor = scale / TEMP_STUDENT
+        g_emb, sums, weight = emb_grads(row_part, s_all, exp_u, hi_u, lo_u, sizes, n_img, factor)
+        g_own = grad_pass(base, weight, s_all, exp_lo, q_hi, protos, factor, n_img)
+        g_own, half_wide = lax.optimization_barrier((g_own, half_wide))
         g_protos = lax.all_gather(g_own, data, axis=1, tiled=True)
-
-        per_dev = n_student // dp_size
-        g_emb = packed[:n_student].reshape(dp_size // 2, 2, per_dev, depth)
-        g_emb = lax.dynamic_slice_in_dim(g_emb, core, 1, axis=1).reshape(n_student // 2, depth)
+        half_x = round_rows(half_wide)
+
+        per_view = q_row[:n_rows // LANES].reshape(dp_size, GLOBAL_CROPS, n_img)
+        pad = jnp.pad(per_view, ((0, 0), (0, ALL_CROPS - GLOBAL_CROPS), (0, 0)))
+        t_row = (jnp.sum(per_view, axis=1, keepdims=True) - pad).reshape(-1)
+        row_line = sums.reshape(-1)[:n_student]
+        hits = sums[n_student // LANES, 0]
+        loss = (jnp.sum(t_row * jnp.log(row_line)) - hits / TEMP_STUDENT) * scale
+
         _, saved = mlp_forward(half_x, w_in, b_in, w_mid, b_mid, w_out, b_out)
         grads = mlp_backward(g_emb, half_x, saved, w_mid, w_out)
         swap = lambda g: g + lax.ppermute(g, 'core', [(0, 1), (1, 0)])

time: 518 us -> 442 us (0.85)
  Pallas kernels: 86.8 us -> 148 us
  waiting for transfers between devices: 99.3 us -> 51 us
  matrix products: 170 us -> 133 us
  local copies, waits for them, and re-layouts: 70.3 us -> 40 us
  other arithmetic: 62.3 us -> 42.2 us
    pallas_call x3 -> x4, Pallas kernels: 48.5 us -> 108 us  [the longest x1 52.8 us: emb_grads(): pl.pallas_call(functools.partial(emb_kernel, sizes, n_img, factor), out_s...]
    psum x1 -> x0, waiting for transfers between devices: 52.1 us -> none  [local_step(): packed = lax.psum(packed, AXES)]
    dot_general x4 -> x0, matrix products: 34.9 us -> none  [the longest x1 21.6 us: mlp_project(): jnp.dot(hid_one, w_mid, preferred_element_type=jnp.float32)]
    reshape x5 -> x1, local copies, waits for them, and re-layouts: 9.88 us -> 0.09 us  [local_step(): per_view = q_row[:n_rows // LANES].reshape(dp_size, GLOBAL_CROPS, n_img)]
    convert_element_type x10 -> x3, other arithmetic: 10.3 us -> 1.94 us  [head_pass(): b.astype(jnp.float32)]
    reduce_sum x7 -> x2, other arithmetic: 8.38 us -> 0.64 us  [the longest x1 0.62 us: local_step(): loss = (jnp.sum(t_row * jnp.log(row_line)) - hits / TEMP_STUDENT) * scale]
    dynamic_slice x2 -> x0, local copies, waits for them, and re-layouts: 6.53 us -> none  [the longest x1 4.08 us: local_step(): protos_own = lax.dynamic_slice_in_dim(protos, data_idx * part, part, axis=1)]
    slice x4 -> x2, local copies, waits for them, and re-layouts: 6.16 us -> 0.51 us  [the longest x1 0.51 us: local_step(): hits = sums[n_student // LANES, 0]]
  transfers between devices with their start and end apart: 8 -> 7, of which waited for: 3 -> 2; matrix products, arithmetic and copies ran while one was open for 44% -> 40% of each run, Pallas kernels for 16% -> 31%
where the time goes in v2:
time: 442 us; the launch traced here: 433 us
  Pallas kernels  148 us (33%)
  matrix products  133 us (30%)
  waiting for transfers between devices  51 us (12%)
  other arithmetic  42.2 us (10%)
  local copies, waits for them, and re-layouts  40 us (9%)
  between operations  16.9 us (4%)
    pallas_call x1, Pallas kernels, emb_grads(): pl.pallas_call(functools.partial(emb_kernel, sizes, n_img, factor), out_s...  52.8 us
    dot_general x1, matrix products, mlp_forward(): jnp.dot(hid_one, w_mid, preferred_element_type=jnp.float32)  36 us
    add x4, other arithmetic, local_step(): swap = lambda g: g + lax.ppermute(g, 'core', [(0, 1), (1, 0)])  35.1 us
    pallas_call x1, Pallas kernels, sinkhorn(): pl.pallas_call(functools.partial(sink_kernel, sizes, n_proto, 512), out_s...  34.3 us
    dot_general x1, matrix products, mlp_forward(): jnp.dot(feats, w_in, preferred_element_type=jnp.float32)  34 us
    unnamed x35, local copies, waits for them, and re-layouts  32.2 us
    all_gather x2, waiting for transfers between devices, gather_rows(): lax.all_gather(vals.astype(jnp.float32), axis_name, axis=0, tiled=True)  31.1 us
    pallas_call x1, Pallas kernels, soft_pass(): pl.pallas_call(functools.partial(soft_kernel, 640), grid_spec=pltpu.Prefe...  26.4 us
  transfers between devices with their start and end apart: 7, of which 2 were waited for; matrix products, arithmetic and copies ran while one was open for 40% of the time, Pallas kernels for 31%

profile of v2, /device:TPU:0, one launch (start us, length us, event | category | flops | bytes accessed | tf_op | source)
XLA Modules:
  0.0 433.1 jit_solution(16816146978250396221)
XLA Ops:
  16.6 15.3 %shard_map.215 = f32[384,256]{1,0:T(8,128)} custom-call(bf16[64,1536]{1,0:T(8,128)(2,1)} %bitcast.34, bf16[320,1536]{1,0:T(8,128)(2,1)} %bitcast.32, f32[8,2048]{1,0:T(8,128)} %stack.41.bias_ref, bf16[1536,2048]{1,0:T(8,128)(2,1)} %refs_0_.1, bf16[2048,2048]{1,0:T(8,128)(2,1)} %refs_1_.1, bf16[2048,256]{1,0:T(8,128)(2,1)} %refs_2_.1, ...), custom_call_target="tpu_custom_call" | custom-call | flops 10000000000 | bytes 35651584 | tf_op jit(solution)/shard_map/pallas_call | solution.py:204
  32.0 31.1 %all-gather.9.cloned.1.call-done = f32[3072,256]{1,0:T(8,128)} async-done(((f32[384,256]{1,0:T(8,128)}), f32[3072,256]{1,0:T(8,128)}) %all-gather.9.cloned.1.call-update) | async-done | bytes 3145744 | tf_op jit(solution)/shard_map/all_gather | solution.py:60
  64.7 1.9 copy-done.3
  66.5 34.3 %shard_map.216 = (bf16[512,4096]{1,0:T(8,128)(2,1)S(1)}, bf16[512,4096]{1,0:T(8,128)(2,1)S(1)}, f32[8,128]{1,0:T(8,128)S(1)}, bf16[2560,256]{1,0:T(8,128)(2,1)S(1)}) custom-call(f32[8,384,256]{2,1,0:T(8,128)S(1)} %bitcast.30, bf16[256,32768]{1,0:T(8,128)(2,1)} %ema_ref.1), custom_call_target="tpu_custom_call" | custom-call | flops 20000000000 | bytes 12582912 | tf_op jit(solution)/shard_map/pallas_call | solution.py:301
  100.8 2.0 copy-done.1
  102.9 2.0 copy-done.4
  104.9 26.4 %shard_map.217 = (bf16[2560,4096]{1,0:T(8,128)(2,1)}, f32[2560,128]{1,0:T(8,128)S(1)}, f32[2560,256]{1,0:T(8,128)}, f32[512,256]{1,0:T(8,128)S(1)}, f32[512,256]{1,0:T(8,128)S(1)}) custom-call(s32[1]{0:T(128)} %bitcast.11.base_ref, bf16[2560,256]{1,0:T(8,128)(2,1)S(1)} %get-tuple-element.26.s_ref, bf16[256,32768]{1,0:T(8,128)(2,1)} %v_ref.3, ...), custom_call_target="tpu_custom_call" | custom-call | flops 12999999488 | bytes 36700160 | tf_op jit(solution)/shard_map/pallas_call | solution.py:353
  131.3 1.7 copy-done.5
  133.0 52.8 %shard_map.218 = (f32[1280,256]{1,0:T(8,128)S(1)}, f32[24,128]{1,0:T(8,128)S(1)}, f32[24,128]{1,0:T(8,128)S(1)}) custom-call(f32[2560,128]{1,0:T(8,128)S(1)} %get-tuple-element.29.part_ref, bf16[2560,256]{1,0:T(8,128)(2,1)S(1)} %get-tuple-element.26.s_ref, f32[2560,256]{1,0:T(8,128)S(1)} %copy-done.5, f32[512,256]{1,0:T(8,128)S(1)} %get-tuple-element.31.hi_u_ref, ...), custom_call_target="tpu_custom_call" | custom-call | flops 20000000000 | bytes 8388608 | tf_op jit(solution)/shard_map/pallas_call | solution.py:482
  185.9 13.9 %shard_map.219 = f32[256,4096]{1,0:T(8,128)S(1)} custom-call(s32[1]{0:T(128)} %bitcast.11.base_ref, f32[24,128]{1,0:T(8,128)S(1)} %get-tuple-element.34.weight_ref, bf16[2560,256]{1,0:T(8,128)(2,1)S(1)} %get-tuple-element.26.s_ref, bf16[2560,4096]{1,0:T(8,128)(2,1)} %get-tuple-element.35.exp_ref, bf16[512,4096]{1,0:T(8,128)(2,1)S(1)} %copy-done.2, ...), custom_call_target="tpu_custom_call" | custom-call | flops 7000000000 | bytes 34603008 | tf_op jit(solution)/shard_map/pallas_call | solution.py:535
  199.8 2.0 copy-done
  202.4 5.6 %shard_map.220 = bf16[1280,1536]{1,0:T(8,128)(2,1)} custom-call(f32[1280,1536]{1,0:T(8,128)} %all-gather.5.cloned.1.call-done.wide_ref), custom_call_target="tpu_custom_call" | custom-call | flops 1966080 | bytes 11796480 | tf_op jit(solution)/shard_map/pallas_call | solution.py:70
  208.0 34.0 %fusion.2 = (bf16[1280,2048]{1,0:T(8,128)(2,1)S(1)}, f32[1280,2048]{1,0:T(8,128)}) fusion(f32[2048]{0:T(1024)S(1)} %convert_element_type.50, bf16[1280,1536]{1,0:T(8,128)(2,1)} %shard_map.220, bf16[1536,2048]{1,0:T(8,128)(2,1)} %refs_3_.1), kind=kOutput, calls=%fused_computation.6 | convolution fusion | flops 8226078720 | bytes 25960448 | tf_op jit(solution)/shard_map/dot_general | solution.py:23
  242.0 36.0 %fusion.5 = (bf16[1280,2048]{1,0:T(8,128)(2,1)S(1)}, f32[1280,2048]{1,0:T(8,128)S(1)}) fusion(f32[2048]{0:T(1024)S(1)} %copy-done.9, bf16[1280,2048]{1,0:T(8,128)(2,1)S(1)} %get-tuple-element.44, bf16[2048,2048]{1,0:T(8,128)(2,1)} %refs_4_.1), kind=kOutput, calls=%fused_computation.9 | convolution fusion | flops 10910433280 | bytes 29368320 | tf_op jit(solution)/shard_map/dot_general | solution.py:25
  280.7 6.2 %fusion.41 = (f32[2048]{0:T(1024)S(1)}, bf16[1280,2048]{1,0:T(8,128)(2,1)S(1)}) fusion(f32[1280,2048]{1,0:T(8,128)S(1)} %get-tuple-element.47, f32[2048]{0:T(1024)S(1)} %copy-done.9, bf16[2048,256]{1,0:T(8,128)(2,1)S(1)} %copy-done.11, bf16[1280,256]{1,0:T(8,128)(2,1)S(1)} %get-tuple-element.41), kind=kOutput, calls=%fused_computation.71 | convolution fusion | flops 1378875392 | bytes 17448960 | tf_op jit(solution)/shard_map/nb,hb->nh/dot_general | solution.py:38
  286.9 18.4 %fusion.32 = f32[2048,2048]{1,0:T(8,128)} fusion(bf16[1280,2048]{1,0:T(8,128)(2,1)} %copy-done.16, bf16[1280,2048]{1,0:T(8,128)(2,1)S(1)} %get-tuple-element.51), kind=kOutput, calls=%fused_computation.55 | convolution fusion | flops 10737418240 | bytes 27262976 | tf_op jit(solution)/shard_map/ng,nh->gh/dot_general | solution.py:41
  305.3 22.0 %fusion.42 = (f32[2048]{0:T(1024)S(1)}, bf16[1280,2048]{1,0:T(8,128)(2,1)}) fusion(f32[1280,2048]{1,0:T(8,128)} %get-tuple-element.45, f32[2048]{0:T(1024)S(1)} %convert_element_type.50, bf16[2048,2048]{1,0:T(8,128)(2,1)} %refs_4_.1, bf16[1280,2048]{1,0:T(8,128)(2,1)} %copy-done.15), kind=kOutput, calls=%fused_computation.72 | convolution fusion | flops 10774116352 | bytes 29376512 | tf_op jit(solution)/shard_map/nh,gh->ng/dot_general | solution.py:42
  327.3 13.4 %fusion.30 = f32[1536,2048]{1,0:T(8,128)} fusion(bf16[1280,1536]{1,0:T(8,128)(2,1)S(1)} %copy-done.6, bf16[1280,2048]{1,0:T(8,128)(2,1)} %get-tuple-element.53), kind=kOutput, calls=%fused_computation.52 | convolution fusion | flops 8053063680 | bytes 21757952 | tf_op jit(solution)/shard_map/nf,nh->fh/dot_general | solution.py:44
  341.3 1.7 fusion.35
  346.2 19.9 %collective-permute-done.1 = f32[4352]{0:T(1024)S(1)} collective-permute-done((f32[4352]{0:T(1024)S(1)}, f32[4352]{0:T(1024)S(1)}, u32[]{:S(2)}, u32[]{:S(2)}) %collective-permute-start.1) | collective-permute-done | bytes 17440 | tf_op jit(solution)/shard_map/ppermute | solution.py:593
  367.3 3.2 add.75
  370.5 14.4 %add.72 = f32[1536,2048]{1,0:T(8,128)} add(f32[1536,2048]{1,0:T(8,128)} %fusion.30, f32[1536,2048]{1,0:T(8,128)} %collective-permute-done) | non-fusion elementwise | flops 3145728 | bytes 37748736 | tf_op jit(solution)/shard_map/add | solution.py:593
  384.9 17.5 %add.74 = f32[2048,2048]{1,0:T(8,128)} add(f32[2048,2048]{1,0:T(8,128)} %fusion.32, f32[2048,2048]{1,0:T(8,128)} %collective-permute-done.2) | non-fusion elementwise | flops 4194304 | bytes 50331648 | tf_op jit(solution)/shard_map/add | solution.py:593
  402.4 22.5 %copy.32 = f32[256,32768]{1,0:T(8,128)} copy(f32[256,32768]{1,0:T(8,128)} %all-gather.7.cloned.1.call-done) | data formatting | bytes 67108864
  (72 shorter events, 17.8 us)
Async XLA Ops:
  7.2 55.9 %all-gather.9.cloned.1.call-start = ((), (), s32[]{:S(2)}) async-start(), calls=%async_computation.2 | async-start | bytes 3538944 | tf_op jit(solution)/shard_map/all_gather | solution.py:60
  8.6 23.3 %copy-start.8 = (f32[2048]{0:T(1024)}, f32[2048]{0:T(1024)S(1)}, u32[]{:S(2)}) copy-start(f32[2048]{0:T(1024)S(1)} %convert_element_type.51) | copy-start | bytes 24580
  16.6 46.5 %copy-start.7 = (bf16[10,32,1536]{2,1,0:T(8,128)(2,1)S(1)}, bf16[10,32,1536]{2,1,0:T(8,128)(2,1)}, u32[]{:S(2)}) copy-start(bf16[10,32,1536]{2,1,0:T(8,128)(2,1)} %copy.28) | copy-start | bytes 2949124
  31.9 169.9 %all-gather.5.cloned.1.call-start = ((), (), s32[]{:S(2)}) async-start(), calls=%async_computation | async-start | bytes 9830400 | tf_op jit(solution)/shard_map/all_gather | solution.py:60
  64.6 337.9 %all-gather.7.cloned.1.call-start = ((), (), s32[]{:S(2)}) async-start(), calls=%async_computation.1 | async-start | bytes 37748736 | tf_op jit(solution)/shard_map/all_gather | solution.py:581
  64.6 1.9 copy-start.3
  100.8 2.0 copy-start.1
  102.9 2.0 copy-start.4
  131.3 1.7 copy-start.5
  133.0 52.9 %copy-start.2 = (bf16[512,4096]{1,0:T(8,128)(2,1)S(1)}, bf16[512,4096]{1,0:T(8,128)(2,1)}, u32[]{:S(2)}) copy-start(bf16[512,4096]{1,0:T(8,128)(2,1)} %copy-done.1) | copy-start | bytes 12582916
  185.9 16.0 %copy-start.10 = (bf16[256]{0:T(256)(128)(2,1)S(1)}, bf16[256]{0:T(256)(128)(2,1)}, u32[]{:S(2)}) copy-start(bf16[256]{0:T(256)(128)(2,1)} %param.23) | copy-start | bytes 1540
  199.8 2.0 copy-start
  208.0 34.0 %copy-start.9 = (f32[2048]{0:T(1024)S(1)}, f32[2048]{0:T(1024)}, u32[]{:S(2)}) copy-start(f32[2048]{0:T(1024)} %copy-done.8) | copy-start | bytes 24580
  242.0 36.1 %copy-start.16 = (bf16[1280,2048]{1,0:T(8,128)(2,1)}, bf16[1280,2048]{1,0:T(8,128)(2,1)S(1)}, u32[]{:S(2)}) copy-start(bf16[1280,2048]{1,0:T(8,128)(2,1)S(1)} %get-tuple-element.44) | copy-start | bytes 15728644
  242.0 36.1 %copy-start.11 = (bf16[2048,256]{1,0:T(8,128)(2,1)S(1)}, bf16[2048,256]{1,0:T(8,128)(2,1)}, u32[]{:S(2)}) copy-start(bf16[2048,256]{1,0:T(8,128)(2,1)} %refs_5_.1) | copy-start | bytes 3145732
  242.0 36.1 %copy-start.12 = (f32[256]{0:T(256)S(1)}, f32[256]{0:T(256)}, u32[]{:S(2)}) copy-start(f32[256]{0:T(256)} %convert_element_type.52) | copy-start | bytes 3076
  278.1 8.8 %copy-start.13 = (bf16[1280,2048]{1,0:T(8,128)(2,1)}, bf16[1280,2048]{1,0:T(8,128)(2,1)S(1)}, u32[]{:S(2)}) copy-start(bf16[1280,2048]{1,0:T(8,128)(2,1)S(1)} %get-tuple-element.46) | copy-start | bytes 15728644
  286.9 18.4 %copy-start.15 = (bf16[1280,2048]{1,0:T(8,128)(2,1)}, bf16[1280,2048]{1,0:T(8,128)(2,1)S(1)}, u32[]{:S(2)}) copy-start(bf16[1280,2048]{1,0:T(8,128)(2,1)S(1)} %get-tuple-element.51) | copy-start | bytes 15728644
  305.3 79.6 %collective-permute-start.2 = (f32[2048,2048]{1,0:T(8,128)}, f32[2048,2048]{1,0:T(8,128)}, u32[]{:S(2)}, u32[]{:S(2)}) collective-permute-start(f32[2048,2048]{1,0:T(8,128)} %fusion.32), channel_id=1, source_target_pairs={{0,1},{1,0},{2,3},{3,2},{4,5},{5,4},{6,7},{7,6},{8,9},{9,8},{10,11... | collective-permute-start | bytes 50331656 | tf_op jit(solution)/shard_map/ppermute | solution.py:593
  305.3 22.0 %copy-start.6 = (bf16[1280,1536]{1,0:T(8,128)(2,1)S(1)}, bf16[1280,1536]{1,0:T(8,128)(2,1)}, u32[]{:S(2)}) copy-start(bf16[1280,1536]{1,0:T(8,128)(2,1)} %shard_map.220) | copy-start | bytes 11796484
  327.3 14.0 %copy-start.14 = (bf16[1280,2048]{1,0:T(8,128)(2,1)S(1)}, bf16[1280,2048]{1,0:T(8,128)(2,1)}, u32[]{:S(2)}) copy-start(bf16[1280,2048]{1,0:T(8,128)(2,1)} %copy-done.13) | copy-start | bytes 15728644
  340.8 29.7 %collective-permute-start = (f32[1536,2048]{1,0:T(8,128)}, f32[1536,2048]{1,0:T(8,128)}, u32[]{:S(2)}, u32[]{:S(2)}) collective-permute-start(f32[1536,2048]{1,0:T(8,128)} %fusion.30), channel_id=1, source_target_pairs={{0,1},{1,0},{2,3},{3,2},{4,5},{5,4},{6,7},{7,6},{8,9},{9,8},{10,11... | collective-permute-start | bytes 37748744 | tf_op jit(solution)/shard_map/ppermute | solution.py:593
  343.0 24.3 %collective-permute-start.3 = (f32[2048,256]{1,0:T(8,128)S(1)}, f32[2048,256]{1,0:T(8,128)}, u32[]{:S(2)}, u32[]{:S(2)}) collective-permute-start(f32[2048,256]{1,0:T(8,128)S(1)} %fusion.35), channel_id=1, source_target_pairs={{0,1},{1,0},{2,3},{3,2},{4,5},{5,4},{6,7},{7,6},{8,9},{9,8},{10,11... | collective-permute-start | bytes 6291464 | tf_op jit(solution)/shard_map/ppermute | solution.py:593
  343.3 22.8 %collective-permute-start.1 = (f32[4352]{0:T(1024)S(1)}, f32[4352]{0:T(1024)S(1)}, u32[]{:S(2)}, u32[]{:S(2)}) collective-permute-start(f32[4352]{0:T(1024)S(1)} %pad_maximum_fusion), channel_id=1, source_target_pairs={{0,1},{1,0},{2,3},{3,2},{4,5},{5,4},{6,7},{7,6},{8,9},{9,8},{10,11... | collective-permute-start | bytes 52232 | tf_op jit(solution)/shard_map/ppermute | solution.py:593
Sparse Core Ops, SparseCore 0:
  32.0 30.9 all-gather.8
  65.4 87.9 all-gather.4
  202.0 159.0 all-gather.6

commit v3 on v2

--- a/solution.py
+++ b/solution.py
@@ -14,33 +14,57 @@
 TEMP_TEACHER = 0.04
 
 
-def gelu_slope(pre):
-    cdf = 0.5 * (1.0 + lax.erf(pre * 0.7071067811865476))
-    return cdf + pre * jnp.exp(-0.5 * pre * pre) * 0.3989422804014327
-
-
-def mlp_forward(feats, w_in, b_in, w_mid, b_mid, w_out, b_out):
-    pre_one = jnp.dot(feats, w_in, preferred_element_type=jnp.float32) + b_in.astype(jnp.float32)
-    hid_one = jax.nn.gelu(pre_one, approximate=False).astype(jnp.bfloat16)
-    pre_two = jnp.dot(hid_one, w_mid, preferred_element_type=jnp.float32) + b_mid.astype(jnp.float32)
-    hid_two = jax.nn.gelu(pre_two, approximate=False).astype(jnp.bfloat16)
+def layer_kernel(rows, feats_ref, w_ref, bias_ref, hid_ref, slope_ref, *narrow):
+    if narrow:
+        @pl.when(pl.program_id(0) == 0)
+        def _():
+            narrow[0][...] = feats_ref[...].astype(jnp.bfloat16)
+        feats_ref = narrow[0]
+
+    def one(step, carry):
+        at = pl.ds(pl.multiple_of(step * rows, rows), rows)
+        pre = jnp.dot(feats_ref[at, :], w_ref[...], preferred_element_type=jnp.float32) + bias_ref[...]
+        cdf = 0.5 * (1.0 + lax.erf(pre * 0.7071067811865476))
+        hid_ref[at, :] = (pre * cdf).astype(hid_ref.dtype)
+        slope_ref[at, :] = cdf + pre * jnp.exp(-0.5 * pre * pre) * 0.3989422804014327
+        return carry
+
+    lax.fori_loop(0, feats_ref.shape[0] // rows, one, 0)
+
+
+def mlp_layer(feats, w, biases, offset):
+    count, fan_in = feats.shape
+    width = w.shape[1]
+    block = 512
+    whole = pl.BlockSpec((count, fan_in), lambda k: (0, 0))
+    out = pl.BlockSpec((count, block), lambda k: (0, k))
+    narrow = feats.dtype != jnp.bfloat16
+    shapes = [jax.ShapeDtypeStruct((count, width), jnp.bfloat16), jax.ShapeDtypeStruct((count, width), jnp.float32)]
+    return pl.pallas_call(
+        functools.partial(layer_kernel, count // 4), grid=(width // block,),
+        out_shape=tuple(shapes + [jax.ShapeDtypeStruct((count, fan_in), jnp.bfloat16)] * narrow),
+        in_specs=[whole, pl.BlockSpec((fan_in, block), lambda k: (0, k)),
+                  pl.BlockSpec((1, block), lambda k: (0, offset // block + k))],
+        out_specs=tuple([out, out] + [whole] * narrow),
+        compiler_params=pltpu.CompilerParams(dimension_semantics=('arbitrary',), vmem_limit_bytes=56 << 20),
+        cost_estimate=pl.CostEstimate(flops=2 * count * fan_in * width, bytes_accessed=30 << 20,
+                                      transcendentals=2 * count * width))(feats, w, biases)
+
+
+def mlp_backward(g_emb, feats, saved, w_mid, w_out, b_out):
+    hid_one, slope_one, hid_two, slope_two = saved
     proj = jnp.dot(hid_two, w_out, preferred_element_type=jnp.float32) + b_out.astype(jnp.float32)
     inv_norm = lax.rsqrt(jnp.sum(proj * proj, axis=-1, keepdims=True))
     unit = proj * inv_norm
-    return unit.astype(jnp.bfloat16), (pre_one, hid_one, pre_two, hid_two, unit, inv_norm)
-
-
-def mlp_backward(g_emb, feats, saved, w_mid, w_out):
-    pre_one, hid_one, pre_two, hid_two, unit, inv_norm = saved
     g_proj = (g_emb - unit * jnp.sum(unit * g_emb, axis=-1, keepdims=True)) * inv_norm
     g_proj_lo = g_proj.astype(jnp.bfloat16)
     g_w_out = jnp.einsum('nh,nb->hb', hid_two, g_proj_lo, preferred_element_type=jnp.float32)
     g_hid_two = jnp.einsum('nb,hb->nh', g_proj_lo, w_out, preferred_element_type=jnp.float32)
-    g_pre_two = g_hid_two.astype(jnp.bfloat16).astype(jnp.float32) * gelu_slope(pre_two)
+    g_pre_two = g_hid_two.astype(jnp.bfloat16).astype(jnp.float32) * slope_two
     g_pre_two_lo = g_pre_two.astype(jnp.bfloat16)
     g_w_mid = jnp.einsum('ng,nh->gh', hid_one, g_pre_two_lo, preferred_element_type=jnp.float32)
     g_hid_one = jnp.einsum('nh,gh->ng', g_pre_two_lo, w_mid, preferred_element_type=jnp.float32)
-    g_pre_one = g_hid_one.astype(jnp.bfloat16).astype(jnp.float32) * gelu_slope(pre_one)
+    g_pre_one = g_hid_one.astype(jnp.bfloat16).astype(jnp.float32) * slope_one
     g_w_in = jnp.einsum('nf,nh->fh', feats, g_pre_one.astype(jnp.bfloat16), preferred_element_type=jnp.float32)
     return (g_w_in, jnp.sum(g_pre_one, axis=0), g_w_mid, jnp.sum(g_pre_two, axis=0), g_w_out, jnp.sum(g_proj, axis=0))
 
@@ -58,24 +82,6 @@
 
 def gather_rows(vals, axis_name):
     return lax.all_gather(vals.astype(jnp.float32), axis_name, axis=0, tiled=True)
-
-
-def round_kernel(wide_ref, out_ref):
-    out_ref[...] = wide_ref[...].astype(out_ref.dtype)
-
-
-def round_rows(wide):
-    rows, width = wide.shape
-    block = pl.BlockSpec((rows // 4, width), lambda i: (i, 0))
-    return pl.pallas_call(
-        round_kernel, out_shape=jax.ShapeDtypeStruct((rows, width), jnp.bfloat16), grid=(4,),
-        in_specs=[block], out_specs=block,
-        cost_estimate=pl.CostEstimate(flops=rows * width, bytes_accessed=6 * rows * width, transcendentals=0))(wide)
-
-
-def view_major(rows, n_img, views):
-    width = rows.shape[1]
-    return rows.reshape(n_img, views, width).transpose(1, 0, 2).reshape(n_img * views, width)
 
 
 LANES = 128
@@ -148,8 +154,8 @@
     return total
 
 
-def head_kernel(chunk, tx_ref, sx_ref, bias_ref, *refs):
-    weights, (out_ref,), bufs, (hid_one, hid_two, sems) = refs[:6], refs[6:7], refs[7:13], refs[13:]
+def head_kernel(chunk, offsets, tx_ref, sx_ref, bias_ref, *refs):
+    weights, (out_ref,), bufs, (hid_one, hid_two, proj_ref, sems) = refs[:6], refs[6:7], refs[7:13], refs[13:]
     t_rows = tx_ref.shape[0]
     order = (0, 3, 1, 4, 2, 5)
     slot = {}
@@ -162,14 +168,15 @@
             pltpu.make_async_copy(weights[which].at[:, cols], bufs[which].at[:, cols], sems.at[used]).start()
             used += 1
 
-    def layer(which, feats, bias_row, store):
+    def layer(which, feats, store):
         buf = bufs[which]
         span = min(chunk, buf.shape[1])
 
         def one(step, carry):
             cols = pl.ds(pl.multiple_of(step * span, span), span)
             pltpu.make_async_copy(weights[which].at[:, cols], buf.at[:, cols], sems.at[slot[which] + step]).wait()
-            store(cols, jnp.dot(feats[...], buf[:, cols], preferred_element_type=jnp.float32) + bias_ref[bias_row, cols])
+            bias_at = pl.ds(pl.multiple_of(offsets[which] + step * span, LANES), span)
+            store(cols, jnp.dot(feats[...], buf[:, cols], preferred_element_type=jnp.float32) + bias_ref[:, bias_at])
             return carry
 
         lax.fori_loop(0, buf.shape[1] // span, one, 0)
@@ -181,32 +188,37 @@
 
     def project(rows):
         def store(cols, proj):
-            out_ref[rows, cols] = proj
+            for lane in range(proj_ref.shape[0]):
+                proj_ref[lane, rows, :] = proj[:, lane * LANES:(lane + 1) * LANES]
         return store
 
     ours, theirs = pl.ds(t_rows, sx_ref.shape[0]), pl.ds(0, t_rows)
-    layer(0, tx_ref, slice(0, 1), hidden(hid_one, theirs))
-    layer(3, sx_ref, slice(3, 4), hidden(hid_one, ours))
-    layer(1, hid_one.at[theirs], slice(1, 2), hidden(hid_two, theirs))
-    layer(4, hid_one.at[ours], slice(4, 5), hidden(hid_two, ours))
-    layer(2, hid_two.at[theirs], slice(2, 3), project(theirs))
-    layer(5, hid_two.at[ours], slice(5, 6), project(ours))
-
-
-def head_pass(own_tx, own_x, teacher, student):
+    layer(0, tx_ref, hidden(hid_one, theirs))
+    layer(3, sx_ref, hidden(hid_one, ours))
+    layer(1, hid_one.at[theirs], hidden(hid_two, theirs))
+    layer(4, hid_one.at[ours], hidden(hid_two, ours))
+    layer(2, hid_two.at[theirs], project(theirs))
+    layer(5, hid_two.at[ours], project(ours))
+    for start, views, count in ((0, GLOBAL_CROPS, t_rows), (t_rows, ALL_CROPS, sx_ref.shape[0])):
+        n_img = count // views
+        for view in range(views):
+            for lane in range(proj_ref.shape[0]):
+                at = pl.ds(lane * LANES, LANES)
+                rows = pl.ds(start + view, n_img, stride=views)
+                out_ref[pl.ds(start + view * n_img, n_img), at] = proj_ref[lane, rows, :]
+
+
+def head_pass(own_tx, own_x, biases, offsets, teacher, student):
     hidden = student[0].shape[1]
-    lines = [jnp.pad(b.astype(jnp.float32), (0, hidden - b.shape[0])) for b in
-             (teacher[1], teacher[3], teacher[5], student[1], student[3], student[5])]
-    biases = jnp.stack(lines + lines[:2])
-    weights = (teacher[0], teacher[2], teacher[4], student[0], student[2], student[4])
+    weights = teacher + student
     rows = own_tx.shape[0] + own_x.shape[0]
     vmem, hbm = pl.BlockSpec(memory_space=pltpu.VMEM), pl.BlockSpec(memory_space=pl.ANY)
     return pl.pallas_call(
-        functools.partial(head_kernel, 512),
-        out_shape=jax.ShapeDtypeStruct((rows, student[4].shape[1]), jnp.float32),
+        functools.partial(head_kernel, 512, offsets),
+        out_shape=jax.ShapeDtypeStruct((rows, student[2].shape[1]), jnp.float32),
         in_specs=[vmem] * 3 + [hbm] * 6, out_specs=vmem,
         scratch_shapes=[pltpu.VMEM(w.shape, w.dtype) for w in weights]
-        + [pltpu.VMEM((rows, hidden), jnp.bfloat16)] * 2 + [pltpu.SemaphoreType.DMA((24,))],
+        + [pltpu.VMEM((rows, hidden), jnp.bfloat16)] * 2 + [pltpu.VMEM((student[2].shape[1] // LANES, rows, LANES), jnp.float32)] + [pltpu.SemaphoreType.DMA((24,))],
         compiler_params=pltpu.CompilerParams(vmem_limit_bytes=56 << 20),
         cost_estimate=pl.CostEstimate(flops=10 ** 10, bytes_accessed=34 << 20, transcendentals=rows * hidden * 2),
     )(own_tx, own_x, biases, *weights)
@@ -371,10 +383,45 @@
     return jnp.where(is_global, float(GLOBAL_CROPS - 1), float(GLOBAL_CROPS))
 
 
-def emb_kernel(sizes, n_img, factor, part_ref, s_ref, exp_u_ref, hi_u_ref, lo_u_ref, out_ref, sum_ref, weight_ref,
-               line_ref, line_recv, wide_ref, g_ref, near_recv, acc_ref, piece_recv, piece_ref, gathered,
-               line_send_sem, line_recv_sem, near_send_sem, near_recv_sem,
-               piece_send_sem, piece_recv_sem, all_send_sem, all_recv_sem):
+def line_kernel(sizes, n_img, part_ref, s_ref, hi_u_ref, lo_u_ref, sum_ref, weight_ref,
+                line_ref, line_recv, line_send_sem, line_recv_sem):
+    n_dev = 1
+    for size in sizes:
+        n_dev *= size
+    shards = n_dev // sizes[0]
+    n_student, depth = s_ref.shape
+    per_dev = n_student // shards
+    groups = n_student // LANES
+    greet_all(sizes, n_dev)
+    line_ref[...] = jnp.zeros_like(line_ref)
+    for group in range(groups):
+        rows = pl.ds(group * LANES, LANES)
+        line_ref[group:group + 1, :] = to_lanes(jnp.sum(part_ref[rows, :], axis=1, keepdims=True))
+
+    def view_sum(shard, hits):
+        base = pl.multiple_of(shard * per_dev, n_img)
+        views = [s_ref[pl.ds(base + view * n_img, n_img), :].astype(jnp.float32) for view in range(ALL_CROPS)]
+        total = views[0]
+        for view in views[1:]:
+            total = total + view
+        for crop in range(GLOBAL_CROPS):
+            rows = pl.ds(pl.multiple_of((shard * GLOBAL_CROPS + crop) * n_img, n_img), n_img)
+            hits = hits + (total - views[crop]) * (hi_u_ref[rows, :] + lo_u_ref[rows, :])
+        return hits
+
+    hits = lax.fori_loop(0, shards, view_sum, jnp.zeros((n_img, depth), jnp.float32))
+    hits = jnp.sum(jnp.sum(hits, axis=1, keepdims=True), axis=0, keepdims=True)
+    line_ref[groups:groups + 1, :] = jnp.broadcast_to(hits, (1, LANES))
+    await_all(n_dev)
+    sums = exchange(line_ref, line_recv, line_send_sem, line_recv_sem, sizes, n_dev)
+    sum_ref[...] = sums
+    lines = sums.shape[0]
+    weight_ref[...] = crop_weights(lines, per_dev, n_img) / sums
+
+
+def emb_kernel(sizes, n_img, factor, weight_ref, exp_u_ref, hi_u_ref, out_ref,
+               wide_ref, g_ref, near_recv, acc_ref, piece_recv, piece_ref, gathered, full_ref,
+               near_send_sem, near_recv_sem, piece_send_sem, piece_recv_sem, all_send_sem, all_recv_sem):
     n_dev = 1
     for size in sizes:
         n_dev *= size
@@ -388,31 +435,7 @@
     core = lax.rem(me, 2)
     chip = me // 2
     greet_all(sizes, n_dev)
-    line_ref[...] = jnp.zeros_like(line_ref)
-    for group in range(groups):
-        rows = pl.ds(group * LANES, LANES)
-        line_ref[group:group + 1, :] = to_lanes(jnp.sum(part_ref[rows, :], axis=1, keepdims=True))
-
-    def view_sum(shard, hits):
-        base = pl.multiple_of(shard * per_dev, n_img)
-        views = [s_ref[pl.ds(base + view * n_img, n_img), :].astype(jnp.float32) for view in range(ALL_CROPS)]
-        total = views[0]
-        for view in views[1:]:
-            total = total + view
-        for crop in range(GLOBAL_CROPS):
-            rows = pl.ds(pl.multiple_of((shard * GLOBAL_CROPS + crop) * n_img, n_img), n_img)
-            hits = hits + (total - views[crop]) * (hi_u_ref[rows, :] + lo_u_ref[rows, :])
-        return hits
-
-    hits = lax.fori_loop(0, shards, view_sum, jnp.zeros((n_img, depth), jnp.float32))
-    hits = jnp.sum(jnp.sum(hits, axis=1, keepdims=True), axis=0, keepdims=True)
-    line_ref[groups:groups + 1, :] = jnp.broadcast_to(hits, (1, LANES))
-    await_all(n_dev)
-    sums = exchange(line_ref, line_recv, line_send_sem, line_recv_sem, sizes, n_dev)
-    sum_ref[...] = sums
-    lines = sums.shape[0]
-    weight = crop_weights(lines, per_dev, n_img) / sums
-    weight_ref[...] = weight
+    weight = weight_ref[...]
     for group in range(groups):
         rows = pl.ds(group * LANES, LANES)
         wide_ref[rows, :] = jnp.broadcast_to(to_rows(weight[group:group + 1]), (LANES, LANES))
@@ -433,6 +456,7 @@
         return carry
 
     lax.fori_loop(0, shards, combine, 0)
+    await_all(n_dev)
     near = pltpu.make_async_remote_copy(
         src_ref=g_ref.at[1 - core], dst_ref=near_recv, send_sem=near_send_sem, recv_sem=near_recv_sem,
         device_id=place_of(chip * 2 + (1 - core), sizes), device_id_type=mesh_type)
@@ -462,16 +486,38 @@
             device_id=place_of(peer * 2 + core, sizes), device_id_type=mesh_type)
         copy.start()
         copies.append(copy)
-    out_ref[pl.ds(pl.multiple_of(chip * piece, n_img), piece), :] = total
+    full_ref[pl.ds(pl.multiple_of(chip * piece, n_img), piece), :] = total
     for step in range(1, chips):
         copies[step - 1].wait()
         owner = lax.rem(chip + chips - step, chips)
-        out_ref[pl.ds(pl.multiple_of(owner * piece, n_img), piece), :] = gathered[step]
-
-
-def emb_grads(part, s_all, exp_u, hi_u, lo_u, sizes, n_img, factor):
+        full_ref[pl.ds(pl.multiple_of(owner * piece, n_img), piece), :] = gathered[step]
+    for base in range(0, full_ref.shape[0], per_dev):
+        for view in range(ALL_CROPS):
+            for lane in range(depth // LANES):
+                at = pl.ds(lane * LANES, LANES)
+                rows = pl.ds(base + view, n_img, stride=ALL_CROPS)
+                out_ref[lane, rows, :] = full_ref[pl.ds(base + view * n_img, n_img), at]
+
+
+def crop_lines(part, s_all, hi_u, lo_u, sizes, n_img):
+    lines = (part.shape[0] // LANES // 8 + 1) * 8
+    n_dev = 1
+    for size in sizes:
+        n_dev *= size
+    vmem = pl.BlockSpec(memory_space=pltpu.VMEM)
+    line = jax.ShapeDtypeStruct((lines, LANES), jnp.float32)
+    return pl.pallas_call(
+        functools.partial(line_kernel, sizes, n_img), out_shape=(line, line), in_specs=[vmem] * 4, out_specs=(vmem,) * 2,
+        scratch_shapes=[
+            pltpu.VMEM((lines, LANES), jnp.float32), pltpu.VMEM((n_dev, lines, LANES), jnp.float32),
+            pltpu.SemaphoreType.DMA((n_dev,)), pltpu.SemaphoreType.DMA((n_dev,))],
+        compiler_params=pltpu.CompilerParams(collective_id=1, has_side_effects=True, vmem_limit_bytes=24 << 20),
+        cost_estimate=pl.CostEstimate(flops=5 * 10 ** 9, bytes_accessed=4 << 20, transcendentals=0),
+    )(part, s_all, hi_u, lo_u)
+
+
+def emb_grads(weight, exp_u, hi_u, sizes, n_img, factor):
     n_student, depth = exp_u.shape
-    lines = (n_student // LANES // 8 + 1) * 8
     n_dev = 1
     for size in sizes:
         n_dev *= size
@@ -481,18 +527,16 @@
     dma = pltpu.SemaphoreType.DMA
     return pl.pallas_call(
         functools.partial(emb_kernel, sizes, n_img, factor),
-        out_shape=(jax.ShapeDtypeStruct((half, depth), wide), jax.ShapeDtypeStruct((lines, LANES), wide),
-                   jax.ShapeDtypeStruct((lines, LANES), wide)),
-        in_specs=[vmem] * 5, out_specs=(vmem,) * 3,
+        out_shape=jax.ShapeDtypeStruct((depth // LANES, half, LANES), wide), in_specs=[vmem] * 3, out_specs=vmem,
         scratch_shapes=[
-            pltpu.VMEM((lines, LANES), wide), pltpu.VMEM((n_dev, lines, LANES), wide),
             pltpu.VMEM((n_student, LANES), wide), pltpu.VMEM((2, half, depth), wide), pltpu.VMEM((half, depth), wide),
             pltpu.VMEM((half, depth), wide), pltpu.VMEM((chips, half // chips, depth), wide),
             pltpu.VMEM((half // chips, depth), wide), pltpu.VMEM((chips, half // chips, depth), wide),
-            dma((n_dev,)), dma((n_dev,)), dma, dma, dma((chips,)), dma((chips,)), dma((chips,)), dma((chips,))],
-        compiler_params=pltpu.CompilerParams(collective_id=1, has_side_effects=True, vmem_limit_bytes=40 << 20),
+            pltpu.VMEM((half, depth), wide),
+            dma, dma, dma((chips,)), dma((chips,)), dma((chips,)), dma((chips,))],
+        compiler_params=pltpu.CompilerParams(collective_id=2, has_side_effects=True, vmem_limit_bytes=32 << 20),
         cost_estimate=pl.CostEstimate(flops=20 * 10 ** 9, bytes_accessed=8 << 20, transcendentals=0),
-    )(part, s_all, exp_u, hi_u, lo_u)
+    )(weight, exp_u, hi_u)
 
 
 def grad_kernel(factor, n_img, base_ref, weight_ref, s_ref, exp_ref, hi_ref, v_ref, out_ref, soft_ref, pair_ref):
@@ -563,23 +607,29 @@
         data_idx = (lax.axis_index('y') * 2 + lax.axis_index('x')) * 2 + core
         base = data_idx.reshape(1)
 
-        own_x = view_major(student_x, n_img, ALL_CROPS)
-        own_tx = view_major(teacher_x, n_img, GLOBAL_CROPS)
-        both = head_pass(own_tx, own_x, (ema_w_in, ema_b_in, ema_w_mid, ema_b_mid, ema_w_out, ema_b_out),
-                         (w_in, b_in, w_mid, b_mid, w_out, b_out))
+        rows_b = (ema_b_in, ema_b_mid, b_in, b_mid, ema_b_out, b_out)
+        biases = jnp.concatenate(rows_b).astype(jnp.float32)[None]
+        starts = []
+        for row in rows_b:
+            starts.append(starts[-1] + width if starts else 0)
+            width = row.shape[0]
+        offsets = (starts[0], starts[1], starts[4], starts[2], starts[3], starts[5])
+        both = head_pass(teacher_x, student_x, biases, offsets, (ema_w_in, ema_w_mid, ema_w_out), (w_in, w_mid, w_out))
         both = gather_rows(both[None], data)
-        both, own_x = lax.optimization_barrier((both, own_x))
+        both, own_x = lax.optimization_barrier((both, student_x))
         half_wide = gather_rows(own_x, ('y', 'x'))
 
         q_hi, q_lo, q_row, s_all = sinkhorn(both, ema_protos, sizes, n_proto, n_rows, part)
         exp_lo, row_part, exp_u, hi_u, lo_u = soft_pass(base, s_all, protos, q_hi, q_lo)
         scale = 1.0 / (n_img * dp_size * GLOBAL_CROPS * (ALL_CROPS - 1))
         factor = scale / TEMP_STUDENT
-        g_emb, sums, weight = emb_grads(row_part, s_all, exp_u, hi_u, lo_u, sizes, n_img, factor)
+        sums, weight = crop_lines(row_part, s_all, hi_u, lo_u, sizes, n_img)
         g_own = grad_pass(base, weight, s_all, exp_lo, q_hi, protos, factor, n_img)
         g_own, half_wide = lax.optimization_barrier((g_own, half_wide))
         g_protos = lax.all_gather(g_own, data, axis=1, tiled=True)
-        half_x = round_rows(half_wide)
+        weight, _ = lax.optimization_barrier((weight, g_own))
+        g_emb = emb_grads(weight, exp_u, hi_u, sizes, n_img, factor)
+        g_emb = jnp.concatenate([g_emb[lane] for lane in range(g_emb.shape[0])], axis=1)
 
         per_view = q_row[:n_rows // LANES].reshape(dp_size, GLOBAL_CROPS, n_img)
         pad = jnp.pad(per_view, ((0, 0), (0, ALL_CROPS - GLOBAL_CROPS), (0, 0)))
@@ -588,8 +638,9 @@
         hits = sums[n_student // LANES, 0]
         loss = (jnp.sum(t_row * jnp.log(row_line)) - hits / TEMP_STUDENT) * scale
 
-        _, saved = mlp_forward(half_x, w_in, b_in, w_mid, b_mid, w_out, b_out)
-        grads = mlp_backward(g_emb, half_x, saved, w_mid, w_out)
+        hid_one, slope_one, half_x = mlp_layer(half_wide, w_in, biases, offsets[3])
+        hid_two, slope_two = mlp_layer(hid_one, w_mid, biases, offsets[4])
+        grads = mlp_backward(g_emb, half_x, (hid_one, slope_one, hid_two, slope_two), w_mid, w_out, b_out)
         swap = lambda g: g + lax.ppermute(g, 'core', [(0, 1), (1, 0)])
         biases = swap(jnp.concatenate([grads[1], grads[3], grads[5]]))
         b_grads = jnp.split(biases, [b_in.shape[0], b_in.shape[0] + b_mid.shape[0]])

time: 442 us -> 404 us (0.914); the launches traced: 433 us -> 403 us
  matrix products: 133 us -> 57.6 us
  Pallas kernels: 148 us -> 204 us
    dot_general x3 -> x1, matrix products: 71.7 us -> 4.26 us  [mlp_backward(): jnp.dot(hid_two, w_out, preferred_element_type=jnp.float32)]
    pallas_call x2 -> x4, Pallas kernels: 20.8 us -> 68.2 us  [the longest x2 43.8 us: mlp_layer(): pl.pallas_call(functools.partial(layer_kernel, count // 4), grid=(width /...]
    pallas_call x1, Pallas kernels: 52.8 us -> 60.8 us  [emb_grads(): pl.pallas_call(functools.partial(emb_kernel, sizes, n_img, factor), out_s...]
    dot_general x1, matrix products: 22 us -> 16.9 us  [mlp_backward(): jnp.einsum('nh,gh->ng', g_pre_two_lo, w_mid, preferred_element_type=jnp.f...]
    dot_general x1, matrix products: 6.19 us -> 1.57 us  [mlp_backward(): jnp.einsum('nb,hb->nh', g_proj_lo, w_out, preferred_element_type=jnp.floa...]
    unnamed x35 -> x30, local copies, waits for them, and re-layouts: 32.2 us -> 33.9 us
  transfers between devices with their start and end apart: 7 -> 7, of which waited for: 2 -> 2; matrix products, arithmetic and copies ran while one was open for 40% -> 24% of each run, Pallas kernels for 31% -> 47%
where the time goes in v3:
time: 404 us; the launch traced here: 403 us
  Pallas kernels  204 us (50%)
  matrix products  57.6 us (14%)
  waiting for transfers between devices  48.6 us (12%)
  other arithmetic  38.8 us (10%)
  local copies, waits for them, and re-layouts  36.5 us (9%)
  between operations  16.4 us (4%)
    pallas_call x1, Pallas kernels, emb_grads(): pl.pallas_call(functools.partial(emb_kernel, sizes, n_img, factor), out_s...  60.8 us
    pallas_call x2, Pallas kernels, mlp_layer(): pl.pallas_call(functools.partial(layer_kernel, count // 4), grid=(width /...  43.8 us
    add x4, other arithmetic, local_step(): swap = lambda g: g + lax.ppermute(g, 'core', [(0, 1), (1, 0)])  35.1 us
    pallas_call x1, Pallas kernels, sinkhorn(): pl.pallas_call(functools.partial(sink_kernel, sizes, n_proto, 512), out_s...  34.3 us
    unnamed x30, local copies, waits for them, and re-layouts  33.9 us
    all_gather x2, waiting for transfers between devices, gather_rows(): lax.all_gather(vals.astype(jnp.float32), axis_name, axis=0, tiled=True)  31.1 us
    pallas_call x1, Pallas kernels, soft_pass(): pl.pallas_call(functools.partial(soft_kernel, 640), grid_spec=pltpu.Prefe...  26.7 us
    ppermute x4, waiting for transfers between devices, local_step(): swap = lambda g: g + lax.ppermute(g, 'core', [(0, 1), (1, 0)])  17.4 us
  transfers between devices with their start and end apart: 7, of which 2 were waited for; matrix products, arithmetic and copies ran while one was open for 24% of the time, Pallas kernels for 47%

profile of v3, /device:TPU:0, one launch (start us, length us, event | category | flops | bytes accessed | tf_op | source)
XLA Modules:
  0.0 403.2 jit_solution(12864094806139663916)
XLA Ops:
  12.0 15.3 %shard_map.215 = f32[384,256]{1,0:T(8,128)} custom-call(bf16[64,1536]{1,0:T(8,128)(2,1)} %tx_ref.1, bf16[320,1536]{1,0:T(8,128)(2,1)} %sx_ref.1, f32[1,8704]{1,0:T(1,128)} %convert_element_type.39.bias_ref, bf16[1536,2048]{1,0:T(8,128)(2,1)} %refs_0_.1, bf16[2048,2048]{1,0:T(8,128)(2,1)} %refs_1_.1, bf16[2048,256]{1,0:T(8,128)(2,1)} %refs_2_.1, ...), custom_call_target="tpu_custom_call" | custom-call | flops 10000000000 | bytes 35651584 | tf_op jit(solution)/shard_map/pallas_call | solution.py:216
  27.3 31.1 %all-gather.9.cloned.1.call-done = f32[3072,256]{1,0:T(8,128)} async-done(((f32[384,256]{1,0:T(8,128)}), f32[3072,256]{1,0:T(8,128)}) %all-gather.9.cloned.1.call-update) | async-done | bytes 3145744 | tf_op jit(solution)/shard_map/all_gather | solution.py:84
  60.2 1.9 copy-done.3
  62.1 34.3 %shard_map.216 = (bf16[512,4096]{1,0:T(8,128)(2,1)S(1)}, bf16[512,4096]{1,0:T(8,128)(2,1)S(1)}, f32[8,128]{1,0:T(8,128)S(1)}, bf16[2560,256]{1,0:T(8,128)(2,1)S(1)}) custom-call(f32[8,384,256]{2,1,0:T(8,128)S(1)} %bitcast.19, bf16[256,32768]{1,0:T(8,128)(2,1)} %ema_ref.1), custom_call_target="tpu_custom_call" | custom-call | flops 20000000000 | bytes 12582912 | tf_op jit(solution)/shard_map/pallas_call | solution.py:313
  96.4 2.0 copy-done.1
  98.4 2.0 copy-done.4
  100.4 26.7 %shard_map.217 = (bf16[2560,4096]{1,0:T(8,128)(2,1)}, f32[2560,128]{1,0:T(8,128)S(1)}, f32[2560,256]{1,0:T(8,128)}, f32[512,256]{1,0:T(8,128)S(1)}, f32[512,256]{1,0:T(8,128)S(1)}) custom-call(s32[1]{0:T(128)} %bitcast.1.base_ref, bf16[2560,256]{1,0:T(8,128)(2,1)S(1)} %get-tuple-element.31.s_ref, bf16[256,32768]{1,0:T(8,128)(2,1)} %v_ref.3, ...), custom_call_target="tpu_custom_call" | custom-call | flops 12999999488 | bytes 36700160 | tf_op jit(solution)/shard_map/pallas_call | solution.py:365
  127.1 9.1 %shard_map.218 = (f32[24,128]{1,0:T(8,128)S(1)}, f32[24,128]{1,0:T(8,128)S(1)}) custom-call(f32[2560,128]{1,0:T(8,128)S(1)} %get-tuple-element.34.part_ref, bf16[2560,256]{1,0:T(8,128)(2,1)S(1)} %get-tuple-element.31.s_ref, f32[512,256]{1,0:T(8,128)S(1)} %get-tuple-element.35.hi_u_ref, f32[512,256]{1,0:T(8,128)S(1)} %get-tuple-element.36.lo_u_ref), custom_call_target="tpu_custom_call" | custom-call | flops 5000000000 | bytes 4194304 | tf_op jit(solution)/shard_map/pallas_call | solution.py:509
  136.3 13.9 %shard_map.219 = f32[256,4096]{1,0:T(8,128)S(1)} custom-call(s32[1]{0:T(128)} %bitcast.1.base_ref, f32[24,128]{1,0:T(8,128)S(1)} %get-tuple-element.44.weight_ref, bf16[2560,256]{1,0:T(8,128)(2,1)S(1)} %get-tuple-element.31.s_ref, bf16[2560,4096]{1,0:T(8,128)(2,1)} %get-tuple-element.39.exp_ref, bf16[512,4096]{1,0:T(8,128)(2,1)S(1)} %copy-done.2, ...), custom_call_target="tpu_custom_call" | custom-call | flops 7000000000 | bytes 34603008 | tf_op jit(solution)/shard_map/pallas_call | solution.py:579
  150.2 2.0 copy-done
  152.2 21.7 %shard_map.220 = (bf16[1280,2048]{1,0:T(8,128)(2,1)}, f32[1280,2048]{1,0:T(8,128)}, bf16[1280,1536]{1,0:T(8,128)(2,1)}) custom-call(f32[1280,1536]{1,0:T(8,128)} %all-gather.5.cloned.1.call-done.feats_ref, bf16[1536,2048]{1,0:T(8,128)(2,1)} %w_ref.2, f32[1,8704]{1,0:T(1,128)} %convert_element_type.39.bias_ref), custom_call_target="tpu_custom_call" | custom-call | flops 8053063680 | bytes 31457280 | tf_op jit(solution)/shard_map/pallas_call | solution.py:43
  173.9 22.1 %shard_map.222 = (bf16[1280,2048]{1,0:T(8,128)(2,1)}, f32[1280,2048]{1,0:T(8,128)}) custom-call(bf16[1280,2048]{1,0:T(8,128)(2,1)} %get-tuple-element.46.feats_ref, bf16[2048,2048]{1,0:T(8,128)(2,1)} %w_ref.3, f32[1,8704]{1,0:T(1,128)} %convert_element_type.39.bias_ref), custom_call_target="tpu_custom_call" | custom-call | flops 10737418240 | bytes 31457280 | tf_op jit(solution)/shard_map/pallas_call | solution.py:43
  196.1 4.3 %multiply_reduce_fusion.1 = (f32[1280]{0:T(1024)S(1)}, f32[1280,256]{1,0:T(8,128)S(1)}) fusion(f32[256]{0:T(256)S(1)} %convert_element_type.41, bf16[1280,2048]{1,0:T(8,128)(2,1)} %get-tuple-element.47, bf16[2048,256]{1,0:T(8,128)(2,1)S(1)} %copy-done.6), kind=kOutput, calls=%fused_computation.13 | convolution fusion | flops 1343159040 | bytes 7608320 | tf_op jit(solution)/shard_map/dot_general | solution.py:56
  200.4 60.8 %shard_map.221 = f32[2,1280,128]{2,1,0:T(8,128)S(1)} custom-call(f32[24,128]{1,0:T(8,128)S(1)} %get-tuple-element.44.weight_ref, f32[2560,256]{1,0:T(8,128)S(1)} %copy-done.5, f32[512,256]{1,0:T(8,128)S(1)} %get-tuple-element.35.hi_u_ref), custom_call_target="tpu_custom_call" | custom-call | flops 20000000000 | bytes 8388608 | tf_op jit(solution)/shard_map/pallas_call | solution.py:528
  262.2 1.6 fusion.11
  263.8 16.5 %fusion.2 = f32[2048,2048]{1,0:T(8,128)} fusion(bf16[1280,2048]{1,0:T(8,128)(2,1)} %get-tuple-element.46.feats_ref, bf16[1280,2048]{1,0:T(8,128)(2,1)S(1)} %get-tuple-element.59), kind=kOutput, calls=%fused_computation.7 | convolution fusion | flops 10737418240 | bytes 27262976 | tf_op jit(solution)/shard_map/ng,nh->gh/dot_general | solution.py:65
  280.3 16.9 %fusion.12 = (f32[2048]{0:T(1024)S(1)}, bf16[1280,2048]{1,0:T(8,128)(2,1)}) fusion(f32[1280,2048]{1,0:T(8,128)} %get-tuple-element.49, bf16[2048,2048]{1,0:T(8,128)(2,1)} %w_ref.3, bf16[1280,2048]{1,0:T(8,128)(2,1)S(1)} %get-tuple-element.59), kind=kOutput, calls=%fused_computation.32 | convolution fusion | flops 10750523392 | bytes 29368320 | tf_op jit(solution)/shard_map/nh,gh->ng/dot_general | solution.py:66
  297.2 14.2 %fusion = f32[1536,2048]{1,0:T(8,128)} fusion(bf16[1280,1536]{1,0:T(8,128)(2,1)} %get-tuple-element.42, bf16[1280,2048]{1,0:T(8,128)(2,1)} %get-tuple-element.61), kind=kOutput, calls=%fused_computation.4 | convolution fusion | flops 8053063680 | bytes 21757952 | tf_op jit(solution)/shard_map/nf,nh->fh/dot_general | solution.py:68
  311.9 4.1 %fusion.5 = f32[2048,256]{1,0:T(8,128)S(1)} fusion(bf16[1280,2048]{1,0:T(8,128)(2,1)} %get-tuple-element.47, bf16[1280,256]{1,0:T(8,128)(2,1)S(1)} %get-tuple-element.51), kind=kOutput, calls=%fused_computation.16 | convolution fusion | flops 1342177280 | bytes 7995392 | tf_op jit(solution)/shard_map/nh,nb->hb/dot_general | solution.py:61
  319.3 17.4 %collective-permute-done.1 = f32[4352]{0:T(1024)S(1)} collective-permute-done((f32[4352]{0:T(1024)S(1)}, f32[4352]{0:T(1024)S(1)}, u32[]{:S(2)}, u32[]{:S(2)}) %collective-permute-start.1) | collective-permute-done | bytes 17440 | tf_op jit(solution)/shard_map/ppermute | solution.py:644
  337.9 3.2 add.35
  341.1 14.4 %add.32 = f32[1536,2048]{1,0:T(8,128)} add(f32[1536,2048]{1,0:T(8,128)} %fusion, f32[1536,2048]{1,0:T(8,128)} %collective-permute-done) | non-fusion elementwise | flops 3145728 | bytes 37748736 | tf_op jit(solution)/shard_map/add | solution.py:644
  355.5 17.5 %add.34 = f32[2048,2048]{1,0:T(8,128)} add(f32[2048,2048]{1,0:T(8,128)} %fusion.2, f32[2048,2048]{1,0:T(8,128)} %collective-permute-done.2) | non-fusion elementwise | flops 4194304 | bytes 50331648 | tf_op jit(solution)/shard_map/add | solution.py:644
  373.0 22.5 %copy.33 = f32[256,32768]{1,0:T(8,128)} copy(f32[256,32768]{1,0:T(8,128)} %all-gather.7.cloned.1.call-done) | data formatting | bytes 67108864
  (60 shorter events, 11.2 us)
Async XLA Ops:
  7.2 51.3 %all-gather.9.cloned.1.call-start = ((), (), s32[]{:S(2)}) async-start(), calls=%async_computation.2 | async-start | bytes 3538944 | tf_op jit(solution)/shard_map/all_gather | solution.py:84
  12.0 46.5 %copy-start.7 = (bf16[320,1536]{1,0:T(8,128)(2,1)S(1)}, bf16[320,1536]{1,0:T(8,128)(2,1)}, u32[]{:S(2)}) copy-start(bf16[320,1536]{1,0:T(8,128)(2,1)} %sx_ref.1) | copy-start | bytes 2949124
  27.3 124.9 %all-gather.5.cloned.1.call-start = ((), (), s32[]{:S(2)}) async-start(), calls=%async_computation | async-start | bytes 9830400 | tf_op jit(solution)/shard_map/all_gather | solution.py:84
  60.0 313.1 %all-gather.7.cloned.1.call-start = ((), (), s32[]{:S(2)}) async-start(), calls=%async_computation.1 | async-start | bytes 37748736 | tf_op jit(solution)/shard_map/all_gather | solution.py:629
  60.2 1.9 copy-start.3
  96.4 2.0 copy-start.1
  98.4 2.0 copy-start.4
  127.1 9.1 %copy-start.2 = (bf16[512,4096]{1,0:T(8,128)(2,1)S(1)}, bf16[512,4096]{1,0:T(8,128)(2,1)}, u32[]{:S(2)}) copy-start(bf16[512,4096]{1,0:T(8,128)(2,1)} %copy-done.1) | copy-start | bytes 12582916
  136.3 15.9 %copy-start.8 = (bf16[256]{0:T(256)(128)(2,1)S(1)}, bf16[256]{0:T(256)(128)(2,1)}, u32[]{:S(2)}) copy-start(bf16[256]{0:T(256)(128)(2,1)} %param.23) | copy-start | bytes 1540
  150.2 2.0 copy-start
  173.9 22.1 %copy-start.6 = (bf16[2048,256]{1,0:T(8,128)(2,1)S(1)}, bf16[2048,256]{1,0:T(8,128)(2,1)}, u32[]{:S(2)}) copy-start(bf16[2048,256]{1,0:T(8,128)(2,1)} %refs_5_.1) | copy-start | bytes 3145732
  196.0 4.3 %copy-start.5 = (f32[2560,256]{1,0:T(8,128)S(1)}, f32[2560,256]{1,0:T(8,128)}, u32[]{:S(2)}) copy-start(f32[2560,256]{1,0:T(8,128)} %get-tuple-element.45.exp_u_ref) | copy-start | bytes 7864324
  200.3 61.8 %slice-start = ((s8[10485760]{0:T(1024)(128)(4,1)}), s8[4194304]{0:T(1024)(128)(4,1)S(1)}, s32[]{:S(2)}) async-start(s8[10485760]{0:T(1024)(128)(4,1)} %bitcast.20), calls=%async_computation.3 | async-start | bytes 8388608
  200.4 61.8 %slice-start.1 = ((s8[10485760]{0:T(1024)(128)(4,1)}), s8[4194304]{0:T(1024)(128)(4,1)S(1)}, s32[]{:S(2)}) async-start(s8[10485760]{0:T(1024)(128)(4,1)} %bitcast.20), calls=%async_computation.4 | async-start | bytes 8388608
  200.4 61.8 %slice-start.2 = ((s8[10485760]{0:T(1024)(128)(4,1)}), s8[2097152]{0:T(1024)(128)(4,1)S(1)}, s32[]{:S(2)}) async-start(s8[10485760]{0:T(1024)(128)(4,1)} %bitcast.20), calls=%async_computation.5 | async-start | bytes 4194304
  280.3 75.3 %collective-permute-start.2 = (f32[2048,2048]{1,0:T(8,128)}, f32[2048,2048]{1,0:T(8,128)}, u32[]{:S(2)}, u32[]{:S(2)}) collective-permute-start(f32[2048,2048]{1,0:T(8,128)} %fusion.2), channel_id=1, source_target_pairs={{0,1},{1,0},{2,3},{3,2},{4,5},{5,4},{6,7},{7,6},{8,9},{9,8},{10,11... | collective-permute-start | bytes 50331656 | tf_op jit(solution)/shard_map/ppermute | solution.py:644
  311.4 29.7 %collective-permute-start = (f32[1536,2048]{1,0:T(8,128)}, f32[1536,2048]{1,0:T(8,128)}, u32[]{:S(2)}, u32[]{:S(2)}) collective-permute-start(f32[1536,2048]{1,0:T(8,128)} %fusion), channel_id=1, source_target_pairs={{0,1},{1,0},{2,3},{3,2},{4,5},{5,4},{6,7},{7,6},{8,9},{9,8},{10,11... | collective-permute-start | bytes 37748744 | tf_op jit(solution)/shard_map/ppermute | solution.py:644
  316.0 21.9 %collective-permute-start.3 = (f32[2048,256]{1,0:T(8,128)S(1)}, f32[2048,256]{1,0:T(8,128)}, u32[]{:S(2)}, u32[]{:S(2)}) collective-permute-start(f32[2048,256]{1,0:T(8,128)S(1)} %fusion.5), channel_id=1, source_target_pairs={{0,1},{1,0},{2,3},{3,2},{4,5},{5,4},{6,7},{7,6},{8,9},{9,8},{10,11... | collective-permute-start | bytes 6291464 | tf_op jit(solution)/shard_map/ppermute | solution.py:644
  316.3 20.4 %collective-permute-start.1 = (f32[4352]{0:T(1024)S(1)}, f32[4352]{0:T(1024)S(1)}, u32[]{:S(2)}, u32[]{:S(2)}) collective-permute-start(f32[4352]{0:T(1024)S(1)} %pad_maximum_fusion.1), channel_id=1, source_target_pairs={{0,1},{1,0},{2,3},{3,2},{4,5},{5,4},{6,7},{7,6},{8,9},{9,8},{10,11... | collective-permute-start | bytes 52232 | tf_op jit(solution)/shard_map/ppermute | solution.py:644
Sparse Core Ops, SparseCore 0:
  27.4 30.9 all-gather.8
  60.8 83.4 all-gather.4
  152.3 182.4 all-gather.6

commit v4 on v3

--- a/solution.py
+++ b/solution.py
@@ -419,9 +419,32 @@
     weight_ref[...] = crop_weights(lines, per_dev, n_img) / sums
 
 
-def emb_kernel(sizes, n_img, factor, weight_ref, exp_u_ref, hi_u_ref, out_ref,
+def turn_factors(n_img, weight_ref, s_ref, soft_ref, pair_ref):
+    n_student = s_ref.shape[0]
+    for group in range(n_student // LANES):
+        rows = pl.ds(group * LANES, LANES)
+        turned = s_ref[rows, :].astype(jnp.float32).T
+        soft_ref[:, rows] = (turned * weight_ref[group:group + 1, :]).astype(soft_ref.dtype)
+    per_dev = ALL_CROPS * n_img
+    pairs = []
+    for shard in range(n_student // per_dev):
+        views = [s_ref[pl.ds(shard * per_dev + view * n_img, n_img), :].astype(jnp.float32) for view in range(ALL_CROPS)]
+        total = views[0]
+        for view in views[1:]:
+            total = total + view
+        pairs += [total - views[crop] for crop in range(GLOBAL_CROPS)]
+    per_tile = LANES // n_img
+    for tile in range(len(pairs) // per_tile):
+        rows = jnp.concatenate(pairs[tile * per_tile:(tile + 1) * per_tile], axis=0)
+        pair_ref[:, pl.ds(tile * LANES, LANES)] = rows.T.astype(pair_ref.dtype)
+
+
+def emb_kernel(sizes, n_img, factor, block, weight_ref, exp_u_ref, hi_u_ref, s_ref, exp_hbm, hi_hbm, protos_hbm,
+               out_ref, own_ref,
                wide_ref, g_ref, near_recv, acc_ref, piece_recv, piece_ref, gathered, full_ref,
-               near_send_sem, near_recv_sem, piece_send_sem, piece_recv_sem, all_send_sem, all_recv_sem):
+               soft_ref, pair_ref, exp_ref, hi_ref, v_ref,
+               near_send_sem, near_recv_sem, piece_send_sem, piece_recv_sem, all_send_sem, all_recv_sem,
+               exp_sem, hi_sem, v_sem):
     n_dev = 1
     for size in sizes:
         n_dev *= size
@@ -435,6 +458,37 @@
     core = lax.rem(me, 2)
     chip = me // 2
     greet_all(sizes, n_dev)
+    width = own_ref.shape[1]
+    steps = width // block
+
+    def fetch(step):
+        cols = pl.ds(pl.multiple_of(step * block, block), block)
+        slot = lax.rem(step, 2)
+        return pltpu.make_async_copy(exp_hbm.at[:, cols], exp_ref.at[slot], exp_sem.at[slot])
+
+    first = pl.multiple_of(lax.rem(me, shards) * width, width)
+    get_v = pltpu.make_async_copy(protos_hbm.at[:, pl.ds(first, width)], v_ref, v_sem)
+    get_hi = pltpu.make_async_copy(hi_hbm, hi_ref, hi_sem)
+    get_v.start()
+    get_hi.start()
+    fetch(0).start()
+
+    def grad_block(step, carry):
+        cols = pl.ds(pl.multiple_of(step * block, block), block)
+
+        @pl.when(step + 1 < steps)
+        def _():
+            fetch(step + 1).start()
+
+        fetch(step).wait()
+        g_unit = jnp.dot(soft_ref[...], exp_ref[lax.rem(step, 2)], preferred_element_type=jnp.float32)
+        g_unit = (g_unit - jnp.dot(pair_ref[...], hi_ref[:, cols], preferred_element_type=jnp.float32)) * factor
+        proto_f = v_ref[:, cols].astype(jnp.float32)
+        inv_col = lax.rsqrt(jnp.sum(proto_f * proto_f, axis=0, keepdims=True))
+        unit = proto_f * inv_col
+        own_ref[:, cols] = (g_unit - unit * jnp.sum(unit * g_unit, axis=0, keepdims=True)) * inv_col
+        return carry
+
     weight = weight_ref[...]
     for group in range(groups):
         rows = pl.ds(group * LANES, LANES)
@@ -461,6 +515,9 @@
         src_ref=g_ref.at[1 - core], dst_ref=near_recv, send_sem=near_send_sem, recv_sem=near_recv_sem,
         device_id=place_of(chip * 2 + (1 - core), sizes), device_id_type=mesh_type)
     near.start()
+    turn_factors(n_img, weight_ref, s_ref, soft_ref, pair_ref)
+    get_v.wait()
+    get_hi.wait()
     near.wait()
     acc_ref[...] = g_ref[core] + near_recv[...]
     piece = acc_ref.shape[0] // chips
@@ -473,6 +530,7 @@
             device_id=place_of(peer * 2 + core, sizes), device_id_type=mesh_type)
         copy.start()
         copies.append(copy)
+    lax.fori_loop(0, steps // 2, grad_block, 0)
     total = acc_ref[pl.ds(pl.multiple_of(chip * piece, n_img), piece), :]
     for step in range(1, chips):
         copies[step - 1].wait()
@@ -487,6 +545,7 @@
         copy.start()
         copies.append(copy)
     full_ref[pl.ds(pl.multiple_of(chip * piece, n_img), piece), :] = total
+    lax.fori_loop(steps // 2, steps, grad_block, 0)
     for step in range(1, chips):
         copies[step - 1].wait()
         owner = lax.rem(chip + chips - step, chips)
@@ -516,77 +575,32 @@
     )(part, s_all, hi_u, lo_u)
 
 
-def emb_grads(weight, exp_u, hi_u, sizes, n_img, factor):
+def emb_grads(weight, exp_u, hi_u, s_all, exp_lo, hi, protos, sizes, n_img, factor):
     n_student, depth = exp_u.shape
+    n_rows, width = hi.shape
+    block = 512
     n_dev = 1
     for size in sizes:
         n_dev *= size
     half, chips = n_student // 2, n_dev // 2
-    vmem = pl.BlockSpec(memory_space=pltpu.VMEM)
-    wide = jnp.float32
+    vmem, hbm = pl.BlockSpec(memory_space=pltpu.VMEM), pl.BlockSpec(memory_space=pl.ANY)
+    wide, low = jnp.float32, jnp.bfloat16
     dma = pltpu.SemaphoreType.DMA
     return pl.pallas_call(
-        functools.partial(emb_kernel, sizes, n_img, factor),
-        out_shape=jax.ShapeDtypeStruct((depth // LANES, half, LANES), wide), in_specs=[vmem] * 3, out_specs=vmem,
+        functools.partial(emb_kernel, sizes, n_img, factor, block),
+        out_shape=(jax.ShapeDtypeStruct((depth // LANES, half, LANES), wide), jax.ShapeDtypeStruct((depth, width), wide)),
+        in_specs=[vmem] * 4 + [hbm] * 3, out_specs=(vmem,) * 2,
         scratch_shapes=[
             pltpu.VMEM((n_student, LANES), wide), pltpu.VMEM((2, half, depth), wide), pltpu.VMEM((half, depth), wide),
             pltpu.VMEM((half, depth), wide), pltpu.VMEM((chips, half // chips, depth), wide),
             pltpu.VMEM((half // chips, depth), wide), pltpu.VMEM((chips, half // chips, depth), wide),
             pltpu.VMEM((half, depth), wide),
-            dma, dma, dma((chips,)), dma((chips,)), dma((chips,)), dma((chips,))],
-        compiler_params=pltpu.CompilerParams(collective_id=2, has_side_effects=True, vmem_limit_bytes=32 << 20),
-        cost_estimate=pl.CostEstimate(flops=20 * 10 ** 9, bytes_accessed=8 << 20, transcendentals=0),
-    )(weight, exp_u, hi_u)
-
-
-def grad_kernel(factor, n_img, base_ref, weight_ref, s_ref, exp_ref, hi_ref, v_ref, out_ref, soft_ref, pair_ref):
-    @pl.when(pl.program_id(0) == 0)
-    def _():
-        n_student = s_ref.shape[0]
-        for group in range(n_student // LANES):
-            rows = pl.ds(group * LANES, LANES)
-            turned = s_ref[rows, :].astype(jnp.float32).T
-            soft_ref[:, rows] = (turned * weight_ref[group:group + 1, :]).astype(soft_ref.dtype)
-        per_dev = ALL_CROPS * n_img
-        pairs = []
-        for shard in range(n_student // per_dev):
-            views = [s_ref[pl.ds(shard * per_dev + view * n_img, n_img), :].astype(jnp.float32)
-                     for view in range(ALL_CROPS)]
-            total = views[0]
-            for view in views[1:]:
-                total = total + view
-            pairs += [total - views[crop] for crop in range(GLOBAL_CROPS)]
-        per_tile = LANES // n_img
-        for tile in range(len(pairs) // per_tile):
-            rows = jnp.concatenate(pairs[tile * per_tile:(tile + 1) * per_tile], axis=0)
-            pair_ref[:, pl.ds(tile * LANES, LANES)] = rows.T.astype(pair_ref.dtype)
-
-    g_unit = jnp.dot(soft_ref[...], exp_ref[...], preferred_element_type=jnp.float32)
-    g_unit = (g_unit - jnp.dot(pair_ref[...], hi_ref[...], preferred_element_type=jnp.float32)) * factor
-    proto_f = v_ref[...].astype(jnp.float32)
-    inv_col = lax.rsqrt(jnp.sum(proto_f * proto_f, axis=0, keepdims=True))
-    unit = proto_f * inv_col
-    out_ref[...] = (g_unit - unit * jnp.sum(unit * g_unit, axis=0, keepdims=True)) * inv_col
-
-
-def grad_pass(base, weight, s_all, exp_lo, hi, protos, factor, n_img):
-    n_student, depth = s_all.shape
-    n_rows, width = hi.shape
-    block = 512
-    whole = lambda shape: pl.BlockSpec(shape, lambda k, base_ref: (0, 0))
-    cols = lambda height: pl.BlockSpec((height, block), lambda k, base_ref: (0, k))
-    own = pl.BlockSpec((depth, block), lambda k, base_ref: (0, base_ref[0] * (width // block) + k))
-    return pl.pallas_call(
-        functools.partial(grad_kernel, factor, n_img),
-        grid_spec=pltpu.PrefetchScalarGridSpec(
-            num_scalar_prefetch=1, grid=(width // block,),
-            in_specs=[whole(weight.shape), whole((n_student, depth)), cols(n_student), cols(n_rows), own],
-            out_specs=cols(depth),
-            scratch_shapes=[pltpu.VMEM((depth, n_student), jnp.bfloat16), pltpu.VMEM((depth, n_rows), jnp.bfloat16)]),
-        out_shape=jax.ShapeDtypeStruct((depth, width), jnp.float32),
-        compiler_params=pltpu.CompilerParams(dimension_semantics=('arbitrary',), vmem_limit_bytes=40 << 20),
-        cost_estimate=pl.CostEstimate(flops=7 * 10 ** 9, bytes_accessed=33 << 20, transcendentals=0),
-    )(base, weight, s_all, exp_lo, hi, protos)
+            pltpu.VMEM((depth, n_student), low), pltpu.VMEM((depth, n_rows), low),
+            pltpu.VMEM((2, n_student, block), low), pltpu.VMEM((n_rows, width), low), pltpu.VMEM((depth, width), low),
+            dma, dma, dma((chips,)), dma((chips,)), dma((chips,)), dma((chips,)), dma((2,)), dma, dma],
+        compiler_params=pltpu.CompilerParams(collective_id=2, has_side_effects=True, vmem_limit_bytes=56 << 20),
+        cost_estimate=pl.CostEstimate(flops=30 * 10 ** 9, bytes_accessed=40 << 20, transcendentals=0),
+    )(weight, exp_u, hi_u, s_all, exp_lo, hi, protos)
 
 
 def solution(mesh):
@@ -608,11 +622,13 @@
         base = data_idx.reshape(1)
 
         rows_b = (ema_b_in, ema_b_mid, b_in, b_mid, ema_b_out, b_out)
-        biases = jnp.concatenate(rows_b).astype(jnp.float32)[None]
         starts = []
         for row in rows_b:
             starts.append(starts[-1] + width if starts else 0)
             width = row.shape[0]
+        total = starts[-1] + width
+        biases = sum(jnp.pad(row.astype(jnp.float32), (start, total - start - row.shape[0]))
+                     for row, start in zip(rows_b, starts))[None]
         offsets = (starts[0], starts[1], starts[4], starts[2], starts[3], starts[5])
         both = head_pass(teacher_x, student_x, biases, offsets, (ema_w_in, ema_w_mid, ema_w_out), (w_in, w_mid, w_out))
         both = gather_rows(both[None], data)
@@ -624,12 +640,10 @@
         scale = 1.0 / (n_img * dp_size * GLOBAL_CROPS * (ALL_CROPS - 1))
         factor = scale / TEMP_STUDENT
         sums, weight = crop_lines(row_part, s_all, hi_u, lo_u, sizes, n_img)
-        g_own = grad_pass(base, weight, s_all, exp_lo, q_hi, protos, factor, n_img)
+        g_emb, g_own = emb_grads(weight, exp_u, hi_u, s_all, exp_lo, q_hi, protos, sizes, n_img, factor)
+        g_emb = jnp.concatenate([g_emb[lane] for lane in range(g_emb.shape[0])], axis=1)
         g_own, half_wide = lax.optimization_barrier((g_own, half_wide))
         g_protos = lax.all_gather(g_own, data, axis=1, tiled=True)
-        weight, _ = lax.optimization_barrier((weight, g_own))
-        g_emb = emb_grads(weight, exp_u, hi_u, sizes, n_img, factor)
-        g_emb = jnp.concatenate([g_emb[lane] for lane in range(g_emb.shape[0])], axis=1)
 
         per_view = q_row[:n_rows // LANES].reshape(dp_size, GLOBAL_CROPS, n_img)
         pad = jnp.pad(per_view, ((0, 0), (0, ALL_CROPS - GLOBAL_CROPS), (0, 0)))
@@ -641,10 +655,16 @@
         hid_one, slope_one, half_x = mlp_layer(half_wide, w_in, biases, offsets[3])
         hid_two, slope_two = mlp_layer(hid_one, w_mid, biases, offsets[4])
         grads = mlp_backward(g_emb, half_x, (hid_one, slope_one, hid_two, slope_two), w_mid, w_out, b_out)
-        swap = lambda g: g + lax.ppermute(g, 'core', [(0, 1), (1, 0)])
-        biases = swap(jnp.concatenate([grads[1], grads[3], grads[5]]))
+        other = lambda g: lax.ppermute(g, 'core', [(0, 1), (1, 0)])
+        got_mid, got_in = other(grads[2]), other(grads[0])
+        sum_mid = grads[2] + got_mid
+        small = jnp.concatenate([grads[1], grads[3], grads[5]])
+        small, g_out, sum_mid = lax.optimization_barrier((small, grads[4], sum_mid))
+        got_small, got_out = other(small), other(g_out)
+        sum_in = grads[0] + got_in
+        biases = small + got_small
         b_grads = jnp.split(biases, [b_in.shape[0], b_in.shape[0] + b_mid.shape[0]])
-        return (loss, swap(grads[0]), b_grads[0], swap(grads[2]), b_grads[1], swap(grads[4]), b_grads[2], g_protos)
+        return (loss, sum_in, b_grads[0], sum_mid, b_grads[1], g_out + got_out, b_grads[2], g_protos)
 
     by_rows = P(data, None)
     by_cols = P(None, 'vp')

time: 404 us -> 371 us (0.918)
  Pallas kernels: 204 us -> 178 us
    pallas_call x2 -> x1, Pallas kernels: 74.7 us -> 48.1 us  [emb_grads(): pl.pallas_call(functools.partial(emb_kernel, sizes, n_img, factor, block)...]
    ppermute x4, waiting for transfers between devices: 17.4 us -> 0.01 us  [local_step(): other = lambda g: lax.ppermute(g, 'core', [(0, 1), (1, 0)])]
    all_gather x1, waiting for transfers between devices: 0.01 us -> 13.4 us  [local_step(): g_protos = lax.all_gather(g_own, data, axis=1, tiled=True)]
    unnamed x30 -> x19, local copies, waits for them, and re-layouts: 33.9 us -> 29.4 us
    add x4 -> x5, other arithmetic: 35.1 us -> 35.9 us  [the longest x1 17.5 us: local_step(): sum_mid = grads[2] + got_mid]
  transfers between devices with their start and end apart: 7 -> 7, of which waited for: 2 -> 2; matrix products, arithmetic and copies ran while one was open for 24% -> 26% of each run, Pallas kernels for 47% -> 44%
where the time goes in v4:
time: 371 us; the launch traced here: 370 us
  Pallas kernels  178 us (48%)
  matrix products  57.5 us (15%)
  waiting for transfers between devices  44.6 us (12%)
  other arithmetic  39.6 us (11%)
  local copies, waits for them, and re-layouts  33.2 us (9%)
  between operations  16.4 us (4%)
    pallas_call x1, Pallas kernels, emb_grads(): pl.pallas_call(functools.partial(emb_kernel, sizes, n_img, factor, block)...  48.1 us
    pallas_call x2, Pallas kernels, mlp_layer(): pl.pallas_call(functools.partial(layer_kernel, count // 4), grid=(width /...  43.8 us
    pallas_call x1, Pallas kernels, sinkhorn(): pl.pallas_call(functools.partial(sink_kernel, sizes, n_proto, 512), out_s...  34.3 us
    all_gather x2, waiting for transfers between devices, gather_rows(): lax.all_gather(vals.astype(jnp.float32), axis_name, axis=0, tiled=True)  31.1 us
    unnamed x19, local copies, waits for them, and re-layouts  29.4 us
    pallas_call x1, Pallas kernels, soft_pass(): pl.pallas_call(functools.partial(soft_kernel, 640), grid_spec=pltpu.Prefe...  26.9 us
    add x1, other arithmetic, local_step(): sum_mid = grads[2] + got_mid  17.5 us
    dot_general x1, matrix products, mlp_backward(): jnp.einsum('nh,gh->ng', g_pre_two_lo, w_mid, preferred_element_type=jnp.f...  16.9 us
  transfers between devices with their start and end apart: 7, of which 2 were waited for; matrix products, arithmetic and copies ran while one was open for 26% of the time, Pallas kernels for 44%

profile of v4, /device:TPU:0, one launch (start us, length us, event | category | flops | bytes accessed | tf_op | source)
XLA Modules:
  0.0 370.2 jit_solution(8461095994890699663)
XLA Ops:
  9.3 15.3 %shard_map.215 = f32[384,256]{1,0:T(8,128)} custom-call(bf16[64,1536]{1,0:T(8,128)(2,1)} %tx_ref.1, bf16[320,1536]{1,0:T(8,128)(2,1)} %sx_ref.1, f32[1,8704]{1,0:T(1,128)} %broadcast_in_dim.4.bias_ref, bf16[1536,2048]{1,0:T(8,128)(2,1)} %refs_0_.1, bf16[2048,2048]{1,0:T(8,128)(2,1)} %refs_1_.1, bf16[2048,256]{1,0:T(8,128)(2,1)} %refs_2_.1, ...), custom_call_target="tpu_custom_call" | custom-call | flops 10000000000 | bytes 35651584 | tf_op jit(solution)/shard_map/pallas_call | solution.py:216
  24.6 31.1 %all-gather.9.cloned.1.call-done = f32[3072,256]{1,0:T(8,128)} async-done(((f32[384,256]{1,0:T(8,128)}), f32[3072,256]{1,0:T(8,128)}) %all-gather.9.cloned.1.call-update) | async-done | bytes 3145744 | tf_op jit(solution)/shard_map/all_gather | solution.py:84
  55.7 1.5 convert_element_type.48
  57.5 1.9 copy-done
  59.4 34.3 %shard_map.216 = (bf16[512,4096]{1,0:T(8,128)(2,1)S(1)}, bf16[512,4096]{1,0:T(8,128)(2,1)S(1)}, f32[8,128]{1,0:T(8,128)S(1)}, bf16[2560,256]{1,0:T(8,128)(2,1)S(1)}) custom-call(f32[8,384,256]{2,1,0:T(8,128)S(1)} %bitcast.19, bf16[256,32768]{1,0:T(8,128)(2,1)} %ema_ref.1), custom_call_target="tpu_custom_call" | custom-call | flops 20000000000 | bytes 12582912 | tf_op jit(solution)/shard_map/pallas_call | solution.py:313
  93.7 2.0 copy-done.1
  95.7 2.0 copy-done.2
  97.7 26.9 %shard_map.217 = (bf16[2560,4096]{1,0:T(8,128)(2,1)}, f32[2560,128]{1,0:T(8,128)S(1)}, f32[2560,256]{1,0:T(8,128)}, f32[512,256]{1,0:T(8,128)S(1)}, f32[512,256]{1,0:T(8,128)S(1)}) custom-call(s32[1]{0:T(128)} %bitcast.1.base_ref, bf16[2560,256]{1,0:T(8,128)(2,1)S(1)} %get-tuple-element.35.s_ref, bf16[256,32768]{1,0:T(8,128)(2,1)} %protos_hbm.1, ...), custom_call_target="tpu_custom_call" | custom-call | flops 12999999488 | bytes 36700160 | tf_op jit(solution)/shard_map/pallas_call | solution.py:365
  124.7 9.2 %shard_map.218 = (f32[24,128]{1,0:T(8,128)S(1)}, f32[24,128]{1,0:T(8,128)S(1)}) custom-call(f32[2560,128]{1,0:T(8,128)S(1)} %get-tuple-element.38.part_ref, bf16[2560,256]{1,0:T(8,128)(2,1)S(1)} %get-tuple-element.35.s_ref, f32[512,256]{1,0:T(8,128)S(1)} %get-tuple-element.39.hi_u_ref, f32[512,256]{1,0:T(8,128)S(1)} %get-tuple-element.40.lo_u_ref), custom_call_target="tpu_custom_call" | custom-call | flops 5000000000 | bytes 4194304 | tf_op jit(solution)/shard_map/pallas_call | solution.py:568
  134.5 48.1 %shard_map.219 = (f32[2,1280,128]{2,1,0:T(8,128)}, f32[256,4096]{1,0:T(8,128)}) custom-call(f32[24,128]{1,0:T(8,128)} %copy-done.5, f32[2560,256]{1,0:T(8,128)} %get-tuple-element.43.exp_u_ref, f32[512,256]{1,0:T(8,128)} %copy-done.4, bf16[2560,256]{1,0:T(8,128)(2,1)} %copy-done.3, bf16[2560,4096]{1,0:T(8,128)(2,1)} %get-tuple-element.44.exp_hbm, ...), custom_call_target="tpu_custom_call" | custom-call | flops 30000001024 | bytes 41943040 | tf_op jit(solution)/shard_map/pallas_call | solution.py:589
  182.7 1.4 slice_bitcast_fusion.1
  184.1 21.7 %shard_map.220 = (bf16[1280,2048]{1,0:T(8,128)(2,1)}, f32[1280,2048]{1,0:T(8,128)}, bf16[1280,1536]{1,0:T(8,128)(2,1)}) custom-call(f32[1280,1536]{1,0:T(8,128)} %all-gather.5.cloned.1.call-done.feats_ref, bf16[1536,2048]{1,0:T(8,128)(2,1)} %w_ref.2, f32[1,8704]{1,0:T(1,128)} %broadcast_in_dim.4.bias_ref), custom_call_target="tpu_custom_call" | custom-call | flops 8053063680 | bytes 31457280 | tf_op jit(solution)/shard_map/pallas_call | solution.py:43
  205.7 22.1 %shard_map.221 = (bf16[1280,2048]{1,0:T(8,128)(2,1)}, f32[1280,2048]{1,0:T(8,128)}) custom-call(bf16[1280,2048]{1,0:T(8,128)(2,1)} %get-tuple-element.50.feats_ref, bf16[2048,2048]{1,0:T(8,128)(2,1)} %w_ref.3, f32[1,8704]{1,0:T(1,128)} %broadcast_in_dim.4.bias_ref), custom_call_target="tpu_custom_call" | custom-call | flops 10737418240 | bytes 31457280 | tf_op jit(solution)/shard_map/pallas_call | solution.py:43
  227.9 4.3 %multiply_reduce_fusion.1 = (f32[1280]{0:T(1024)S(1)}, f32[1280,256]{1,0:T(8,128)S(1)}) fusion(f32[256]{0:T(256)S(1)} %convert_element_type.47, bf16[1280,2048]{1,0:T(8,128)(2,1)} %get-tuple-element.51, bf16[2048,256]{1,0:T(8,128)(2,1)S(1)} %copy-done.7), kind=kOutput, calls=%fused_computation.13 | convolution fusion | flops 1343159040 | bytes 7608320 | tf_op jit(solution)/shard_map/dot_general | solution.py:56
  233.4 1.6 fusion.10
  235.0 16.5 %fusion.2 = f32[2048,2048]{1,0:T(8,128)} fusion(bf16[1280,2048]{1,0:T(8,128)(2,1)} %get-tuple-element.50.feats_ref, bf16[1280,2048]{1,0:T(8,128)(2,1)S(1)} %get-tuple-element.67), kind=kOutput, calls=%fused_computation.7 | convolution fusion | flops 10737418240 | bytes 27262976 | tf_op jit(solution)/shard_map/ng,nh->gh/dot_general | solution.py:65
  251.5 16.9 %fusion.11 = (f32[2048]{0:T(1024)S(1)}, bf16[1280,2048]{1,0:T(8,128)(2,1)}) fusion(f32[1280,2048]{1,0:T(8,128)} %get-tuple-element.53, bf16[2048,2048]{1,0:T(8,128)(2,1)} %w_ref.3, bf16[1280,2048]{1,0:T(8,128)(2,1)S(1)} %get-tuple-element.67), kind=kOutput, calls=%fused_computation.26 | convolution fusion | flops 10750523392 | bytes 29368320 | tf_op jit(solution)/shard_map/nh,gh->ng/dot_general | solution.py:66
  268.4 14.2 %fusion = f32[1536,2048]{1,0:T(8,128)} fusion(bf16[1280,1536]{1,0:T(8,128)(2,1)} %get-tuple-element.48, bf16[1280,2048]{1,0:T(8,128)(2,1)} %get-tuple-element.69), kind=kOutput, calls=%fused_computation.4 | convolution fusion | flops 8053063680 | bytes 21757952 | tf_op jit(solution)/shard_map/nf,nh->fh/dot_general | solution.py:68
  283.1 4.1 %fusion.5 = f32[2048,256]{1,0:T(8,128)S(1)} fusion(bf16[1280,2048]{1,0:T(8,128)(2,1)} %get-tuple-element.51, bf16[1280,256]{1,0:T(8,128)(2,1)S(1)} %get-tuple-element.59), kind=kOutput, calls=%fused_computation.16 | convolution fusion | flops 1342177280 | bytes 7995392 | tf_op jit(solution)/shard_map/nh,nb->hb/dot_general | solution.py:61
  287.2 17.5 %add.65 = f32[2048,2048]{1,0:T(8,128)} add(f32[2048,2048]{1,0:T(8,128)} %fusion.2, f32[2048,2048]{1,0:T(8,128)} %collective-permute-done.1) | non-fusion elementwise | flops 4194304 | bytes 50331648 | tf_op jit(solution)/shard_map/add | solution.py:660
  307.9 14.4 %add.64 = f32[1536,2048]{1,0:T(8,128)} add(f32[1536,2048]{1,0:T(8,128)} %fusion, f32[1536,2048]{1,0:T(8,128)} %collective-permute-done) | non-fusion elementwise | flops 3145728 | bytes 37748736 | tf_op jit(solution)/shard_map/add | solution.py:664
  323.6 3.2 add.67
  326.7 13.4 %all-gather.7.cloned.1.call-done = f32[256,32768]{1,0:T(8,128)} async-done(((f32[256,4096]{1,0:T(8,128)}), f32[256,32768]{1,0:T(8,128)}) %all-gather.7.cloned.1.call-update) | async-done | bytes 33554448 | tf_op jit(solution)/shard_map/all_gather | solution.py:646
  340.1 22.5 %copy.28 = f32[256,32768]{1,0:T(8,128)} copy(f32[256,32768]{1,0:T(8,128)} %all-gather.7.cloned.1.call-done) | data formatting | bytes 67108864
  (47 shorter events, 7.8 us)
Async XLA Ops:
  7.2 48.6 %all-gather.9.cloned.1.call-start = ((), (), s32[]{:S(2)}) async-start(), calls=%async_computation.2 | async-start | bytes 3538944 | tf_op jit(solution)/shard_map/all_gather | solution.py:84
  9.3 46.5 %copy-start.8 = (bf16[320,1536]{1,0:T(8,128)(2,1)S(1)}, bf16[320,1536]{1,0:T(8,128)(2,1)}, u32[]{:S(2)}) copy-start(bf16[320,1536]{1,0:T(8,128)(2,1)} %sx_ref.1) | copy-start | bytes 2949124
  24.6 158.1 %all-gather.5.cloned.1.call-start = ((), (), s32[]{:S(2)}) async-start(), calls=%async_computation | async-start | bytes 9830400 | tf_op jit(solution)/shard_map/all_gather | solution.py:84
  57.3 282.9 %all-gather.7.cloned.1.call-start = ((), (), s32[]{:S(2)}) async-start(), calls=%async_computation.1 | async-start | bytes 37748736 | tf_op jit(solution)/shard_map/all_gather | solution.py:646
  57.5 1.9 copy-start
  93.7 2.0 copy-start.1
  95.7 2.0 copy-start.2
  97.7 26.9 %copy-start.3 = (bf16[2560,256]{1,0:T(8,128)(2,1)}, bf16[2560,256]{1,0:T(8,128)(2,1)S(1)}, u32[]{:S(2)}) copy-start(bf16[2560,256]{1,0:T(8,128)(2,1)S(1)} %get-tuple-element.35.s_ref) | copy-start | bytes 3932164
  124.7 9.2 %copy-start.4 = (f32[512,256]{1,0:T(8,128)}, f32[512,256]{1,0:T(8,128)S(1)}, u32[]{:S(2)}) copy-start(f32[512,256]{1,0:T(8,128)S(1)} %get-tuple-element.39.hi_u_ref) | copy-start | bytes 1572868
  133.9 0.6 copy-start.5
  205.7 22.1 %copy-start.7 = (bf16[2048,256]{1,0:T(8,128)(2,1)S(1)}, bf16[2048,256]{1,0:T(8,128)(2,1)}, u32[]{:S(2)}) copy-start(bf16[2048,256]{1,0:T(8,128)(2,1)} %refs_5_.1) | copy-start | bytes 3145732
  227.9 5.5 %copy-start.6 = (f32[1280,2048]{1,0:T(8,128)S(1)}, f32[1280,2048]{1,0:T(8,128)}, u32[]{:S(2)}) copy-start(f32[1280,2048]{1,0:T(8,128)} %get-tuple-element.52) | copy-start | bytes 31457284
  251.5 35.7 %collective-permute-start.1 = (f32[2048,2048]{1,0:T(8,128)}, f32[2048,2048]{1,0:T(8,128)}, u32[]{:S(2)}, u32[]{:S(2)}) collective-permute-start(f32[2048,2048]{1,0:T(8,128)} %fusion.2), channel_id=1, source_target_pairs={{0,1},{1,0},{2,3},{3,2},{4,5},{5,4},{6,7},{7,6},{8,9},{9,8},{10,11... | collective-permute-start | bytes 50331656 | tf_op jit(solution)/shard_map/ppermute | solution.py:658
  282.6 25.3 %collective-permute-start = (f32[1536,2048]{1,0:T(8,128)}, f32[1536,2048]{1,0:T(8,128)}, u32[]{:S(2)}, u32[]{:S(2)}) collective-permute-start(f32[1536,2048]{1,0:T(8,128)} %fusion), channel_id=1, source_target_pairs={{0,1},{1,0},{2,3},{3,2},{4,5},{5,4},{6,7},{7,6},{8,9},{9,8},{10,11... | collective-permute-start | bytes 37748744 | tf_op jit(solution)/shard_map/ppermute | solution.py:658
  304.7 18.8 %collective-permute-start.3 = (f32[2048,256]{1,0:T(8,128)S(1)}, f32[2048,256]{1,0:T(8,128)}, u32[]{:S(2)}, u32[]{:S(2)}) collective-permute-start(f32[2048,256]{1,0:T(8,128)S(1)} %fusion.5), channel_id=1, source_target_pairs={{0,1},{1,0},{2,3},{3,2},{4,5},{5,4},{6,7},{7,6},{8,9},{9,8},{10,11... | collective-permute-start | bytes 6291464 | tf_op jit(solution)/shard_map/ppermute | solution.py:658
  305.0 17.4 %collective-permute-start.2 = (f32[4352]{0:T(1024)S(1)}, f32[4352]{0:T(1024)S(1)}, u32[]{:S(2)}, u32[]{:S(2)}) collective-permute-start(f32[4352]{0:T(1024)S(1)} %pad_maximum_fusion.1), channel_id=1, source_target_pairs={{0,1},{1,0},{2,3},{3,2},{4,5},{5,4},{6,7},{7,6},{8,9},{9,8},{10,11... | collective-permute-start | bytes 52232 | tf_op jit(solution)/shard_map/ppermute | solution.py:658
Sparse Core Ops, SparseCore 0:
  24.7 30.9 all-gather.8
  58.1 83.4 all-gather.4
  182.8 157.2 all-gather.6

commit v5 on v4

--- a/solution.py
+++ b/solution.py
@@ -440,7 +440,7 @@
 
 
 def emb_kernel(sizes, n_img, factor, block, weight_ref, exp_u_ref, hi_u_ref, s_ref, exp_hbm, hi_hbm, protos_hbm,
-               out_ref, own_ref,
+               out_ref, early_ref, late_ref,
                wide_ref, g_ref, near_recv, acc_ref, piece_recv, piece_ref, gathered, full_ref,
                soft_ref, pair_ref, exp_ref, hi_ref, v_ref,
                near_send_sem, near_recv_sem, piece_send_sem, piece_recv_sem, all_send_sem, all_recv_sem,
@@ -458,8 +458,9 @@
     core = lax.rem(me, 2)
     chip = me // 2
     greet_all(sizes, n_dev)
-    width = own_ref.shape[1]
+    width = hi_hbm.shape[1]
     steps = width // block
+    turn = early_ref.shape[1] // block
 
     def fetch(step):
         cols = pl.ds(pl.multiple_of(step * block, block), block)
@@ -473,7 +474,7 @@
     get_hi.start()
     fetch(0).start()
 
-    def grad_block(step, carry):
+    def grad_block(dest_ref, start, step, carry):
         cols = pl.ds(pl.multiple_of(step * block, block), block)
 
         @pl.when(step + 1 < steps)
@@ -486,7 +487,8 @@
         proto_f = v_ref[:, cols].astype(jnp.float32)
         inv_col = lax.rsqrt(jnp.sum(proto_f * proto_f, axis=0, keepdims=True))
         unit = proto_f * inv_col
-        own_ref[:, cols] = (g_unit - unit * jnp.sum(unit * g_unit, axis=0, keepdims=True)) * inv_col
+        land = pl.ds(pl.multiple_of((step - start) * block, block), block)
+        dest_ref[:, land] = (g_unit - unit * jnp.sum(unit * g_unit, axis=0, keepdims=True)) * inv_col
         return carry
 
     weight = weight_ref[...]
@@ -530,7 +532,8 @@
             device_id=place_of(peer * 2 + core, sizes), device_id_type=mesh_type)
         copy.start()
         copies.append(copy)
-    lax.fori_loop(0, steps // 2, grad_block, 0)
+    into_early = functools.partial(grad_block, early_ref, 0)
+    lax.fori_loop(0, steps // 2, into_early, 0)
     total = acc_ref[pl.ds(pl.multiple_of(chip * piece, n_img), piece), :]
     for step in range(1, chips):
         copies[step - 1].wait()
@@ -545,7 +548,8 @@
         copy.start()
         copies.append(copy)
     full_ref[pl.ds(pl.multiple_of(chip * piece, n_img), piece), :] = total
-    lax.fori_loop(steps // 2, steps, grad_block, 0)
+    lax.fori_loop(steps // 2, turn, into_early, 0)
+    lax.fori_loop(turn, steps, functools.partial(grad_block, late_ref, turn), 0)
     for step in range(1, chips):
         copies[step - 1].wait()
         owner = lax.rem(chip + chips - step, chips)
@@ -588,8 +592,9 @@
     dma = pltpu.SemaphoreType.DMA
     return pl.pallas_call(
         functools.partial(emb_kernel, sizes, n_img, factor, block),
-        out_shape=(jax.ShapeDtypeStruct((depth // LANES, half, LANES), wide), jax.ShapeDtypeStruct((depth, width), wide)),
-        in_specs=[vmem] * 4 + [hbm] * 3, out_specs=(vmem,) * 2,
+        out_shape=(jax.ShapeDtypeStruct((depth // LANES, half, LANES), wide), jax.ShapeDtypeStruct((depth, width - width // 4), wide),
+                   jax.ShapeDtypeStruct((depth, width // 4), wide)),
+        in_specs=[vmem] * 4 + [hbm] * 3, out_specs=(vmem,) * 3,
         scratch_shapes=[
             pltpu.VMEM((n_student, LANES), wide), pltpu.VMEM((2, half, depth), wide), pltpu.VMEM((half, depth), wide),
             pltpu.VMEM((half, depth), wide), pltpu.VMEM((chips, half // chips, depth), wide),
@@ -603,6 +608,25 @@
     )(weight, exp_u, hi_u, s_all, exp_lo, hi, protos)
 
 
+def place_kernel(src_ref, *refs):
+    refs[-1][...] = src_ref[...]
+
+
+def place_blocks(src, shards, block, total, first, held=None):
+    depth, width = src.shape
+    count = width // (shards * block)
+    stride = total // (shards * block)
+    in_specs = [pl.BlockSpec((depth, block), lambda d, j: (0, d * count + j))]
+    return pl.pallas_call(
+        place_kernel, grid=(shards, count), out_shape=jax.ShapeDtypeStruct((depth, total), src.dtype),
+        in_specs=in_specs + [pl.BlockSpec(memory_space=pl.ANY)] * (held is not None),
+        out_specs=pl.BlockSpec((depth, block), lambda d, j: (0, d * stride + first + j)),
+        input_output_aliases={} if held is None else {1: 0},
+        compiler_params=pltpu.CompilerParams(dimension_semantics=('arbitrary', 'arbitrary')),
+        cost_estimate=pl.CostEstimate(flops=10 ** 9, bytes_accessed=8 * depth * width, transcendentals=0),
+    )(*((src,) if held is None else (src, held)))
+
+
 def solution(mesh):
     vp_size = mesh.shape['vp']
     dp_size = mesh.shape['dp']
@@ -632,7 +656,7 @@
         offsets = (starts[0], starts[1], starts[4], starts[2], starts[3], starts[5])
         both = head_pass(teacher_x, student_x, biases, offsets, (ema_w_in, ema_w_mid, ema_w_out), (w_in, w_mid, w_out))
         both = gather_rows(both[None], data)
-        both, own_x = lax.optimization_barrier((both, student_x))
+        both, own_x = lax.optimization_barrier((both, student_x.astype(jnp.float32)))
         half_wide = gather_rows(own_x, ('y', 'x'))
 
         q_hi, q_lo, q_row, s_all = sinkhorn(both, ema_protos, sizes, n_proto, n_rows, part)
@@ -640,10 +664,10 @@
         scale = 1.0 / (n_img * dp_size * GLOBAL_CROPS * (ALL_CROPS - 1))
         factor = scale / TEMP_STUDENT
         sums, weight = crop_lines(row_part, s_all, hi_u, lo_u, sizes, n_img)
-        g_emb, g_own = emb_grads(weight, exp_u, hi_u, s_all, exp_lo, q_hi, protos, sizes, n_img, factor)
+        g_emb, g_early, g_late = emb_grads(weight, exp_u, hi_u, s_all, exp_lo, q_hi, protos, sizes, n_img, factor)
         g_emb = jnp.concatenate([g_emb[lane] for lane in range(g_emb.shape[0])], axis=1)
-        g_own, half_wide = lax.optimization_barrier((g_own, half_wide))
-        g_protos = lax.all_gather(g_own, data, axis=1, tiled=True)
+        g_early, g_late, half_wide = lax.optimization_barrier((g_early, g_late, half_wide))
+        all_early = lax.all_gather(g_early, data, axis=1, tiled=True)
 
         per_view = q_row[:n_rows // LANES].reshape(dp_size, GLOBAL_CROPS, n_img)
         pad = jnp.pad(per_view, ((0, 0), (0, ALL_CROPS - GLOBAL_CROPS), (0, 0)))
@@ -653,6 +677,8 @@
         loss = (jnp.sum(t_row * jnp.log(row_line)) - hits / TEMP_STUDENT) * scale
 
         hid_one, slope_one, half_x = mlp_layer(half_wide, w_in, biases, offsets[3])
+        hid_one, g_late = lax.optimization_barrier((hid_one, g_late))
+        all_late = lax.all_gather(g_late, data, axis=1, tiled=True)
         hid_two, slope_two = mlp_layer(hid_one, w_mid, biases, offsets[4])
         grads = mlp_backward(g_emb, half_x, (hid_one, slope_one, hid_two, slope_two), w_mid, w_out, b_out)
         other = lambda g: lax.ppermute(g, 'core', [(0, 1), (1, 0)])
@@ -663,8 +689,13 @@
         got_small, got_out = other(small), other(g_out)
         sum_in = grads[0] + got_in
         biases = small + got_small
+        sum_out = g_out + got_out
+        all_early, sum_in, sum_out, biases = lax.optimization_barrier((all_early, sum_in, sum_out, biases))
+        block = part // 4
+        g_protos = place_blocks(all_early, dp_size, block, protos.shape[1], 0)
+        g_protos = place_blocks(all_late, dp_size, block, protos.shape[1], 3, g_protos)
         b_grads = jnp.split(biases, [b_in.shape[0], b_in.shape[0] + b_mid.shape[0]])
-        return (loss, sum_in, b_grads[0], sum_mid, b_grads[1], g_out + got_out, b_grads[2], g_protos)
+        return (loss, sum_in, b_grads[0], sum_mid, b_grads[1], sum_out, b_grads[2], g_protos)
 
     by_rows = P(data, None)
     by_cols = P(None, 'vp')

time: 371 us -> 375 us (1.011)
  Pallas kernels: 178 us -> 212 us
  local copies, waits for them, and re-layouts: 33.2 us -> 10.8 us
  waiting for transfers between devices: 44.6 us -> 36.2 us
    pallas_call x0 -> x2, Pallas kernels: none -> 34.9 us  [place_blocks(): pl.pallas_call(place_kernel, grid=(shards, count), out_shape=jax.ShapeDty...]
    unnamed x19 -> x22, local copies, waits for them, and re-layouts: 29.4 us -> 6.92 us
    all_gather x1 -> x2, waiting for transfers between devices: 13.4 us -> 6.53 us  [the longest x1 6.53 us: local_step(): all_late = lax.all_gather(g_late, data, axis=1, tiled=True)]
  transfers between devices with their start and end apart: 7 -> 8, of which waited for: 2 -> 2; matrix products, arithmetic and copies ran while one was open for 26% -> 26% of each run, Pallas kernels for 44% -> 50%
where the time goes in v5:
time: 375 us; the launch traced here: 373 us
  Pallas kernels  212 us (57%)
  matrix products  56.3 us (15%)
  other arithmetic  39.6 us (11%)
  waiting for transfers between devices  36.2 us (10%)
  between operations  16.4 us (4%)
  local copies, waits for them, and re-layouts  10.8 us (3%)
    pallas_call x1, Pallas kernels, emb_grads(): pl.pallas_call(functools.partial(emb_kernel, sizes, n_img, factor, block)...  48.2 us
    pallas_call x2, Pallas kernels, mlp_layer(): pl.pallas_call(functools.partial(layer_kernel, count // 4), grid=(width /...  43.7 us
    pallas_call x2, Pallas kernels, place_blocks(): pl.pallas_call(place_kernel, grid=(shards, count), out_shape=jax.ShapeDty...  34.9 us
    pallas_call x1, Pallas kernels, sinkhorn(): pl.pallas_call(functools.partial(sink_kernel, sizes, n_proto, 512), out_s...  34.3 us
    all_gather x2, waiting for transfers between devices, gather_rows(): lax.all_gather(vals.astype(jnp.float32), axis_name, axis=0, tiled=True)  29.6 us
    pallas_call x1, Pallas kernels, soft_pass(): pl.pallas_call(functools.partial(soft_kernel, 640), grid_spec=pltpu.Prefe...  26.9 us
    dot_general x1, matrix products, mlp_backward(): jnp.einsum('ng,nh->gh', hid_one, g_pre_two_lo, preferred_element_type=jnp...  18.4 us
    add x1, other arithmetic, local_step(): sum_mid = grads[2] + got_mid  17.5 us
  transfers between devices with their start and end apart: 8, of which 2 were waited for; matrix products, arithmetic and copies ran while one was open for 26% of the time, Pallas kernels for 50%

profile of v5, /device:TPU:0, one launch (start us, length us, event | category | flops | bytes accessed | tf_op | source)
XLA Modules:
  0.0 373.4 jit_solution(723541231390080035)
XLA Ops:
  9.3 15.3 %shard_map.215 = f32[384,256]{1,0:T(8,128)} custom-call(bf16[64,1536]{1,0:T(8,128)(2,1)} %tx_ref.1, bf16[320,1536]{1,0:T(8,128)(2,1)} %sx_ref.1, f32[1,8704]{1,0:T(1,128)} %broadcast_in_dim.4.bias_ref, bf16[1536,2048]{1,0:T(8,128)(2,1)} %refs_0_.1, bf16[2048,2048]{1,0:T(8,128)(2,1)} %refs_1_.1, bf16[2048,256]{1,0:T(8,128)(2,1)} %refs_2_.1, ...), custom_call_target="tpu_custom_call" | custom-call | flops 10000000000 | bytes 35651584 | tf_op jit(solution)/shard_map/pallas_call | solution.py:216
  24.6 1.5 convert_element_type.48
  26.1 29.6 %all-gather.12.cloned.1.call-done = f32[3072,256]{1,0:T(8,128)} async-done(((f32[384,256]{1,0:T(8,128)}), f32[3072,256]{1,0:T(8,128)}) %all-gather.12.cloned.1.call-update) | async-done | bytes 3145744 | tf_op jit(solution)/shard_map/all_gather | solution.py:84
  56.0 1.9 copy-done
  57.9 34.3 %shard_map.216 = (bf16[512,4096]{1,0:T(8,128)(2,1)S(1)}, bf16[512,4096]{1,0:T(8,128)(2,1)S(1)}, f32[8,128]{1,0:T(8,128)S(1)}, bf16[2560,256]{1,0:T(8,128)(2,1)S(1)}) custom-call(f32[8,384,256]{2,1,0:T(8,128)S(1)} %bitcast.19, bf16[256,32768]{1,0:T(8,128)(2,1)} %ema_ref.1), custom_call_target="tpu_custom_call" | custom-call | flops 20000000000 | bytes 12582912 | tf_op jit(solution)/shard_map/pallas_call | solution.py:313
  92.2 2.0 copy-done.1
  94.2 2.0 copy-done.2
  96.2 26.9 %shard_map.217 = (bf16[2560,4096]{1,0:T(8,128)(2,1)}, f32[2560,128]{1,0:T(8,128)S(1)}, f32[2560,256]{1,0:T(8,128)}, f32[512,256]{1,0:T(8,128)S(1)}, f32[512,256]{1,0:T(8,128)S(1)}) custom-call(s32[1]{0:T(128)} %bitcast.1.base_ref, bf16[2560,256]{1,0:T(8,128)(2,1)S(1)} %get-tuple-element.43.s_ref, bf16[256,32768]{1,0:T(8,128)(2,1)} %protos_hbm.1, ...), custom_call_target="tpu_custom_call" | custom-call | flops 12999999488 | bytes 36700160 | tf_op jit(solution)/shard_map/pallas_call | solution.py:365
  123.1 9.2 %shard_map.218 = (f32[24,128]{1,0:T(8,128)S(1)}, f32[24,128]{1,0:T(8,128)S(1)}) custom-call(f32[2560,128]{1,0:T(8,128)S(1)} %get-tuple-element.46.part_ref, bf16[2560,256]{1,0:T(8,128)(2,1)S(1)} %get-tuple-element.43.s_ref, f32[512,256]{1,0:T(8,128)S(1)} %get-tuple-element.47.hi_u_ref, f32[512,256]{1,0:T(8,128)S(1)} %get-tuple-element.48.lo_u_ref), custom_call_target="tpu_custom_call" | custom-call | flops 5000000000 | bytes 4194304 | tf_op jit(solution)/shard_map/pallas_call | solution.py:572
  132.9 48.2 %shard_map.219 = (f32[2,1280,128]{2,1,0:T(8,128)}, f32[256,3072]{1,0:T(8,128)}, f32[256,1024]{1,0:T(8,128)}) custom-call(f32[24,128]{1,0:T(8,128)} %copy-done.5, f32[2560,256]{1,0:T(8,128)} %get-tuple-element.51.exp_u_ref, f32[512,256]{1,0:T(8,128)} %copy-done.4, bf16[2560,256]{1,0:T(8,128)(2,1)} %copy-done.3, bf16[2560,4096]{1,0:T(8,128)(2,1)} %get-tuple-element.52.exp_hbm, ...), custom_call_target="tpu_custom_call" | custom-call | flops 30000001024 | bytes 41943040 | tf_op jit(solution)/shard_map/pallas_call | solution.py:593
  182.8 21.6 %shard_map.220 = (bf16[1280,2048]{1,0:T(8,128)(2,1)}, f32[1280,2048]{1,0:T(8,128)}, bf16[1280,1536]{1,0:T(8,128)(2,1)}) custom-call(f32[1280,1536]{1,0:T(8,128)} %all-gather.6.cloned.1.call-done.feats_ref, bf16[1536,2048]{1,0:T(8,128)(2,1)} %w_ref.2, f32[1,8704]{1,0:T(1,128)} %broadcast_in_dim.4.bias_ref), custom_call_target="tpu_custom_call" | custom-call | flops 8053063680 | bytes 31457280 | tf_op jit(solution)/shard_map/pallas_call | solution.py:43
  204.5 22.1 %shard_map.221 = (bf16[1280,2048]{1,0:T(8,128)(2,1)}, f32[1280,2048]{1,0:T(8,128)}) custom-call(bf16[1280,2048]{1,0:T(8,128)(2,1)} %get-tuple-element.62.feats_ref, bf16[2048,2048]{1,0:T(8,128)(2,1)} %w_ref.3, f32[1,8704]{1,0:T(1,128)} %broadcast_in_dim.4.bias_ref), custom_call_target="tpu_custom_call" | custom-call | flops 10737418240 | bytes 31457280 | tf_op jit(solution)/shard_map/pallas_call | solution.py:43
  226.6 4.3 %multiply_reduce_fusion.1 = (f32[1280]{0:T(1024)S(1)}, f32[1280,256]{1,0:T(8,128)S(1)}) fusion(f32[256]{0:T(256)S(1)} %convert_element_type.47, bf16[1280,2048]{1,0:T(8,128)(2,1)} %get-tuple-element.63, bf16[2048,256]{1,0:T(8,128)(2,1)S(1)} %copy-done.8), kind=kOutput, calls=%fused_computation.13 | convolution fusion | flops 1343159040 | bytes 7608320 | tf_op jit(solution)/shard_map/dot_general | solution.py:56
  232.1 1.6 fusion.10
  233.7 18.4 %fusion.2 = f32[2048,2048]{1,0:T(8,128)} fusion(bf16[1280,2048]{1,0:T(8,128)(2,1)} %get-tuple-element.62.feats_ref, bf16[1280,2048]{1,0:T(8,128)(2,1)S(1)} %get-tuple-element.83), kind=kOutput, calls=%fused_computation.7 | convolution fusion | flops 10737418240 | bytes 27262976 | tf_op jit(solution)/shard_map/ng,nh->gh/dot_general | solution.py:65
  252.2 17.0 %fusion.11 = (f32[2048]{0:T(1024)S(1)}, bf16[1280,2048]{1,0:T(8,128)(2,1)S(1)}) fusion(f32[1280,2048]{1,0:T(8,128)} %get-tuple-element.65, bf16[2048,2048]{1,0:T(8,128)(2,1)} %w_ref.3, bf16[1280,2048]{1,0:T(8,128)(2,1)} %copy-done.7), kind=kOutput, calls=%fused_computation.26 | convolution fusion | flops 10750523392 | bytes 29368320 | tf_op jit(solution)/shard_map/nh,gh->ng/dot_general | solution.py:66
  269.2 10.8 %fusion = f32[1536,2048]{1,0:T(8,128)} fusion(bf16[1280,1536]{1,0:T(8,128)(2,1)S(1)} %copy-done.10, bf16[1280,2048]{1,0:T(8,128)(2,1)S(1)} %get-tuple-element.85), kind=kOutput, calls=%fused_computation.4 | convolution fusion | flops 8053063680 | bytes 21757952 | tf_op jit(solution)/shard_map/nf,nh->fh/dot_general | solution.py:68
  280.6 4.1 %fusion.5 = f32[2048,256]{1,0:T(8,128)S(1)} fusion(bf16[1280,2048]{1,0:T(8,128)(2,1)} %get-tuple-element.63, bf16[1280,256]{1,0:T(8,128)(2,1)S(1)} %get-tuple-element.75), kind=kOutput, calls=%fused_computation.16 | convolution fusion | flops 1342177280 | bytes 7995392 | tf_op jit(solution)/shard_map/nh,nb->hb/dot_general | solution.py:61
  284.7 17.5 %add.65 = f32[2048,2048]{1,0:T(8,128)} add(f32[2048,2048]{1,0:T(8,128)} %fusion.2, f32[2048,2048]{1,0:T(8,128)} %collective-permute-done.1) | non-fusion elementwise | flops 4194304 | bytes 50331648 | tf_op jit(solution)/shard_map/add | solution.py:686
  305.5 14.4 %add.64 = f32[1536,2048]{1,0:T(8,128)} add(f32[1536,2048]{1,0:T(8,128)} %fusion, f32[1536,2048]{1,0:T(8,128)} %collective-permute-done) | non-fusion elementwise | flops 3145728 | bytes 37748736 | tf_op jit(solution)/shard_map/add | solution.py:690
  319.9 3.2 add.66
  323.7 25.9 %shard_map.222.refs_0_ = f32[256,32768]{1,0:T(8,128)} custom-call(f32[256,24576]{1,0:T(8,128)} %all-gather.8.cloned.1.call-done.src_ref), custom_call_target="tpu_custom_call" | custom-call | flops 1000000000 | bytes 50331648 | tf_op jit(solution)/shard_map/pallas_call | solution.py:620
  350.2 6.5 %all-gather.10.cloned.1.call-done.src_ref = f32[256,8192]{1,0:T(8,128)} async-done(((f32[256,1024]{1,0:T(8,128)}), f32[256,8192]{1,0:T(8,128)}) %all-gather.10.cloned.1.call-update) | async-done | bytes 8388624 | tf_op jit(solution)/shard_map/all_gather | solution.py:681
  356.7 9.0 %shard_map.223 = f32[256,32768]{1,0:T(8,128)} custom-call(f32[256,8192]{1,0:T(8,128)} %all-gather.10.cloned.1.call-done.src_ref, f32[256,32768]{1,0:T(8,128)} %shard_map.222.refs_0_), custom_call_target="tpu_custom_call", output_to_operand_aliasing={{}: (1, {})} | custom-call | flops 1000000000 | bytes 16777216 | tf_op jit(solution)/shard_map/pallas_call | solution.py:620
  (55 shorter events, 9.5 us)
Async XLA Ops:
  7.2 48.6 %all-gather.12.cloned.1.call-start = ((), (), s32[]{:S(2)}) async-start(), calls=%async_computation.3 | async-start | bytes 3538944 | tf_op jit(solution)/shard_map/all_gather | solution.py:84
  9.3 15.4 %copy-start.9 = (bf16[320,1536]{1,0:T(8,128)(2,1)S(1)}, bf16[320,1536]{1,0:T(8,128)(2,1)}, u32[]{:S(2)}) copy-start(bf16[320,1536]{1,0:T(8,128)(2,1)} %sx_ref.1) | copy-start | bytes 2949124
  24.6 156.6 %all-gather.6.cloned.1.call-start = ((), (), s32[]{:S(2)}) async-start(), calls=%async_computation | async-start | bytes 9830400 | tf_op jit(solution)/shard_map/all_gather | solution.py:84
  55.8 267.4 %all-gather.8.cloned.1.call-start = ((), (), s32[]{:S(2)}) async-start(), calls=%async_computation.1 | async-start | bytes 28311552 | tf_op jit(solution)/shard_map/all_gather | solution.py:670
  56.0 1.9 copy-start
  92.2 2.0 copy-start.1
  94.2 2.0 copy-start.2
  96.2 26.9 %copy-start.3 = (bf16[2560,256]{1,0:T(8,128)(2,1)}, bf16[2560,256]{1,0:T(8,128)(2,1)S(1)}, u32[]{:S(2)}) copy-start(bf16[2560,256]{1,0:T(8,128)(2,1)S(1)} %get-tuple-element.43.s_ref) | copy-start | bytes 3932164
  123.1 9.2 %copy-start.4 = (f32[512,256]{1,0:T(8,128)}, f32[512,256]{1,0:T(8,128)S(1)}, u32[]{:S(2)}) copy-start(f32[512,256]{1,0:T(8,128)S(1)} %get-tuple-element.47.hi_u_ref) | copy-start | bytes 1572868
  132.3 0.6 copy-start.5
  181.2 175.5 %all-gather.10.cloned.1.call-start = ((), (), s32[]{:S(2)}) async-start(), calls=%async_computation.2 | async-start | bytes 9437184 | tf_op jit(solution)/shard_map/all_gather | solution.py:681
  204.4 22.1 %copy-start.8 = (bf16[2048,256]{1,0:T(8,128)(2,1)S(1)}, bf16[2048,256]{1,0:T(8,128)(2,1)}, u32[]{:S(2)}) copy-start(bf16[2048,256]{1,0:T(8,128)(2,1)} %refs_5_.1) | copy-start | bytes 3145732
  226.6 5.5 %copy-start.6 = (f32[1280,2048]{1,0:T(8,128)S(1)}, f32[1280,2048]{1,0:T(8,128)}, u32[]{:S(2)}) copy-start(f32[1280,2048]{1,0:T(8,128)} %get-tuple-element.64) | copy-start | bytes 31457284
  233.7 18.4 %copy-start.7 = (bf16[1280,2048]{1,0:T(8,128)(2,1)}, bf16[1280,2048]{1,0:T(8,128)(2,1)S(1)}, u32[]{:S(2)}) copy-start(bf16[1280,2048]{1,0:T(8,128)(2,1)S(1)} %get-tuple-element.83) | copy-start | bytes 15728644
  252.1 32.6 %collective-permute-start.1 = (f32[2048,2048]{1,0:T(8,128)}, f32[2048,2048]{1,0:T(8,128)}, u32[]{:S(2)}, u32[]{:S(2)}) collective-permute-start(f32[2048,2048]{1,0:T(8,128)} %fusion.2), channel_id=1, source_target_pairs={{0,1},{1,0},{2,3},{3,2},{4,5},{5,4},{6,7},{7,6},{8,9},{9,8},{10,11... | collective-permute-start | bytes 50331656 | tf_op jit(solution)/shard_map/ppermute | solution.py:684
  252.2 17.0 %copy-start.10 = (bf16[1280,1536]{1,0:T(8,128)(2,1)S(1)}, bf16[1280,1536]{1,0:T(8,128)(2,1)}, u32[]{:S(2)}) copy-start(bf16[1280,1536]{1,0:T(8,128)(2,1)} %get-tuple-element.58) | copy-start | bytes 11796484
  280.1 25.4 %collective-permute-start = (f32[1536,2048]{1,0:T(8,128)}, f32[1536,2048]{1,0:T(8,128)}, u32[]{:S(2)}, u32[]{:S(2)}) collective-permute-start(f32[1536,2048]{1,0:T(8,128)} %fusion), channel_id=1, source_target_pairs={{0,1},{1,0},{2,3},{3,2},{4,5},{5,4},{6,7},{7,6},{8,9},{9,8},{10,11... | collective-permute-start | bytes 37748744 | tf_op jit(solution)/shard_map/ppermute | solution.py:684
  302.3 17.6 %collective-permute-start.2 = (f32[2048,256]{1,0:T(8,128)S(1)}, f32[2048,256]{1,0:T(8,128)}, u32[]{:S(2)}, u32[]{:S(2)}) collective-permute-start(f32[2048,256]{1,0:T(8,128)S(1)} %fusion.5), channel_id=1, source_target_pairs={{0,1},{1,0},{2,3},{3,2},{4,5},{5,4},{6,7},{7,6},{8,9},{9,8},{10,11... | collective-permute-start | bytes 6291464 | tf_op jit(solution)/shard_map/ppermute | solution.py:684
  302.5 17.4 %collective-permute-start.3 = (f32[4352]{0:T(1024)S(1)}, f32[4352]{0:T(1024)S(1)}, u32[]{:S(2)}, u32[]{:S(2)}) collective-permute-start(f32[4352]{0:T(1024)S(1)} %pad_maximum_fusion.1), channel_id=1, source_target_pairs={{0,1},{1,0},{2,3},{3,2},{4,5},{5,4},{6,7},{7,6},{8,9},{9,8},{10,11... | collective-permute-start | bytes 52232 | tf_op jit(solution)/shard_map/ppermute | solution.py:684
Sparse Core Ops, SparseCore 0:
  24.7 30.9 all-gather.11
  58.1 83.4 all-gather.5
  181.3 122.3 all-gather.7
  305.5 51.2 all-gather.9
